TPU v7x, 256 devices: a whole 4x4x8 slice. The times are simulated.
256 devices in a mesh: section: 4 (over y), dp: 16 (over z, core), expert: 4 (over x).
Axes of the slice: x: 4, y: 4, z: 8, core: 2. Of those that a mesh axis runs over, the one named last changes fastest.
Arguments:
- inputs: bfloat16 [4, 8192, 2048], P('section', ('dp', 'expert')), may hold values from -6 to 6
- in_cache: bfloat16 [4, 8192, 2048], P('section', ('dp', 'expert')), may hold values from -6 to 6
- out_cache: bfloat16 [4, 8192, 2048], P('section', ('dp', 'expert')), may hold values from -6 to 6
- w_up: bfloat16 [4, 2048, 57344], P('section', None, ('dp', 'expert')), may hold values from -0.125 to 0.125
- w_down: bfloat16 [4, 57344, 2048], P('section', ('dp', 'expert')), may hold values from -0.0625 to 0.0625
- routing: int32 [4, 8192, 2], P('section', ('dp', 'expert')), may hold values from 0 to 7, all different within a row; in each aligned block of 128 rows (0 to 127, 128 to 255, ..., all dimensions but the last counted through in order) at most 32 rows name the same one
- gate_table: int32 [4, 8192, 2], P('section', ('dp', 'expert')), may hold values from 1 to 16
- lengths: int32 [512], P(('dp', 'expert')), may hold values from 1 to 16
- sample_map: int32 [512], replicated, may hold values from 0 to 511, as said below
Outputs:
- next_input: bfloat16 [4, 8192, 2048], P('section', ('dp', 'expert'))
- new_out_cache: bfloat16 [4, 8192, 2048], P('section', ('dp', 'expert'))
Inputs may be any that keep to these rules, and one draw needn't show every extreme that they name: `sample_map`: A permutation. Every sample keeps its index along expert; the samples of one device go to exactly 8 replicas, exactly 1 to each. `routing`: A row names 2 different experts; in the rows of one device each expert is named exactly 32 times.
All inputs are finite; a program needn't handle non-finite values.
Results may differ from a plain program's by a relative error of at most 0.007.
Values may be sent and summed in bfloat16 or wider, within the bound.
No kernel may reach another device: no remote copies, remote signals or barrier semaphores. Data moves between devices by JAX's collectives and lax.ppermute only.
A program may use at most 128 MiB of HBM per device.

v0:
```python
import functools

import jax
import jax.numpy as jnp
from jax import lax
from jax.experimental import pallas as pl
from jax.experimental.pallas import tpu as pltpu
from jax.sharding import Mesh, PartitionSpec as P

EXPERTS = 8
TOPK = 2
ROWS = 16
SAMP_DEV = 8
ROW_CHUNKS = 2
FEATURE_CHUNKS = 2
UP_STEP = 512
DOWN_STEP = 512
SMALL_VMEM = 8 << 20
LARGE_VMEM = 28 << 20
BF16 = jnp.bfloat16
F32 = jnp.float32


def shifted(value, axis, by):
    peers = lax.axis_size(axis)
    return lax.ppermute(value, axis, [(i, (i + by) % peers) for i in range(peers)])


def exchanged(value):
    return lax.all_to_all(value, "z", split_axis=0, concat_axis=0, tiled=True)


def group_kernel(routing_ref, tokens_ref, *out_refs):
    chunk_refs, slot_ref = out_refs[:-1], out_refs[-1]
    rows = tokens_ref.shape[0]
    per_expert = rows * TOPK // EXPERTS
    part = per_expert // ROW_CHUNKS
    experts = lax.broadcasted_iota(jnp.int32, (2 * EXPERTS, rows), 0)
    earlier = (
        lax.broadcasted_iota(jnp.int32, (rows, rows), 0)
        < lax.broadcasted_iota(jnp.int32, (rows, rows), 1)
    ).astype(F32).astype(BF16)
    first = (routing_ref[0:1, :] == experts).astype(F32)
    second = (routing_ref[1:2, :] == experts).astype(F32)
    before_first = jnp.dot(first.astype(BF16), earlier, preferred_element_type=F32)
    before_second = jnp.dot(second.astype(BF16), earlier, preferred_element_type=F32) + jnp.sum(
        first, axis=1, keepdims=True
    )
    base = (experts * per_expert).astype(F32)
    slot_first = jnp.sum(first * (before_first + base), axis=0, keepdims=True).astype(jnp.int32)
    slot_second = jnp.sum(second * (before_second + base), axis=0, keepdims=True).astype(jnp.int32)
    slot_ref[0:1, :] = slot_first
    slot_ref[1:2, :] = slot_second
    tokens = tokens_ref[...]
    index = lax.broadcasted_iota(jnp.int32, (EXPERTS * part, rows), 0)
    for chunk, chunk_ref in enumerate(chunk_refs):
        wanted = index // part * per_expert + chunk * part + index % part
        chosen = ((slot_first == wanted) | (slot_second == wanted)).astype(F32).astype(BF16)
        chunk_ref[...] = jnp.dot(chosen, tokens, preferred_element_type=F32).astype(BF16)


def group_rows(routing, tokens):
    rows, width = tokens.shape
    slots = rows * TOPK
    chunk = jax.ShapeDtypeStruct((slots // ROW_CHUNKS, width), BF16)
    out = pl.pallas_call(
        group_kernel,
        out_shape=(chunk,) * ROW_CHUNKS + (jax.ShapeDtypeStruct((TOPK, rows), jnp.int32),),
        compiler_params=pltpu.CompilerParams(vmem_limit_bytes=SMALL_VMEM),
        cost_estimate=pl.CostEstimate(
            flops=2 * slots * rows * width, bytes_accessed=3 * slots * width, transcendentals=0
        ),
        name="group_rows",
    )(routing, tokens)
    return out[:-1], out[-1]


def up_kernel(count, *refs):
    row_refs, own_ref, other_ref = refs[:count], refs[count], refs[count + 1]
    out_refs, total_ref = refs[count + 2 : -1], refs[-1]
    step = pl.program_id(0)
    rows = jnp.concatenate([ref[...] for ref in row_refs], axis=0)
    weights = jnp.concatenate([own_ref[...], other_ref[...]], axis=1)
    term = jnp.dot(rows, weights, preferred_element_type=F32)

    @pl.when(step == 0)
    def _():
        total_ref[...] = term

    @pl.when((step > 0) & (step < pl.num_programs(0) - 1))
    def _():
        total_ref[...] += term

    @pl.when(step == pl.num_programs(0) - 1)
    def _():
        value = total_ref[...] + term
        hidden = (value / (1.0 + jnp.exp(-value))).astype(BF16)
        at = 0
        for ref in out_refs:
            ref[...] = hidden[at : at + ref.shape[0]]
            at += ref.shape[0]


def up(blocks, own, other):
    depth, units = own.shape
    count = len(blocks)
    total = sum(block.shape[0] for block in blocks)
    weight = pl.BlockSpec((UP_STEP, units), lambda k: (k, 0))
    return pl.pallas_call(
        functools.partial(up_kernel, count),
        grid=(depth // UP_STEP,),
        in_specs=[pl.BlockSpec((block.shape[0], UP_STEP), lambda k: (0, k)) for block in blocks]
        + [weight, weight],
        out_specs=[pl.BlockSpec((block.shape[0], 2 * units), lambda k: (0, 0)) for block in blocks],
        out_shape=[jax.ShapeDtypeStruct((block.shape[0], 2 * units), BF16) for block in blocks],
        scratch_shapes=[pltpu.VMEM((total, 2 * units), F32)],
        compiler_params=pltpu.CompilerParams(vmem_limit_bytes=LARGE_VMEM),
        cost_estimate=pl.CostEstimate(
            flops=4 * total * depth * units,
            bytes_accessed=4 * depth * units + 2 * total * depth,
            transcendentals=2 * total * units,
        ),
    )(*blocks, own, other)


def down_kernel(count, added, split, *refs):
    hidden_refs, own_ref, other_ref = refs[:count], refs[count], refs[count + 1]
    extra_refs = refs[count + 2 : len(refs) - len(added)]
    out_refs = refs[len(refs) - len(added) :]
    hidden = jnp.concatenate([ref[...] for ref in hidden_refs], axis=0)
    weights = jnp.concatenate([own_ref[...], other_ref[...]], axis=0)
    term = jnp.dot(hidden, weights, preferred_element_type=F32)
    rows = hidden_refs[0].shape[0]
    at = 0
    for parts, out_ref in zip(added, out_refs):
        for number, operands in enumerate(parts):
            value = term[at : at + rows]
            for which, lead in operands:
                extra = extra_refs[which]
                value += (extra[...] if lead is None else extra[lead]).astype(F32)
            value = value.astype(BF16)
            if split:
                out_ref[:, number] = value.reshape(out_ref.shape[0], *out_ref.shape[2:])
            elif len(parts) == 1:
                out_ref[...] = value
            else:
                out_ref[number] = value
            at += rows


def down(hidden, own, other, chunk, added, extras=(), split=0):
    rows, units = hidden[0].shape
    units //= 2
    width = own.shape[1] // FEATURE_CHUNKS
    steps = width // DOWN_STEP
    weight = pl.BlockSpec((units, DOWN_STEP), lambda n: (0, chunk * steps + n))
    out_shape, out_specs = [], []
    for parts in added:
        if split:
            lead = (split, len(parts), rows // split)
        elif len(parts) == 1:
            lead = (rows,)
        else:
            lead = (len(parts), rows)
        out_shape.append(jax.ShapeDtypeStruct(lead + (width,), BF16))
        out_specs.append(
            pl.BlockSpec(lead + (DOWN_STEP,), lambda n, lead=lead: (0,) * len(lead) + (n,))
        )
    total = rows * len(hidden)
    return pl.pallas_call(
        functools.partial(down_kernel, len(hidden), added, split),
        grid=(steps,),
        in_specs=[pl.BlockSpec((rows, 2 * units), lambda n: (0, 0)) for _ in hidden]
        + [weight, weight]
        + [
            pl.BlockSpec(
                extra.shape[:-1] + (DOWN_STEP,), lambda n, rank=extra.ndim: (0,) * (rank - 1) + (n,)
            )
            for extra in extras
        ],
        out_specs=out_specs,
        out_shape=out_shape,
        compiler_params=pltpu.CompilerParams(vmem_limit_bytes=LARGE_VMEM),
        cost_estimate=pl.CostEstimate(
            flops=4 * total * width * units,
            bytes_accessed=4 * width * units + 2 * total * width,
            transcendentals=0,
        ),
    )(*hidden, own, other, *extras)


def combine_kernel(slot_ref, gate_ref, live_ref, moved_ref, back_ref, delta_ref, cache_ref):
    rows = slot_ref.shape[0]
    back = back_ref[...]
    slots = back.shape[0]
    slot_lanes = lax.broadcasted_iota(jnp.int32, (rows, slots), 1)
    slot = slot_ref[...]
    pick_first = (slot[:, 0:1] == slot_lanes).astype(F32).astype(BF16)
    pick_second = (slot[:, 1:2] == slot_lanes).astype(F32).astype(BF16)
    first = jnp.dot(pick_first, back, preferred_element_type=F32)
    second = jnp.dot(pick_second, back, preferred_element_type=F32)
    gates = gate_ref[...].astype(F32)
    total = gates[:, 0:1] + gates[:, 1:2]
    mixed = gates[:, 0:1] / total * first + gates[:, 1:2] / total * second
    moved = moved_ref[...].astype(F32)
    delta = jnp.where(live_ref[...] > 0, mixed - moved, 0.0).astype(BF16)
    delta_ref[...] = delta
    cache_ref[...] = (moved + delta.astype(F32)).astype(BF16)


def combine(back, slot, gates, live, moved):
    rows, width = moved.shape
    out = jax.ShapeDtypeStruct((rows, width), BF16)
    return pl.pallas_call(
        combine_kernel,
        out_shape=(out, out),
        compiler_params=pltpu.CompilerParams(vmem_limit_bytes=SMALL_VMEM),
        cost_estimate=pl.CostEstimate(
            flops=4 * TOPK * rows * rows * width,
            bytes_accessed=(2 * TOPK + 6) * moved.size,
            transcendentals=0,
        ),
    )(slot, gates, live, moved, back)


def section_step(
    inputs, in_cache, out_cache, w_up, w_down, routing, gate_table, lengths, sample_map
):
    width = inputs.shape[2]
    tok_rows = inputs.shape[1]
    z_count = lax.axis_size("z")
    x_count = lax.axis_size("x")
    dp_count = z_count * lax.axis_size("core")
    own_dp = lax.axis_index(("z", "core"))
    own_device = own_dp * x_count + lax.axis_index("x")

    chunks, slot = group_rows(routing[0].T, inputs[0])
    up_own, down_own = w_up[0], w_down[0]
    blocks = [exchanged(chunk.reshape(z_count, -1, width)).reshape(-1, width) for chunk in chunks]
    up_other = shifted(up_own, "core", 1)
    down_other = shifted(down_own, "core", 1)
    from_left = [shifted(block, "x", 1) for block in blocks]
    from_right = [shifted(block, "x", -1) for block in blocks]
    far = [shifted(from_left[0], "x", 1), shifted(from_right[1], "x", -1)]
    near_hidden = [
        up([blocks[c], from_left[c], from_right[c]], up_own, up_other)
        for c in range(ROW_CHUNKS)
    ]
    far_hidden = up(far, up_own, up_other)
    own_hidden = [hidden[0] for hidden in near_hidden]
    side_hidden = [hidden[1] for hidden in near_hidden] + [hidden[2] for hidden in near_hidden]

    backs = []
    for f in range(FEATURE_CHUNKS):
        far_first, far_second = down(far_hidden, down_own, down_other, f, (((),), ((),)))
        for_left = shifted(far_first, "x", -1)
        for_right = shifted(far_second, "x", 1)
        to_left, to_right = down(
            side_hidden,
            down_own,
            down_other,
            f,
            ((((0, None),), ()), ((), ((1, None),))),
            (for_left, for_right),
        )
        got_right = shifted(to_left, "x", -1)
        got_left = shifted(to_right, "x", 1)
        (summed,) = down(
            own_hidden,
            down_own,
            down_other,
            f,
            ((((0, 0), (1, 0)), ((0, 1), (1, 1))),),
            (got_left, got_right),
            split=z_count,
        )
        backs.append(exchanged(summed).reshape(tok_rows * TOPK, -1))

    own_map = lax.dynamic_slice_in_dim(sample_map, own_device * SAMP_DEV, SAMP_DEV)
    dest_dp = own_map // SAMP_DEV // x_count
    sample_ids = jnp.arange(SAMP_DEV, dtype=jnp.int32)
    goes = dest_dp[None, :] == jnp.arange(dp_count, dtype=jnp.int32)[:, None]
    slot_sample = jnp.sum(jnp.where(goes, sample_ids[None, :], 0), axis=1)
    own_places = own_device * SAMP_DEV + sample_ids
    sources = jnp.sum(
        jnp.where(
            sample_map[None, :] == own_places[:, None],
            jnp.arange(sample_map.shape[0], dtype=jnp.int32)[None, :],
            0,
        ),
        axis=1,
    )
    source_dp = sources // SAMP_DEV // x_count

    sent = jnp.concatenate(
        [
            cache.reshape(SAMP_DEV, 1, ROWS, width)[slot_sample]
            for cache in (out_cache[0], in_cache[0])
        ],
        axis=1,
    )
    sent, _ = lax.optimization_barrier((sent, blocks[1]))
    got = lax.all_to_all(sent, ("z", "core"), split_axis=0, concat_axis=0, tiled=True)
    moved = got[source_dp]
    out_moved = moved[:, 0].reshape(tok_rows, width)
    in_moved = moved[:, 1].reshape(tok_rows, width)

    live = (
        jnp.arange(tok_rows, dtype=jnp.int32) % ROWS < jnp.repeat(lengths, ROWS)
    ).astype(jnp.int32)[:, None]
    slot = slot.T
    sections = lax.axis_size("section")
    caches, arrivals = [], []
    part = width // FEATURE_CHUNKS
    for f, back in enumerate(backs):
        columns = out_moved[:, f * part : (f + 1) * part]
        delta, cache = combine(back, slot, gate_table[0], live, columns)
        caches.append(cache)
        arrivals.append(lax.ppermute(delta, "section", [(i, i + 1) for i in range(sections - 1)]))
    new_out = jnp.concatenate(caches, axis=1)
    received = jnp.concatenate(arrivals, axis=1)
    next_input = (in_moved.astype(F32) + received.astype(F32)).astype(BF16)
    return next_input[None], new_out[None]


def solution(mesh):
    sections, dp, expert = mesh.devices.shape
    split = Mesh(
        mesh.devices.reshape(sections, dp // 2, 2, expert), ("section", "z", "core", "x")
    )
    group = ("z", "core", "x")
    rows = P("section", group, None)
    placed = (rows, rows, rows, P("section", None, group), rows, rows, rows, P(group), P())
    return jax.shard_map(
        section_step, mesh=split, in_specs=placed, out_specs=(rows, rows), check_vma=False
    )
```

profile of v0, /device:TPU:22, one launch (start us, length us, event | category | flops | bytes accessed | tf_op | source)
XLA Modules:
  0.0 192.6 jit_solution(111407912353759141)
XLA Ops:
  0.6 0.0 copy-start
  0.7 1.1 copy-done.7
  1.8 0.7 copy-done.10
  2.4 1.4 group_rows.1
  3.8 8.6 %all-to-all-start = ((bf16[8,16,2048]{2,1,0:T(8,128)(2,1)}), bf16[8,16,2048]{2,1,0:T(8,128)(2,1)S(1)}, u32[]{:S(2)}, u32[]{:S(2)}) async-start(bf16[8,16,2048]{2,1,0:T(8,128)(2,1)} %bitcast.9), calls=%async_computation | async-start | bytes 1048576 | tf_op jit(solution)/shard_map/all_to_all | solution.py:30
  12.4 0.5 collective-permute-start.5
  12.9 17.0 %all-to-all-done = bf16[8,16,2048]{2,1,0:T(8,128)(2,1)S(1)} async-done(((bf16[8,16,2048]{2,1,0:T(8,128)(2,1)}), bf16[8,16,2048]{2,1,0:T(8,128)(2,1)S(1)}, u32[]{:S(2)}, u32[]{:S(2)}) %all-to-all-start) | async-done | bytes 524320 | tf_op jit(solution)/shard_map/all_to_all | solution.py:30
  29.9 3.5 %all-to-all-start.2 = ((bf16[8,16,2048]{2,1,0:T(8,128)(2,1)}), bf16[8,16,2048]{2,1,0:T(8,128)(2,1)S(1)}, u32[]{:S(2)}, u32[]{:S(2)}) async-start(bf16[8,16,2048]{2,1,0:T(8,128)(2,1)} %bitcast.17), calls=%async_computation.2 | async-start | bytes 1048576 | tf_op jit(solution)/shard_map/all_to_all | solution.py:30
  33.4 0.1 and_select_fusion.2
  33.5 0.1 select_reduce_fusion.1
  33.6 0.6 gather_fusion.1
  34.3 1.6 gather_fusion
  35.9 2.7 %pad_maximum_fusion = bf16[16,2,16,2048]{3,2,1,0:T(8,128)(2,1)} fusion(bf16[16,1,16,2048]{3,2,1,0:T(8,128)(2,1)S(1)} %bitcast.67, bf16[16,1,16,2048]{3,2,1,0:T(8,128)(2,1)} %bitcast.68), kind=kLoop, calls=%fused_computation.3 | loop fusion | flops 1048576 | bytes 4194304 | tf_op jit(solution)/shard_map/concatenate | solution.py:295
  38.7 12.6 %all-to-all-done.2 = bf16[8,16,2048]{2,1,0:T(8,128)(2,1)S(1)} async-done(((bf16[8,16,2048]{2,1,0:T(8,128)(2,1)}), bf16[8,16,2048]{2,1,0:T(8,128)(2,1)S(1)}, u32[]{:S(2)}, u32[]{:S(2)}) %all-to-all-start.2) | async-done | bytes 524320 | tf_op jit(solution)/shard_map/all_to_all | solution.py:30
  51.3 4.4 %all-to-all-start.1 = ((bf16[16,2,16,2048]{3,2,1,0:T(8,128)(2,1)}), bf16[16,2,16,2048]{3,2,1,0:T(8,128)(2,1)}, u32[]{:S(2)}, u32[]{:S(2)}) async-start(bf16[16,2,16,2048]{3,2,1,0:T(8,128)(2,1)} %pad_maximum_fusion), calls=%async_computation.1 | async-start | bytes 4194304 | tf_op jit(solution)/shard_map/all_to_all | solution.py:303
  55.7 0.6 collective-permute-start
  56.3 1.5 collective-permute-start.4
  57.8 12.0 %collective-permute-done.refs_1_ = bf16[128,2048]{1,0:T(8,128)(2,1)S(1)} collective-permute-done((bf16[128,2048]{1,0:T(8,128)(2,1)S(1)}, bf16[128,2048]{1,0:T(8,128)(2,1)S(1)}, u32[]{:S(2)}, u32[]{:S(2)}) %collective-permute-start) | collective-permute-done | bytes 524320 | tf_op jit(solution)/shard_map/ppermute | solution.py:26
  69.8 1.7 collective-permute-start.6
  71.5 0.3 collective-permute-start.7
  71.8 2.9 %collective-permute-start.3 = (bf16[128,2048]{1,0:T(8,128)(2,1)S(1)}, bf16[128,2048]{1,0:T(8,128)(2,1)S(1)}, u32[]{:S(2)}, u32[]{:S(2)}) collective-permute-start(bf16[128,2048]{1,0:T(8,128)(2,1)S(1)} %bitcast.61), channel_id=1, source_target_pairs={{0,1},{1,2},{2,3},{3,0},{4,5},{5,6},{6,7},{7,4},{8,9},{9,10},{10,1... | collective-permute-start | bytes 1572872 | tf_op jit(solution)/shard_map/ppermute | solution.py:26
  74.7 9.9 %collective-permute-done.6.refs_0_ = bf16[128,2048]{1,0:T(8,128)(2,1)S(1)} collective-permute-done((bf16[128,2048]{1,0:T(8,128)(2,1)S(1)}, bf16[128,2048]{1,0:T(8,128)(2,1)S(1)}, u32[]{:S(2)}, u32[]{:S(2)}) %collective-permute-start.6) | collective-permute-done | bytes 524320 | tf_op jit(solution)/shard_map/ppermute | solution.py:26
  84.6 0.8 collective-permute-start.1
  85.4 0.4 collective-permute-done.7.refs_1_
  85.8 2.0 %copy-done.3 = bf16[1,2048,896]{2,1,0:T(8,128)(2,1)S(1)} copy-done((bf16[1,2048,896]{2,1,0:T(8,128)(2,1)S(1)}, bf16[1,2048,896]{2,1,0:T(8,128)(2,1)}, u32[]{:S(2)}) %copy-start.3) | copy-done | bytes 3670040
  87.9 5.4 %shard_map.106 = (bf16[128,1792]{1,0:T(8,128)(2,1)S(1)}, bf16[128,1792]{1,0:T(8,128)(2,1)S(1)}) custom-call(bf16[128,2048]{1,0:T(8,128)(2,1)S(1)} %collective-permute-done.6.refs_0_, bf16[128,2048]{1,0:T(8,128)(2,1)S(1)} %collective-permute-done.7.refs_1_, bf16[2048,896]{1,0:T(8,128)(2,1)S(1)} %bitcast.50, ...), custom_call_target="tpu_custom_call" | custom-call | flops 1879048192 | bytes 8388608 | tf_op jit(solution)/shard_map/pallas_call | solution.py:109
  93.3 2.7 %shard_map.107 = (bf16[128,1024]{1,0:T(8,128)(2,1)S(1)}, bf16[128,1024]{1,0:T(8,128)(2,1)S(1)}) custom-call(bf16[128,1792]{1,0:T(8,128)(2,1)S(1)} %get-tuple-element.36.refs_0_, bf16[128,1792]{1,0:T(8,128)(2,1)S(1)} %get-tuple-element.37.refs_1_, bf16[896,2048]{1,0:T(8,128)(2,1)S(1)} %bitcast.43, bf16[896,2048]{1,0:T(8,128)(2,1)} %collective-permute-done.5.refs_3_.refs_5_), custom_call_target="tpu_custom_call" | custom-call | flops 939524096 | bytes 4194304 | tf_op jit(solution)/shard_map/pallas_call | solution.py:170
  96.0 0.2 collective-permute-start.8
  96.3 3.1 %collective-permute-start.9 = (bf16[128,1024]{1,0:T(8,128)(2,1)S(1)}, bf16[128,1024]{1,0:T(8,128)(2,1)S(1)}, u32[]{:S(2)}, u32[]{:S(2)}) collective-permute-start(bf16[128,1024]{1,0:T(8,128)(2,1)S(1)} %get-tuple-element.39), channel_id=1, source_target_pairs={{0,1},{1,2},{2,3},{3,0},{4,5},{5,6},{6,7},{7,4},{8,9},{9,10},{10,1... | collective-permute-start | bytes 786440 | tf_op jit(solution)/shard_map/ppermute | solution.py:26
  99.4 6.3 %shard_map.105 = (bf16[128,1792]{1,0:T(8,128)(2,1)S(1)}, bf16[128,1792]{1,0:T(8,128)(2,1)S(1)}, bf16[128,1792]{1,0:T(8,128)(2,1)S(1)}) custom-call(bf16[128,2048]{1,0:T(8,128)(2,1)S(1)} %bitcast.62, bf16[128,2048]{1,0:T(8,128)(2,1)S(1)} %collective-permute-done.3.refs_1_, bf16[128,2048]{1,0:T(8,128)(2,1)S(1)} %collective-permute-done.4.refs_2_, ...), custom_call_target="tpu_custom_call" | custom-call | flops 2818572288 | bytes 8912896 | tf_op jit(solution)/shard_map/pallas_call | solution.py:109
  105.6 6.3 %shard_map.104 = (bf16[128,1792]{1,0:T(8,128)(2,1)S(1)}, bf16[128,1792]{1,0:T(8,128)(2,1)S(1)}, bf16[128,1792]{1,0:T(8,128)(2,1)S(1)}) custom-call(bf16[128,2048]{1,0:T(8,128)(2,1)S(1)} %bitcast.65, bf16[128,2048]{1,0:T(8,128)(2,1)S(1)} %collective-permute-done.refs_1_, bf16[128,2048]{1,0:T(8,128)(2,1)S(1)} %collective-permute-done.1.refs_2_, ...), custom_call_target="tpu_custom_call" | custom-call | flops 2818572288 | bytes 8912896 | tf_op jit(solution)/shard_map/pallas_call | solution.py:109
  111.9 3.7 %shard_map.108 = (bf16[2,128,1024]{2,1,0:T(8,128)(2,1)S(1)}, bf16[2,128,1024]{2,1,0:T(8,128)(2,1)S(1)}) custom-call(bf16[128,1792]{1,0:T(8,128)(2,1)S(1)} %get-tuple-element.32.refs_0_, bf16[128,1792]{1,0:T(8,128)(2,1)S(1)} %get-tuple-element.33.refs_1_, bf16[128,1792]{1,0:T(8,128)(2,1)S(1)} %get-tuple-element.34.refs_2_, ...), custom_call_target="tpu_custom_call" | custom-call | flops 1879048192 | bytes 4718592 | tf_op jit(solution)/shard_map/pallas_call | solution.py:170
  115.6 0.9 collective-permute-start.10
  116.5 1.2 collective-permute-start.11
  117.7 3.3 %shard_map.111 = (bf16[128,1024]{1,0:T(8,128)(2,1)}, bf16[128,1024]{1,0:T(8,128)(2,1)}) custom-call(bf16[128,1792]{1,0:T(8,128)(2,1)S(1)} %get-tuple-element.36.refs_0_, bf16[128,1792]{1,0:T(8,128)(2,1)S(1)} %get-tuple-element.37.refs_1_, bf16[896,2048]{1,0:T(8,128)(2,1)S(1)} %bitcast.45, bf16[896,2048]{1,0:T(8,128)(2,1)} %collective-permute-done.5.refs_3_.refs_5_), custom_call_target="tpu_custom_call" | custom-call | flops 939524096 | bytes 4194304 | tf_op jit(solution)/shard_map/pallas_call | solution.py:170
  121.0 3.2 %collective-permute-start.14 = (bf16[128,1024]{1,0:T(8,128)(2,1)}, bf16[128,1024]{1,0:T(8,128)(2,1)}, u32[]{:S(2)}, u32[]{:S(2)}) collective-permute-start(bf16[128,1024]{1,0:T(8,128)(2,1)} %get-tuple-element.44), channel_id=1, source_target_pairs={{0,1},{1,2},{2,3},{3,0},{4,5},{5,6},{6,7},{7,4},{8,9},{9,10},{10,1... | collective-permute-start | bytes 786440 | tf_op jit(solution)/shard_map/ppermute | solution.py:26
  124.2 5.7 %collective-permute-done.10.refs_4_ = bf16[2,128,1024]{2,1,0:T(8,128)(2,1)S(1)} collective-permute-done((bf16[2,128,1024]{2,1,0:T(8,128)(2,1)S(1)}, bf16[2,128,1024]{2,1,0:T(8,128)(2,1)S(1)}, u32[]{:S(2)}, u32[]{:S(2)}) %collective-permute-start.10) | collective-permute-done | bytes 524320 | tf_op jit(solution)/shard_map/ppermute | solution.py:26
  130.0 1.3 collective-permute-done.11.refs_5_
  131.3 3.3 %shard_map.109 = bf16[8,2,16,1024]{3,2,1,0:T(8,128)(2,1)} custom-call(bf16[128,1792]{1,0:T(8,128)(2,1)S(1)} %get-tuple-element.30.refs_0_, bf16[128,1792]{1,0:T(8,128)(2,1)S(1)} %get-tuple-element.31.refs_1_, bf16[896,2048]{1,0:T(8,128)(2,1)S(1)} %bitcast.46, bf16[896,2048]{1,0:T(8,128)(2,1)} %collective-permute-done.5.refs_3_.refs_5_, ...), custom_call_target="tpu_custom_call" | custom-call | flops 939524096 | bytes 4194304 | tf_op jit(solution)/shard_map/pallas_call | solution.py:170
  134.5 6.7 %all-to-all-start.3 = ((bf16[8,2,16,1024]{3,2,1,0:T(8,128)(2,1)}), bf16[8,2,16,1024]{3,2,1,0:T(8,128)(2,1)S(1)}, u32[]{:S(2)}, u32[]{:S(2)}) async-start(bf16[8,2,16,1024]{3,2,1,0:T(8,128)(2,1)} %shard_map.109), calls=%async_computation.3 | async-start | bytes 1048576 | tf_op jit(solution)/shard_map/all_to_all | solution.py:30
  141.3 0.1 broadcast_in_dim.45
  141.3 0.1 reshape.267
  141.4 0.1 copy.18
  141.5 0.1 copy.17
  141.7 2.0 %copy-done.2 = bf16[1,896,2048]{2,1,0:T(8,128)(2,1)S(1)} copy-done((bf16[1,896,2048]{2,1,0:T(8,128)(2,1)S(1)}, bf16[1,896,2048]{2,1,0:T(8,128)(2,1)}, u32[]{:S(2)}) %copy-start.2) | copy-done | bytes 3670040
  143.7 1.0 copy-done.6
  144.7 3.7 %shard_map.112 = (bf16[2,128,1024]{2,1,0:T(8,128)(2,1)S(1)}, bf16[2,128,1024]{2,1,0:T(8,128)(2,1)S(1)}) custom-call(bf16[128,1792]{1,0:T(8,128)(2,1)S(1)} %get-tuple-element.32.refs_0_, bf16[128,1792]{1,0:T(8,128)(2,1)S(1)} %get-tuple-element.33.refs_1_, bf16[128,1792]{1,0:T(8,128)(2,1)S(1)} %copy-done.6, bf16[128,1792]{1,0:T(8,128)(2,1)S(1)} %get-tuple-element.35.refs_3_, ...), custom_call_target="tpu_custom_call" | custom-call | flops 1879048192 | bytes 4718592 | tf_op jit(solution)/shard_map/pallas_call | solution.py:170
  148.4 0.4 collective-permute-start.15
  148.8 1.8 collective-permute-start.16
  150.5 0.2 select_reduce_fusion
  150.7 6.9 %collective-permute-done.15.refs_4_ = bf16[2,128,1024]{2,1,0:T(8,128)(2,1)S(1)} collective-permute-done((bf16[2,128,1024]{2,1,0:T(8,128)(2,1)S(1)}, bf16[2,128,1024]{2,1,0:T(8,128)(2,1)S(1)}, u32[]{:S(2)}, u32[]{:S(2)}) %collective-permute-start.15) | collective-permute-done | bytes 524320 | tf_op jit(solution)/shard_map/ppermute | solution.py:26
  157.7 1.5 collective-permute-done.16.refs_5_
  159.2 3.3 %shard_map.113 = bf16[8,2,16,1024]{3,2,1,0:T(8,128)(2,1)} custom-call(bf16[128,1792]{1,0:T(8,128)(2,1)S(1)} %get-tuple-element.30.refs_0_, bf16[128,1792]{1,0:T(8,128)(2,1)S(1)} %get-tuple-element.31.refs_1_, bf16[896,2048]{1,0:T(8,128)(2,1)S(1)} %bitcast.48, bf16[896,2048]{1,0:T(8,128)(2,1)} %collective-permute-done.5.refs_3_.refs_5_, ...), custom_call_target="tpu_custom_call" | custom-call | flops 939524096 | bytes 4194304 | tf_op jit(solution)/shard_map/pallas_call | solution.py:170
  162.4 7.2 %all-to-all-start.4 = ((bf16[8,2,16,1024]{3,2,1,0:T(8,128)(2,1)}), bf16[8,2,16,1024]{3,2,1,0:T(8,128)(2,1)S(1)}, u32[]{:S(2)}, u32[]{:S(2)}) async-start(bf16[8,2,16,1024]{3,2,1,0:T(8,128)(2,1)} %shard_map.113), calls=%async_computation.4 | async-start | bytes 1048576 | tf_op jit(solution)/shard_map/all_to_all | solution.py:30
  169.7 2.2 %gather_fusion.2 = bf16[8,2,16,2048]{3,2,1,0:T(8,128)(2,1)S(1)} fusion(bf16[16,2,16,2048]{3,2,1,0:T(8,128)(2,1)} %all-to-all-done.1, s32[1024]{0:T(1024)S(1)} %pad_clamp_fusion), kind=kCustom, calls=%fused_computation.2 | custom fusion | bytes 2097184 | tf_op jit(solution)/shard_map/gather | solution.py:304
  171.9 0.9 fusion.8
  172.8 0.5 shard_map.110
  173.3 3.2 %collective-permute-start.12 = (bf16[128,1024]{1,0:T(8,128)(2,1)S(1)}, bf16[128,1024]{1,0:T(8,128)(2,1)S(1)}, u32[]{:S(2)}, u32[]{:S(2)}) collective-permute-start(bf16[128,1024]{1,0:T(8,128)(2,1)S(1)} %get-tuple-element.42), channel_id=1, source_target_pairs={{0,64},{64,128},{128,192},{1,65},{65,129},{129,193},{2,66},{66,130... | collective-permute-start | bytes 786440 | tf_op jit(solution)/shard_map/ppermute | solution.py:319
  176.5 6.5 %all-to-all-done.4 = bf16[8,2,16,1024]{3,2,1,0:T(8,128)(2,1)S(1)} async-done(((bf16[8,2,16,1024]{3,2,1,0:T(8,128)(2,1)}), bf16[8,2,16,1024]{3,2,1,0:T(8,128)(2,1)S(1)}, u32[]{:S(2)}, u32[]{:S(2)}) %all-to-all-start.4) | async-done | bytes 524320 | tf_op jit(solution)/shard_map/all_to_all | solution.py:30
  182.9 0.5 shard_map.114
  183.4 3.2 %collective-permute-start.17 = (bf16[128,1024]{1,0:T(8,128)(2,1)S(1)}, bf16[128,1024]{1,0:T(8,128)(2,1)S(1)}, u32[]{:S(2)}, u32[]{:S(2)}) collective-permute-start(bf16[128,1024]{1,0:T(8,128)(2,1)S(1)} %get-tuple-element.47), channel_id=1, source_target_pairs={{0,64},{64,128},{128,192},{1,65},{65,129},{129,193},{2,66},{66,130... | collective-permute-start | bytes 786440 | tf_op jit(solution)/shard_map/ppermute | solution.py:319
  186.6 0.8 maximum_bitcast_fusion
  187.4 4.2 %collective-permute-done.17 = bf16[128,1024]{1,0:T(8,128)(2,1)S(1)} collective-permute-done((bf16[128,1024]{1,0:T(8,128)(2,1)S(1)}, bf16[128,1024]{1,0:T(8,128)(2,1)S(1)}, u32[]{:S(2)}, u32[]{:S(2)}) %collective-permute-start.17) | collective-permute-done | bytes 262176 | tf_op jit(solution)/shard_map/ppermute | solution.py:319
  191.7 0.9 fusion
  (47 shorter events, 0.2 us)
Async XLA Ops:
  0.6 33.0 %copy-start = (bf16[1,128,2048]{2,1,0:T(8,128)(2,1)S(1)}, bf16[1,128,2048]{2,1,0:T(8,128)(2,1)}, u32[]{:S(2)}) copy-start(bf16[1,128,2048]{2,1,0:T(8,128)(2,1)} %param.10) | copy-start | bytes 1572868
  0.6 32.8 %copy-start.13 = (s32[512]{0:T(512)S(1)}, s32[512]{0:T(512)}, u32[]{:S(2)}) copy-start(s32[512]{0:T(512)} %param.17) | copy-start | bytes 6148
  0.7 1.1 copy-start.7
  1.8 0.7 copy-start.10
  3.8 30.4 %copy-start.11 = (bf16[1,128,2048]{2,1,0:T(8,128)(2,1)S(1)}, bf16[1,128,2048]{2,1,0:T(8,128)(2,1)}, u32[]{:S(2)}) copy-start(bf16[1,128,2048]{2,1,0:T(8,128)(2,1)} %param.11) | copy-start | bytes 1572868
  3.8 26.1 %all-to-all-start = ((bf16[8,16,2048]{2,1,0:T(8,128)(2,1)}), bf16[8,16,2048]{2,1,0:T(8,128)(2,1)S(1)}, u32[]{:S(2)}, u32[]{:S(2)}) async-start(bf16[8,16,2048]{2,1,0:T(8,128)(2,1)} %bitcast.9), calls=%async_computation | async-start | bytes 1048576 | tf_op jit(solution)/shard_map/all_to_all | solution.py:30
  12.4 73.4 %collective-permute-start.2 = (bf16[2048,896]{1,0:T(8,128)(2,1)}, bf16[2048,896]{1,0:T(8,128)(2,1)}, u32[]{:S(2)}, u32[]{:S(2)}) collective-permute-start(bf16[2048,896]{1,0:T(8,128)(2,1)} %bitcast.49), channel_id=1, source_target_pairs={{0,4},{4,0},{1,5},{5,1},{2,6},{6,2},{3,7},{7,3},{8,12},{12,8},{9,1... | collective-permute-start | bytes 11010056 | tf_op jit(solution)/shard_map/ppermute | solution.py:26
  12.4 80.8 %collective-permute-start.5 = (bf16[896,2048]{1,0:T(8,128)(2,1)}, bf16[896,2048]{1,0:T(8,128)(2,1)}, u32[]{:S(2)}, u32[]{:S(2)}) collective-permute-start(bf16[896,2048]{1,0:T(8,128)(2,1)} %bitcast.42), channel_id=1, source_target_pairs={{0,4},{4,0},{1,5},{5,1},{2,6},{6,2},{3,7},{7,3},{8,12},{12,8},{9,1... | collective-permute-start | bytes 11010056 | tf_op jit(solution)/shard_map/ppermute | solution.py:26
  29.9 21.4 %all-to-all-start.2 = ((bf16[8,16,2048]{2,1,0:T(8,128)(2,1)}), bf16[8,16,2048]{2,1,0:T(8,128)(2,1)S(1)}, u32[]{:S(2)}, u32[]{:S(2)}) async-start(bf16[8,16,2048]{2,1,0:T(8,128)(2,1)} %bitcast.17), calls=%async_computation.2 | async-start | bytes 1048576 | tf_op jit(solution)/shard_map/all_to_all | solution.py:30
  51.3 33.3 %copy-start.8 = (bf16[8,16,2048]{2,1,0:T(8,128)(2,1)}, bf16[8,16,2048]{2,1,0:T(8,128)(2,1)S(1)}, u32[]{:S(2)}) copy-start(bf16[8,16,2048]{2,1,0:T(8,128)(2,1)S(1)} %all-to-all-done.2) | copy-start | bytes 1572868
  51.3 83.3 %all-to-all-start.1 = ((bf16[16,2,16,2048]{3,2,1,0:T(8,128)(2,1)}), bf16[16,2,16,2048]{3,2,1,0:T(8,128)(2,1)}, u32[]{:S(2)}, u32[]{:S(2)}) async-start(bf16[16,2,16,2048]{3,2,1,0:T(8,128)(2,1)} %pad_maximum_fusion), calls=%async_computation.1 | async-start | bytes 4194304 | tf_op jit(solution)/shard_map/all_to_all | solution.py:303
  55.7 14.1 %collective-permute-start = (bf16[128,2048]{1,0:T(8,128)(2,1)S(1)}, bf16[128,2048]{1,0:T(8,128)(2,1)S(1)}, u32[]{:S(2)}, u32[]{:S(2)}) collective-permute-start(bf16[128,2048]{1,0:T(8,128)(2,1)S(1)} %bitcast.63), channel_id=1, source_target_pairs={{0,1},{1,2},{2,3},{3,0},{4,5},{5,6},{6,7},{7,4},{8,9},{9,10},{10,1... | collective-permute-start | bytes 1572872 | tf_op jit(solution)/shard_map/ppermute | solution.py:26
  56.3 15.2 %collective-permute-start.4 = (bf16[128,2048]{1,0:T(8,128)(2,1)S(1)}, bf16[128,2048]{1,0:T(8,128)(2,1)S(1)}, u32[]{:S(2)}, u32[]{:S(2)}) collective-permute-start(bf16[128,2048]{1,0:T(8,128)(2,1)S(1)} %bitcast.60), channel_id=1, source_target_pairs={{0,3},{1,0},{2,1},{3,2},{4,7},{5,4},{6,5},{7,6},{8,11},{9,8},{10,9... | collective-permute-start | bytes 1572872 | tf_op jit(solution)/shard_map/ppermute | solution.py:26
  69.8 14.8 %collective-permute-start.6 = (bf16[128,2048]{1,0:T(8,128)(2,1)S(1)}, bf16[128,2048]{1,0:T(8,128)(2,1)S(1)}, u32[]{:S(2)}, u32[]{:S(2)}) collective-permute-start(bf16[128,2048]{1,0:T(8,128)(2,1)S(1)} %collective-permute-done.refs_1_), channel_id=1, source_target_pairs={{0,1},{1,2},{2,3},{3,0},{4,5},{5,6},{6,7},{7,4},{8,9},{9,10},{10,1... | collective-permute-start | bytes 1572872 | tf_op jit(solution)/shard_map/ppermute | solution.py:26
  71.5 14.3 %collective-permute-start.7 = (bf16[128,2048]{1,0:T(8,128)(2,1)S(1)}, bf16[128,2048]{1,0:T(8,128)(2,1)S(1)}, u32[]{:S(2)}, u32[]{:S(2)}) collective-permute-start(bf16[128,2048]{1,0:T(8,128)(2,1)S(1)} %collective-permute-done.4.refs_2_), channel_id=1, source_target_pairs={{0,3},{1,0},{2,1},{3,2},{4,7},{5,4},{6,5},{7,6},{8,11},{9,8},{10,9... | collective-permute-start | bytes 1572872 | tf_op jit(solution)/shard_map/ppermute | solution.py:26
  71.8 27.5 %collective-permute-start.3 = (bf16[128,2048]{1,0:T(8,128)(2,1)S(1)}, bf16[128,2048]{1,0:T(8,128)(2,1)S(1)}, u32[]{:S(2)}, u32[]{:S(2)}) collective-permute-start(bf16[128,2048]{1,0:T(8,128)(2,1)S(1)} %bitcast.61), channel_id=1, source_target_pairs={{0,1},{1,2},{2,3},{3,0},{4,5},{5,6},{6,7},{7,4},{8,9},{9,10},{10,1... | collective-permute-start | bytes 1572872 | tf_op jit(solution)/shard_map/ppermute | solution.py:26
  84.6 21.0 %collective-permute-start.1 = (bf16[128,2048]{1,0:T(8,128)(2,1)S(1)}, bf16[128,2048]{1,0:T(8,128)(2,1)S(1)}, u32[]{:S(2)}, u32[]{:S(2)}) collective-permute-start(bf16[128,2048]{1,0:T(8,128)(2,1)S(1)} %bitcast.64), channel_id=1, source_target_pairs={{0,3},{1,0},{2,1},{3,2},{4,7},{5,4},{6,5},{7,6},{8,11},{9,8},{10,9... | collective-permute-start | bytes 1572872 | tf_op jit(solution)/shard_map/ppermute | solution.py:26
  85.8 2.0 %copy-start.3 = (bf16[1,2048,896]{2,1,0:T(8,128)(2,1)S(1)}, bf16[1,2048,896]{2,1,0:T(8,128)(2,1)}, u32[]{:S(2)}) copy-start(bf16[1,2048,896]{2,1,0:T(8,128)(2,1)} %param.12) | copy-start | bytes 11010052
  87.9 5.4 %copy-start.1 = (bf16[1,896,2048]{2,1,0:T(8,128)(2,1)S(1)}, bf16[1,896,2048]{2,1,0:T(8,128)(2,1)}, u32[]{:S(2)}) copy-start(bf16[1,896,2048]{2,1,0:T(8,128)(2,1)} %param.13) | copy-start | bytes 11010052
  93.3 6.1 %copy-start.4 = (bf16[1,2048,896]{2,1,0:T(8,128)(2,1)S(1)}, bf16[1,2048,896]{2,1,0:T(8,128)(2,1)}, u32[]{:S(2)}) copy-start(bf16[1,2048,896]{2,1,0:T(8,128)(2,1)} %param.12) | copy-start | bytes 11010052
  96.0 15.9 %collective-permute-start.8 = (bf16[128,1024]{1,0:T(8,128)(2,1)S(1)}, bf16[128,1024]{1,0:T(8,128)(2,1)S(1)}, u32[]{:S(2)}, u32[]{:S(2)}) collective-permute-start(bf16[128,1024]{1,0:T(8,128)(2,1)S(1)} %get-tuple-element.38), channel_id=1, source_target_pairs={{0,3},{1,0},{2,1},{3,2},{4,7},{5,4},{6,5},{7,6},{8,11},{9,8},{10,9... | collective-permute-start | bytes 786440 | tf_op jit(solution)/shard_map/ppermute | solution.py:26
  96.3 9.4 %copy-start.9 = (bf16[8,16,2048]{2,1,0:T(8,128)(2,1)S(1)}, bf16[8,16,2048]{2,1,0:T(8,128)(2,1)}, u32[]{:S(2)}) copy-start(bf16[8,16,2048]{2,1,0:T(8,128)(2,1)} %copy-done.8) | copy-start | bytes 1572868
  96.3 15.7 %collective-permute-start.9 = (bf16[128,1024]{1,0:T(8,128)(2,1)S(1)}, bf16[128,1024]{1,0:T(8,128)(2,1)S(1)}, u32[]{:S(2)}, u32[]{:S(2)}) collective-permute-start(bf16[128,1024]{1,0:T(8,128)(2,1)S(1)} %get-tuple-element.39), channel_id=1, source_target_pairs={{0,1},{1,2},{2,3},{3,0},{4,5},{5,6},{6,7},{7,4},{8,9},{9,10},{10,1... | collective-permute-start | bytes 786440 | tf_op jit(solution)/shard_map/ppermute | solution.py:26
  111.9 3.7 %copy-start.5 = (bf16[128,1792]{1,0:T(8,128)(2,1)}, bf16[128,1792]{1,0:T(8,128)(2,1)S(1)}, u32[]{:S(2)}) copy-start(bf16[128,1792]{1,0:T(8,128)(2,1)S(1)} %get-tuple-element.34.refs_2_) | copy-start | bytes 1376260
  115.6 14.4 %collective-permute-start.10 = (bf16[2,128,1024]{2,1,0:T(8,128)(2,1)S(1)}, bf16[2,128,1024]{2,1,0:T(8,128)(2,1)S(1)}, u32[]{:S(2)}, u32[]{:S(2)}) collective-permute-start(bf16[2,128,1024]{2,1,0:T(8,128)(2,1)S(1)} %get-tuple-element.40), channel_id=1, source_target_pairs={{0,1},{1,2},{2,3},{3,0},{4,5},{5,6},{6,7},{7,4},{8,9},{9,10},{10,1... | collective-permute-start | bytes 1572872 | tf_op jit(solution)/shard_map/ppermute | solution.py:26
  116.5 14.8 %collective-permute-start.11 = (bf16[2,128,1024]{2,1,0:T(8,128)(2,1)S(1)}, bf16[2,128,1024]{2,1,0:T(8,128)(2,1)S(1)}, u32[]{:S(2)}, u32[]{:S(2)}) collective-permute-start(bf16[2,128,1024]{2,1,0:T(8,128)(2,1)S(1)} %get-tuple-element.41), channel_id=1, source_target_pairs={{0,3},{1,0},{2,1},{3,2},{4,7},{5,4},{6,5},{7,6},{8,11},{9,8},{10,9... | collective-permute-start | bytes 1572872 | tf_op jit(solution)/shard_map/ppermute | solution.py:26
  121.0 20.7 %collective-permute-start.13 = (bf16[128,1024]{1,0:T(8,128)(2,1)}, bf16[128,1024]{1,0:T(8,128)(2,1)}, u32[]{:S(2)}, u32[]{:S(2)}) collective-permute-start(bf16[128,1024]{1,0:T(8,128)(2,1)} %get-tuple-element.43), channel_id=1, source_target_pairs={{0,3},{1,0},{2,1},{3,2},{4,7},{5,4},{6,5},{7,6},{8,11},{9,8},{10,9... | collective-permute-start | bytes 786440 | tf_op jit(solution)/shard_map/ppermute | solution.py:26
  121.0 20.7 %collective-permute-start.14 = (bf16[128,1024]{1,0:T(8,128)(2,1)}, bf16[128,1024]{1,0:T(8,128)(2,1)}, u32[]{:S(2)}, u32[]{:S(2)}) collective-permute-start(bf16[128,1024]{1,0:T(8,128)(2,1)} %get-tuple-element.44), channel_id=1, source_target_pairs={{0,1},{1,2},{2,3},{3,0},{4,5},{5,6},{6,7},{7,4},{8,9},{9,10},{10,1... | collective-permute-start | bytes 786440 | tf_op jit(solution)/shard_map/ppermute | solution.py:26
  131.3 10.0 %copy-start.15 = (s32[8]{0:T(128)S(1)}, s32[8]{0:T(128)}, u32[]{:S(2)}) copy-start(s32[8]{0:T(128)} %param.16) | copy-start | bytes 100
  131.3 10.2 %copy-start.14 = (s32[1,128,2]{1,2,0:T(2,128)S(1)}, s32[1,128,2]{1,2,0:T(2,128)}, u32[]{:S(2)}) copy-start(s32[1,128,2]{1,2,0:T(2,128)} %param.15) | copy-start | bytes 3076
  134.5 27.9 %all-to-all-start.3 = ((bf16[8,2,16,1024]{3,2,1,0:T(8,128)(2,1)}), bf16[8,2,16,1024]{3,2,1,0:T(8,128)(2,1)S(1)}, u32[]{:S(2)}, u32[]{:S(2)}) async-start(bf16[8,2,16,1024]{3,2,1,0:T(8,128)(2,1)} %shard_map.109), calls=%async_computation.3 | async-start | bytes 1048576 | tf_op jit(solution)/shard_map/all_to_all | solution.py:30
  141.7 2.0 %copy-start.2 = (bf16[1,896,2048]{2,1,0:T(8,128)(2,1)S(1)}, bf16[1,896,2048]{2,1,0:T(8,128)(2,1)}, u32[]{:S(2)}) copy-start(bf16[1,896,2048]{2,1,0:T(8,128)(2,1)} %param.13) | copy-start | bytes 11010052
  143.7 1.0 copy-start.6
  148.4 9.3 %collective-permute-start.15 = (bf16[2,128,1024]{2,1,0:T(8,128)(2,1)S(1)}, bf16[2,128,1024]{2,1,0:T(8,128)(2,1)S(1)}, u32[]{:S(2)}, u32[]{:S(2)}) collective-permute-start(bf16[2,128,1024]{2,1,0:T(8,128)(2,1)S(1)} %get-tuple-element.45), channel_id=1, source_target_pairs={{0,1},{1,2},{2,3},{3,0},{4,5},{5,6},{6,7},{7,4},{8,9},{9,10},{10,1... | collective-permute-start | bytes 1572872 | tf_op jit(solution)/shard_map/ppermute | solution.py:26
  148.8 10.4 %collective-permute-start.16 = (bf16[2,128,1024]{2,1,0:T(8,128)(2,1)S(1)}, bf16[2,128,1024]{2,1,0:T(8,128)(2,1)S(1)}, u32[]{:S(2)}, u32[]{:S(2)}) collective-permute-start(bf16[2,128,1024]{2,1,0:T(8,128)(2,1)S(1)} %get-tuple-element.46), channel_id=1, source_target_pairs={{0,3},{1,0},{2,1},{3,2},{4,7},{5,4},{6,5},{7,6},{8,11},{9,8},{10,9... | collective-permute-start | bytes 1572872 | tf_op jit(solution)/shard_map/ppermute | solution.py:26
  162.4 20.5 %all-to-all-start.4 = ((bf16[8,2,16,1024]{3,2,1,0:T(8,128)(2,1)}), bf16[8,2,16,1024]{3,2,1,0:T(8,128)(2,1)S(1)}, u32[]{:S(2)}, u32[]{:S(2)}) async-start(bf16[8,2,16,1024]{3,2,1,0:T(8,128)(2,1)} %shard_map.113), calls=%async_computation.4 | async-start | bytes 1048576 | tf_op jit(solution)/shard_map/all_to_all | solution.py:30
  172.8 18.9 %copy-start.12 = (bf16[8,1,16,2048]{3,2,1,0:T(8,128)(2,1)S(1)}, bf16[8,1,16,2048]{3,2,1,0:T(8,128)(2,1)}, u32[]{:S(2)}) copy-start(bf16[8,1,16,2048]{3,2,1,0:T(8,128)(2,1)} %get-tuple-element.51) | copy-start | bytes 1572868
  173.3 14.2 %collective-permute-start.12 = (bf16[128,1024]{1,0:T(8,128)(2,1)S(1)}, bf16[128,1024]{1,0:T(8,128)(2,1)S(1)}, u32[]{:S(2)}, u32[]{:S(2)}) collective-permute-start(bf16[128,1024]{1,0:T(8,128)(2,1)S(1)} %get-tuple-element.42), channel_id=1, source_target_pairs={{0,64},{64,128},{128,192},{1,65},{65,129},{129,193},{2,66},{66,130... | collective-permute-start | bytes 786440 | tf_op jit(solution)/shard_map/ppermute | solution.py:319
  183.4 8.3 %collective-permute-start.17 = (bf16[128,1024]{1,0:T(8,128)(2,1)S(1)}, bf16[128,1024]{1,0:T(8,128)(2,1)S(1)}, u32[]{:S(2)}, u32[]{:S(2)}) collective-permute-start(bf16[128,1024]{1,0:T(8,128)(2,1)S(1)} %get-tuple-element.47), channel_id=1, source_target_pairs={{0,64},{64,128},{128,192},{1,65},{65,129},{129,193},{2,66},{66,130... | collective-permute-start | bytes 786440 | tf_op jit(solution)/shard_map/ppermute | solution.py:319
where the time goes:
time: 194 us; the launch traced here: 193 us
  waiting for transfers between devices  78 us (40%)
  starting transfers between devices  56 us (29%)
  Pallas kernels  40.1 us (21%)
  local copies, waits for them, and re-layouts  12.7 us (7%)
  other arithmetic  4.91 us (3%)
    ppermute x16, waiting for transfers between devices, shifted(): lax.ppermute(value, axis, [(i, (i + by) % peers) for i in range(peers)])  37.7 us
    all_to_all x4, waiting for transfers between devices, exchanged(): return lax.all_to_all(value, 'z', split_axis=0, concat_axis=0, tiled=True)  36.1 us
    all_to_all x4, starting transfers between devices, exchanged(): return lax.all_to_all(value, 'z', split_axis=0, concat_axis=0, tiled=True)  26 us
    pallas_call x6, Pallas kernels, down(): pl.pallas_call(functools.partial(down_kernel, len(hidden), added, split),...  19.9 us
    ppermute x16, starting transfers between devices, shifted(): lax.ppermute(value, axis, [(i, (i + by) % peers) for i in range(peers)])  19.1 us
    pallas_call x3, Pallas kernels, up(): pl.pallas_call(functools.partial(up_kernel, count), grid=(depth // UP_STE...  17.9 us
    unnamed x33, local copies, waits for them, and re-layouts  7.03 us
    ppermute x2, starting transfers between devices, section_step(): lax.ppermute(delta, 'section', [(i, i + 1) for i in range(sections - 1)])  6.38 us
  transfers between devices with their start and end apart: 23, of which 11 were waited for; matrix products, arithmetic and copies ran while one was open for 5% of the time, Pallas kernels for 20%

commit v1 on v0

--- a/solution.py
+++ b/solution.py
@@ -13,10 +13,9 @@
 SAMP_DEV = 8
 ROW_CHUNKS = 2
 FEATURE_CHUNKS = 2
-UP_STEP = 512
-DOWN_STEP = 512
+TILE = 256
 SMALL_VMEM = 8 << 20
-LARGE_VMEM = 28 << 20
+LARGE_VMEM = 12 << 20
 BF16 = jnp.bfloat16
 F32 = jnp.float32
 
@@ -75,45 +74,59 @@
     return out[:-1], out[-1]
 
 
+def stage_kernel(own_ref, other_ref, own_out_ref, other_out_ref, sems):
+    copies = [
+        pltpu.make_async_copy(own_ref, own_out_ref, sems.at[0]),
+        pltpu.make_async_copy(other_ref, other_out_ref, sems.at[1]),
+    ]
+    for copy in copies:
+        copy.start()
+    for copy in copies:
+        copy.wait()
+
+
+def stage(own, other):
+    return pl.pallas_call(
+        stage_kernel,
+        in_specs=[pl.BlockSpec(memory_space=pl.ANY)] * 2,
+        out_specs=[pl.BlockSpec(memory_space=pltpu.VMEM)] * 2,
+        out_shape=[jax.ShapeDtypeStruct(own.shape, BF16)] * 2,
+        scratch_shapes=[pltpu.SemaphoreType.DMA((2,))],
+        compiler_params=pltpu.CompilerParams(vmem_limit_bytes=LARGE_VMEM),
+        cost_estimate=pl.CostEstimate(
+            flops=1000000, bytes_accessed=8 * own.size, transcendentals=0
+        ),
+    )(own, other)
+
+
+def beside(first_ref, second_ref, start, stop):
+    width = first_ref.shape[1]
+    if stop <= width:
+        return first_ref[:, start:stop]
+    if start >= width:
+        return second_ref[:, start - width : stop - width]
+    return jnp.concatenate([first_ref[:, start:], second_ref[:, : stop - width]], axis=1)
+
+
 def up_kernel(count, *refs):
-    row_refs, own_ref, other_ref = refs[:count], refs[count], refs[count + 1]
-    out_refs, total_ref = refs[count + 2 : -1], refs[-1]
-    step = pl.program_id(0)
+    row_refs, own_ref, other_ref, out_refs = refs[:count], refs[count], refs[count + 1], refs[count + 2 :]
     rows = jnp.concatenate([ref[...] for ref in row_refs], axis=0)
-    weights = jnp.concatenate([own_ref[...], other_ref[...]], axis=1)
-    term = jnp.dot(rows, weights, preferred_element_type=F32)
-
-    @pl.when(step == 0)
-    def _():
-        total_ref[...] = term
-
-    @pl.when((step > 0) & (step < pl.num_programs(0) - 1))
-    def _():
-        total_ref[...] += term
-
-    @pl.when(step == pl.num_programs(0) - 1)
-    def _():
-        value = total_ref[...] + term
+    for start in range(0, 2 * own_ref.shape[1], TILE):
+        weights = beside(own_ref, other_ref, start, start + TILE)
+        value = jnp.dot(rows, weights, preferred_element_type=F32)
         hidden = (value / (1.0 + jnp.exp(-value))).astype(BF16)
         at = 0
         for ref in out_refs:
-            ref[...] = hidden[at : at + ref.shape[0]]
+            ref[:, start : start + TILE] = hidden[at : at + ref.shape[0]]
             at += ref.shape[0]
 
 
 def up(blocks, own, other):
     depth, units = own.shape
-    count = len(blocks)
     total = sum(block.shape[0] for block in blocks)
-    weight = pl.BlockSpec((UP_STEP, units), lambda k: (k, 0))
     return pl.pallas_call(
-        functools.partial(up_kernel, count),
-        grid=(depth // UP_STEP,),
-        in_specs=[pl.BlockSpec((block.shape[0], UP_STEP), lambda k: (0, k)) for block in blocks]
-        + [weight, weight],
-        out_specs=[pl.BlockSpec((block.shape[0], 2 * units), lambda k: (0, 0)) for block in blocks],
+        functools.partial(up_kernel, len(blocks)),
         out_shape=[jax.ShapeDtypeStruct((block.shape[0], 2 * units), BF16) for block in blocks],
-        scratch_shapes=[pltpu.VMEM((total, 2 * units), F32)],
         compiler_params=pltpu.CompilerParams(vmem_limit_bytes=LARGE_VMEM),
         cost_estimate=pl.CostEstimate(
             flops=4 * total * depth * units,
@@ -123,38 +136,40 @@
     )(*blocks, own, other)
 
 
-def down_kernel(count, added, split, *refs):
+def down_kernel(count, chunk, added, split, *refs):
     hidden_refs, own_ref, other_ref = refs[:count], refs[count], refs[count + 1]
     extra_refs = refs[count + 2 : len(refs) - len(added)]
     out_refs = refs[len(refs) - len(added) :]
     hidden = jnp.concatenate([ref[...] for ref in hidden_refs], axis=0)
-    weights = jnp.concatenate([own_ref[...], other_ref[...]], axis=0)
-    term = jnp.dot(hidden, weights, preferred_element_type=F32)
     rows = hidden_refs[0].shape[0]
-    at = 0
-    for parts, out_ref in zip(added, out_refs):
-        for number, operands in enumerate(parts):
-            value = term[at : at + rows]
-            for which, lead in operands:
-                extra = extra_refs[which]
-                value += (extra[...] if lead is None else extra[lead]).astype(F32)
-            value = value.astype(BF16)
-            if split:
-                out_ref[:, number] = value.reshape(out_ref.shape[0], *out_ref.shape[2:])
-            elif len(parts) == 1:
-                out_ref[...] = value
-            else:
-                out_ref[number] = value
-            at += rows
+    width = out_refs[0].shape[-1]
+    for start in range(0, width, TILE):
+        here = slice(start, start + TILE)
+        there = slice(chunk * width + start, chunk * width + start + TILE)
+        weights = jnp.concatenate([own_ref[:, there], other_ref[:, there]], axis=0)
+        term = jnp.dot(hidden, weights, preferred_element_type=F32)
+        at = 0
+        for parts, out_ref in zip(added, out_refs):
+            for number, operands in enumerate(parts):
+                value = term[at : at + rows]
+                for which, lead in operands:
+                    extra = extra_refs[which]
+                    value += (extra[:, here] if lead is None else extra[lead, :, here]).astype(F32)
+                value = value.astype(BF16)
+                if split:
+                    out_ref[:, number, :, here] = value.reshape(split, rows // split, TILE)
+                elif len(parts) == 1:
+                    out_ref[:, here] = value
+                else:
+                    out_ref[number, :, here] = value
+                at += rows
 
 
 def down(hidden, own, other, chunk, added, extras=(), split=0):
     rows, units = hidden[0].shape
     units //= 2
     width = own.shape[1] // FEATURE_CHUNKS
-    steps = width // DOWN_STEP
-    weight = pl.BlockSpec((units, DOWN_STEP), lambda n: (0, chunk * steps + n))
-    out_shape, out_specs = [], []
+    out_shape = []
     for parts in added:
         if split:
             lead = (split, len(parts), rows // split)
@@ -163,22 +178,9 @@
         else:
             lead = (len(parts), rows)
         out_shape.append(jax.ShapeDtypeStruct(lead + (width,), BF16))
-        out_specs.append(
-            pl.BlockSpec(lead + (DOWN_STEP,), lambda n, lead=lead: (0,) * len(lead) + (n,))
-        )
     total = rows * len(hidden)
     return pl.pallas_call(
-        functools.partial(down_kernel, len(hidden), added, split),
-        grid=(steps,),
-        in_specs=[pl.BlockSpec((rows, 2 * units), lambda n: (0, 0)) for _ in hidden]
-        + [weight, weight]
-        + [
-            pl.BlockSpec(
-                extra.shape[:-1] + (DOWN_STEP,), lambda n, rank=extra.ndim: (0,) * (rank - 1) + (n,)
-            )
-            for extra in extras
-        ],
-        out_specs=out_specs,
+        functools.partial(down_kernel, len(hidden), chunk, added, split),
         out_shape=out_shape,
         compiler_params=pltpu.CompilerParams(vmem_limit_bytes=LARGE_VMEM),
         cost_estimate=pl.CostEstimate(
@@ -239,6 +241,8 @@
     blocks = [exchanged(chunk.reshape(z_count, -1, width)).reshape(-1, width) for chunk in chunks]
     up_other = shifted(up_own, "core", 1)
     down_other = shifted(down_own, "core", 1)
+    up_own, up_other = stage(up_own, up_other)
+    down_own, down_other = stage(down_own, down_other)
     from_left = [shifted(block, "x", 1) for block in blocks]
     from_right = [shifted(block, "x", -1) for block in blocks]
     far = [shifted(from_left[0], "x", 1), shifted(from_right[1], "x", -1)]

time: 194 us -> 184 us (0.948)
  Pallas kernels: 40.1 us -> 28 us
  local copies, waits for them, and re-layouts: 12.7 us -> 15.4 us
    pallas_call x9 -> x11, Pallas kernels: 37.8 us -> 25.7 us  [the longest x6 12.3 us: down(): pl.pallas_call(functools.partial(down_kernel, len(hidden), chunk, added,...]
    unnamed x33 -> x41, local copies, waits for them, and re-layouts: 7.03 us -> 9.73 us
  transfers between devices with their start and end apart: 23 -> 23, of which waited for: 11 -> 13; matrix products, arithmetic and copies ran while one was open for 5% -> 6% of each run, Pallas kernels for 20% -> 15%
where the time goes in v1:
time: 184 us; the launch traced here: 183 us
  waiting for transfers between devices  76.7 us (42%)
  starting transfers between devices  56.1 us (30%)
  Pallas kernels  28 us (15%)
  local copies, waits for them, and re-layouts  15.4 us (8%)
  other arithmetic  5.58 us (3%)
    ppermute x16, waiting for transfers between devices, shifted(): lax.ppermute(value, axis, [(i, (i + by) % peers) for i in range(peers)])  37.1 us
    all_to_all x4, waiting for transfers between devices, exchanged(): return lax.all_to_all(value, 'z', split_axis=0, concat_axis=0, tiled=True)  35.4 us
    all_to_all x4, starting transfers between devices, exchanged(): return lax.all_to_all(value, 'z', split_axis=0, concat_axis=0, tiled=True)  26 us
    ppermute x16, starting transfers between devices, shifted(): lax.ppermute(value, axis, [(i, (i + by) % peers) for i in range(peers)])  19.2 us
    pallas_call x6, Pallas kernels, down(): pl.pallas_call(functools.partial(down_kernel, len(hidden), chunk, added,...  12.3 us
    unnamed x41, local copies, waits for them, and re-layouts  9.73 us
    pallas_call x3, Pallas kernels, up(): pl.pallas_call(functools.partial(up_kernel, len(blocks)), out_shape=[jax....  8.62 us
    ppermute x2, starting transfers between devices, section_step(): lax.ppermute(delta, 'section', [(i, i + 1) for i in range(sections - 1)])  6.38 us
  transfers between devices with their start and end apart: 23, of which 13 were waited for; matrix products, arithmetic and copies ran while one was open for 6% of the time, Pallas kernels for 15%

profile of v1, /device:TPU:22, one launch (start us, length us, event | category | flops | bytes accessed | tf_op | source)
XLA Modules:
  0.0 182.8 jit_solution(11724963374638314011)
XLA Ops:
  0.7 1.1 copy-done.11
  1.7 0.7 copy-done.14
  2.4 1.4 group_rows.1
  3.8 8.5 %all-to-all-start = ((bf16[8,16,2048]{2,1,0:T(8,128)(2,1)}), bf16[8,16,2048]{2,1,0:T(8,128)(2,1)S(1)}, u32[]{:S(2)}, u32[]{:S(2)}) async-start(bf16[8,16,2048]{2,1,0:T(8,128)(2,1)} %bitcast.9), calls=%async_computation | async-start | bytes 1048576 | tf_op jit(solution)/shard_map/all_to_all | solution.py:29
  12.3 0.5 collective-permute-start.5
  12.8 17.0 %all-to-all-done = bf16[8,16,2048]{2,1,0:T(8,128)(2,1)S(1)} async-done(((bf16[8,16,2048]{2,1,0:T(8,128)(2,1)}), bf16[8,16,2048]{2,1,0:T(8,128)(2,1)S(1)}, u32[]{:S(2)}, u32[]{:S(2)}) %all-to-all-start) | async-done | bytes 524320 | tf_op jit(solution)/shard_map/all_to_all | solution.py:29
  29.8 3.5 %all-to-all-start.2 = ((bf16[8,16,2048]{2,1,0:T(8,128)(2,1)}), bf16[8,16,2048]{2,1,0:T(8,128)(2,1)S(1)}, u32[]{:S(2)}, u32[]{:S(2)}) async-start(bf16[8,16,2048]{2,1,0:T(8,128)(2,1)} %bitcast.17), calls=%async_computation.2 | async-start | bytes 1048576 | tf_op jit(solution)/shard_map/all_to_all | solution.py:29
  33.3 0.8 and_select_fusion.2
  34.1 0.1 select_reduce_fusion.1
  34.2 0.6 gather_fusion.1
  34.8 1.7 gather_fusion
  36.5 2.7 %pad_maximum_fusion = bf16[16,2,16,2048]{3,2,1,0:T(8,128)(2,1)} fusion(bf16[16,1,16,2048]{3,2,1,0:T(8,128)(2,1)S(1)} %bitcast.60, bf16[16,1,16,2048]{3,2,1,0:T(8,128)(2,1)} %bitcast.61), kind=kLoop, calls=%fused_computation.3 | loop fusion | flops 1048576 | bytes 4194304 | tf_op jit(solution)/shard_map/concatenate | solution.py:299
  39.2 12.0 %all-to-all-done.2 = bf16[8,16,2048]{2,1,0:T(8,128)(2,1)S(1)} async-done(((bf16[8,16,2048]{2,1,0:T(8,128)(2,1)}), bf16[8,16,2048]{2,1,0:T(8,128)(2,1)S(1)}, u32[]{:S(2)}, u32[]{:S(2)}) %all-to-all-start.2) | async-done | bytes 524320 | tf_op jit(solution)/shard_map/all_to_all | solution.py:29
  51.2 4.5 %all-to-all-start.1 = ((bf16[16,2,16,2048]{3,2,1,0:T(8,128)(2,1)}), bf16[16,2,16,2048]{3,2,1,0:T(8,128)(2,1)}, u32[]{:S(2)}, u32[]{:S(2)}) async-start(bf16[16,2,16,2048]{3,2,1,0:T(8,128)(2,1)} %pad_maximum_fusion), calls=%async_computation.1 | async-start | bytes 4194304 | tf_op jit(solution)/shard_map/all_to_all | solution.py:307
  55.6 0.5 collective-permute-start
  56.2 1.6 collective-permute-start.4
  57.7 12.0 %collective-permute-done.refs_1_ = bf16[128,2048]{1,0:T(8,128)(2,1)S(1)} collective-permute-done((bf16[128,2048]{1,0:T(8,128)(2,1)S(1)}, bf16[128,2048]{1,0:T(8,128)(2,1)S(1)}, u32[]{:S(2)}, u32[]{:S(2)}) %collective-permute-start) | collective-permute-done | bytes 524320 | tf_op jit(solution)/shard_map/ppermute | solution.py:25
  69.7 1.7 collective-permute-start.6
  71.4 0.3 collective-permute-start.7
  71.7 2.9 %collective-permute-start.3 = (bf16[128,2048]{1,0:T(8,128)(2,1)S(1)}, bf16[128,2048]{1,0:T(8,128)(2,1)S(1)}, u32[]{:S(2)}, u32[]{:S(2)}) collective-permute-start(bf16[128,2048]{1,0:T(8,128)(2,1)S(1)} %bitcast.54), channel_id=1, source_target_pairs={{0,1},{1,2},{2,3},{3,0},{4,5},{5,6},{6,7},{7,4},{8,9},{9,10},{10,1... | collective-permute-start | bytes 1572872 | tf_op jit(solution)/shard_map/ppermute | solution.py:25
  74.6 2.0 %copy-done.7 = bf16[1,2048,896]{2,1,0:T(8,128)(2,1)S(1)} copy-done((bf16[1,2048,896]{2,1,0:T(8,128)(2,1)S(1)}, bf16[1,2048,896]{2,1,0:T(8,128)(2,1)}, u32[]{:S(2)}) %copy-start.7) | copy-done | bytes 3670040
  76.7 2.4 %shard_map.104 = (bf16[2048,896]{1,0:T(8,128)(2,1)S(1)}, bf16[2048,896]{1,0:T(8,128)(2,1)S(1)}) custom-call(bf16[2048,896]{1,0:T(8,128)(2,1)S(1)} %bitcast.43, bf16[2048,896]{1,0:T(8,128)(2,1)} %collective-permute-done.2.other_ref), custom_call_target="tpu_custom_call" | custom-call | flops 1000000 | bytes 14680064 | tf_op jit(solution)/shard_map/pallas_call | solution.py:89
  79.1 0.7 copy-done.8
  79.8 2.3 %shard_map.107 = (bf16[896,2048]{1,0:T(8,128)(2,1)S(1)}, bf16[896,2048]{1,0:T(8,128)(2,1)S(1)}) custom-call(bf16[896,2048]{1,0:T(8,128)(2,1)S(1)} %bitcast.45, bf16[896,2048]{1,0:T(8,128)(2,1)} %collective-permute-done.5.other_ref), custom_call_target="tpu_custom_call" | custom-call | flops 1000000 | bytes 14680064 | tf_op jit(solution)/shard_map/pallas_call | solution.py:89
  82.1 2.4 %collective-permute-done.6.refs_0_ = bf16[128,2048]{1,0:T(8,128)(2,1)S(1)} collective-permute-done((bf16[128,2048]{1,0:T(8,128)(2,1)S(1)}, bf16[128,2048]{1,0:T(8,128)(2,1)S(1)}, u32[]{:S(2)}, u32[]{:S(2)}) %collective-permute-start.6) | collective-permute-done | bytes 524320 | tf_op jit(solution)/shard_map/ppermute | solution.py:25
  84.5 2.9 %collective-permute-done.7.refs_1_ = bf16[128,2048]{1,0:T(8,128)(2,1)S(1)} collective-permute-done((bf16[128,2048]{1,0:T(8,128)(2,1)S(1)}, bf16[128,2048]{1,0:T(8,128)(2,1)S(1)}, u32[]{:S(2)}, u32[]{:S(2)}) %collective-permute-start.7) | collective-permute-done | bytes 524320 | tf_op jit(solution)/shard_map/ppermute | solution.py:25
  87.4 2.1 %shard_map.108 = (bf16[128,1792]{1,0:T(8,128)(2,1)S(1)}, bf16[128,1792]{1,0:T(8,128)(2,1)S(1)}) custom-call(bf16[128,2048]{1,0:T(8,128)(2,1)S(1)} %collective-permute-done.6.refs_0_, bf16[128,2048]{1,0:T(8,128)(2,1)S(1)} %collective-permute-done.7.refs_1_, bf16[2048,896]{1,0:T(8,128)(2,1)S(1)} %get-tuple-element.34.refs_3_.refs_2_, ...), custom_call_target="tpu_custom_call" | custom-call | flops 1879048192 | bytes 8388608 | tf_op jit(solution)/shard_map/pallas_call | solution.py:127
  89.5 1.1 shard_map.109
  90.8 3.2 %collective-permute-start.9 = (bf16[128,1024]{1,0:T(8,128)(2,1)S(1)}, bf16[128,1024]{1,0:T(8,128)(2,1)S(1)}, u32[]{:S(2)}, u32[]{:S(2)}) collective-permute-start(bf16[128,1024]{1,0:T(8,128)(2,1)S(1)} %get-tuple-element.47), channel_id=1, source_target_pairs={{0,1},{1,2},{2,3},{3,0},{4,5},{5,6},{6,7},{7,4},{8,9},{9,10},{10,1... | collective-permute-start | bytes 786440 | tf_op jit(solution)/shard_map/ppermute | solution.py:25
  94.0 1.8 collective-permute-done.3.refs_1_
  95.7 3.2 %shard_map.106 = (bf16[128,1792]{1,0:T(8,128)(2,1)S(1)}, bf16[128,1792]{1,0:T(8,128)(2,1)S(1)}, bf16[128,1792]{1,0:T(8,128)(2,1)S(1)}) custom-call(bf16[128,2048]{1,0:T(8,128)(2,1)S(1)} %bitcast.55, bf16[128,2048]{1,0:T(8,128)(2,1)S(1)} %collective-permute-done.3.refs_1_, bf16[128,2048]{1,0:T(8,128)(2,1)S(1)} %collective-permute-done.4.refs_2_, ...), custom_call_target="tpu_custom_call" | custom-call | flops 2818572288 | bytes 8912896 | tf_op jit(solution)/shard_map/pallas_call | solution.py:127
  99.0 3.2 %shard_map.105 = (bf16[128,1792]{1,0:T(8,128)(2,1)S(1)}, bf16[128,1792]{1,0:T(8,128)(2,1)S(1)}, bf16[128,1792]{1,0:T(8,128)(2,1)S(1)}) custom-call(bf16[128,2048]{1,0:T(8,128)(2,1)S(1)} %bitcast.58, bf16[128,2048]{1,0:T(8,128)(2,1)S(1)} %collective-permute-done.refs_1_, bf16[128,2048]{1,0:T(8,128)(2,1)S(1)} %collective-permute-done.1.refs_2_, ...), custom_call_target="tpu_custom_call" | custom-call | flops 2818572288 | bytes 8912896 | tf_op jit(solution)/shard_map/pallas_call | solution.py:127
  102.2 0.1 collective-permute-done.8.refs_6_
  102.4 2.1 %shard_map.110 = (bf16[2,128,1024]{2,1,0:T(8,128)(2,1)S(1)}, bf16[2,128,1024]{2,1,0:T(8,128)(2,1)S(1)}) custom-call(bf16[128,1792]{1,0:T(8,128)(2,1)S(1)} %get-tuple-element.40.refs_0_, bf16[128,1792]{1,0:T(8,128)(2,1)S(1)} %get-tuple-element.41.refs_1_, bf16[128,1792]{1,0:T(8,128)(2,1)S(1)} %get-tuple-element.42.refs_2_, ...), custom_call_target="tpu_custom_call" | custom-call | flops 1879048192 | bytes 4718592 | tf_op jit(solution)/shard_map/pallas_call | solution.py:182
  104.5 2.8 %collective-permute-start.10 = (bf16[2,128,1024]{2,1,0:T(8,128)(2,1)S(1)}, bf16[2,128,1024]{2,1,0:T(8,128)(2,1)S(1)}, u32[]{:S(2)}, u32[]{:S(2)}) collective-permute-start(bf16[2,128,1024]{2,1,0:T(8,128)(2,1)S(1)} %get-tuple-element.48), channel_id=1, source_target_pairs={{0,1},{1,2},{2,3},{3,0},{4,5},{5,6},{6,7},{7,4},{8,9},{9,10},{10,1... | collective-permute-start | bytes 1572872 | tf_op jit(solution)/shard_map/ppermute | solution.py:25
  107.3 1.9 %shard_map.113 = (bf16[128,1024]{1,0:T(8,128)(2,1)}, bf16[128,1024]{1,0:T(8,128)(2,1)}) custom-call(bf16[128,1792]{1,0:T(8,128)(2,1)S(1)} %get-tuple-element.44.refs_0_, bf16[128,1792]{1,0:T(8,128)(2,1)S(1)} %get-tuple-element.45.refs_1_, bf16[896,2048]{1,0:T(8,128)(2,1)S(1)} %get-tuple-element.38.refs_2_.refs_4_, ...), custom_call_target="tpu_custom_call" | custom-call | flops 939524096 | bytes 4194304 | tf_op jit(solution)/shard_map/pallas_call | solution.py:182
  109.2 3.2 %collective-permute-start.14 = (bf16[128,1024]{1,0:T(8,128)(2,1)}, bf16[128,1024]{1,0:T(8,128)(2,1)}, u32[]{:S(2)}, u32[]{:S(2)}) collective-permute-start(bf16[128,1024]{1,0:T(8,128)(2,1)} %get-tuple-element.52), channel_id=1, source_target_pairs={{0,1},{1,2},{2,3},{3,0},{4,5},{5,6},{6,7},{7,4},{8,9},{9,10},{10,1... | collective-permute-start | bytes 786440 | tf_op jit(solution)/shard_map/ppermute | solution.py:25
  112.5 6.9 %collective-permute-done.10.refs_4_ = bf16[2,128,1024]{2,1,0:T(8,128)(2,1)S(1)} collective-permute-done((bf16[2,128,1024]{2,1,0:T(8,128)(2,1)S(1)}, bf16[2,128,1024]{2,1,0:T(8,128)(2,1)S(1)}, u32[]{:S(2)}, u32[]{:S(2)}) %collective-permute-start.10) | collective-permute-done | bytes 524320 | tf_op jit(solution)/shard_map/ppermute | solution.py:25
  119.4 2.6 %collective-permute-done.11.refs_5_ = bf16[2,128,1024]{2,1,0:T(8,128)(2,1)S(1)} collective-permute-done((bf16[2,128,1024]{2,1,0:T(8,128)(2,1)S(1)}, bf16[2,128,1024]{2,1,0:T(8,128)(2,1)S(1)}, u32[]{:S(2)}, u32[]{:S(2)}) %collective-permute-start.11) | collective-permute-done | bytes 524320 | tf_op jit(solution)/shard_map/ppermute | solution.py:25
  122.0 2.0 %shard_map.111 = bf16[8,2,16,1024]{3,2,1,0:T(8,128)(2,1)} custom-call(bf16[128,1792]{1,0:T(8,128)(2,1)S(1)} %get-tuple-element.36.refs_0_, bf16[128,1792]{1,0:T(8,128)(2,1)S(1)} %get-tuple-element.37.refs_1_, bf16[896,2048]{1,0:T(8,128)(2,1)S(1)} %get-tuple-element.38.refs_2_.refs_4_, bf16[896,2048]{1,0:T(8,128)(2,1)S(1)} %get-tuple-element.39.refs_3_.refs_5_, ...), custom_call_target="tpu_custom_call" | custom-call | flops 939524096 | bytes 4194304 | tf_op jit(solution)/shard_map/pallas_call | solution.py:182
  124.0 6.8 %all-to-all-start.3 = ((bf16[8,2,16,1024]{3,2,1,0:T(8,128)(2,1)}), bf16[8,2,16,1024]{3,2,1,0:T(8,128)(2,1)S(1)}, u32[]{:S(2)}, u32[]{:S(2)}) async-start(bf16[8,2,16,1024]{3,2,1,0:T(8,128)(2,1)} %shard_map.111), calls=%async_computation.3 | async-start | bytes 1048576 | tf_op jit(solution)/shard_map/all_to_all | solution.py:29
  131.0 0.1 copy.18
  131.1 0.1 copy.17
  131.2 2.0 %copy-done.2 = bf16[896,2048]{1,0:T(8,128)(2,1)S(1)} copy-done((bf16[896,2048]{1,0:T(8,128)(2,1)S(1)}, bf16[896,2048]{1,0:T(8,128)(2,1)}, u32[]{:S(2)}) %copy-start.2) | copy-done | bytes 3670040
  133.3 2.0 %copy-done.5 = bf16[896,2048]{1,0:T(8,128)(2,1)S(1)} copy-done((bf16[896,2048]{1,0:T(8,128)(2,1)S(1)}, bf16[896,2048]{1,0:T(8,128)(2,1)}, u32[]{:S(2)}) %copy-start.5) | copy-done | bytes 3670040
  135.3 1.0 copy-done.10
  136.3 3.3 %shard_map.114 = (bf16[2,128,1024]{2,1,0:T(8,128)(2,1)S(1)}, bf16[2,128,1024]{2,1,0:T(8,128)(2,1)S(1)}) custom-call(bf16[128,1792]{1,0:T(8,128)(2,1)S(1)} %get-tuple-element.40.refs_0_, bf16[128,1792]{1,0:T(8,128)(2,1)S(1)} %get-tuple-element.41.refs_1_, bf16[128,1792]{1,0:T(8,128)(2,1)S(1)} %copy-done.10, bf16[128,1792]{1,0:T(8,128)(2,1)S(1)} %get-tuple-element.43.refs_3_, ...), custom_call_target="tpu_custom_call" | custom-call | flops 1879048192 | bytes 4718592 | tf_op jit(solution)/shard_map/pallas_call | solution.py:182
  139.6 0.6 collective-permute-start.15
  140.2 1.7 collective-permute-start.16
  141.9 0.2 select_reduce_fusion
  142.2 6.9 %collective-permute-done.15.refs_4_ = bf16[2,128,1024]{2,1,0:T(8,128)(2,1)S(1)} collective-permute-done((bf16[2,128,1024]{2,1,0:T(8,128)(2,1)S(1)}, bf16[2,128,1024]{2,1,0:T(8,128)(2,1)S(1)}, u32[]{:S(2)}, u32[]{:S(2)}) %collective-permute-start.15) | collective-permute-done | bytes 524320 | tf_op jit(solution)/shard_map/ppermute | solution.py:25
  149.1 1.5 collective-permute-done.16.refs_5_
  150.6 2.0 %shard_map.115 = bf16[8,2,16,1024]{3,2,1,0:T(8,128)(2,1)} custom-call(bf16[128,1792]{1,0:T(8,128)(2,1)S(1)} %get-tuple-element.36.refs_0_, bf16[128,1792]{1,0:T(8,128)(2,1)S(1)} %get-tuple-element.37.refs_1_, bf16[896,2048]{1,0:T(8,128)(2,1)S(1)} %copy-done.3, bf16[896,2048]{1,0:T(8,128)(2,1)S(1)} %copy-done.6, ...), custom_call_target="tpu_custom_call" | custom-call | flops 939524096 | bytes 4194304 | tf_op jit(solution)/shard_map/pallas_call | solution.py:182
  152.6 7.2 %all-to-all-start.4 = ((bf16[8,2,16,1024]{3,2,1,0:T(8,128)(2,1)}), bf16[8,2,16,1024]{3,2,1,0:T(8,128)(2,1)S(1)}, u32[]{:S(2)}, u32[]{:S(2)}) async-start(bf16[8,2,16,1024]{3,2,1,0:T(8,128)(2,1)} %shard_map.115), calls=%async_computation.4 | async-start | bytes 1048576 | tf_op jit(solution)/shard_map/all_to_all | solution.py:29
  159.8 2.2 %gather_fusion.2 = bf16[8,2,16,2048]{3,2,1,0:T(8,128)(2,1)S(1)} fusion(bf16[16,2,16,2048]{3,2,1,0:T(8,128)(2,1)} %all-to-all-done.1, s32[1024]{0:T(1024)S(1)} %pad_clamp_fusion), kind=kCustom, calls=%fused_computation.2 | custom fusion | bytes 2097184 | tf_op jit(solution)/shard_map/gather | solution.py:308
  162.0 0.9 fusion.8
  163.0 0.5 shard_map.112
  163.4 3.2 %collective-permute-start.12 = (bf16[128,1024]{1,0:T(8,128)(2,1)S(1)}, bf16[128,1024]{1,0:T(8,128)(2,1)S(1)}, u32[]{:S(2)}, u32[]{:S(2)}) collective-permute-start(bf16[128,1024]{1,0:T(8,128)(2,1)S(1)} %get-tuple-element.50), channel_id=1, source_target_pairs={{0,64},{64,128},{128,192},{1,65},{65,129},{129,193},{2,66},{66,130... | collective-permute-start | bytes 786440 | tf_op jit(solution)/shard_map/ppermute | solution.py:323
  166.6 6.5 %all-to-all-done.4 = bf16[8,2,16,1024]{3,2,1,0:T(8,128)(2,1)S(1)} async-done(((bf16[8,2,16,1024]{3,2,1,0:T(8,128)(2,1)}), bf16[8,2,16,1024]{3,2,1,0:T(8,128)(2,1)S(1)}, u32[]{:S(2)}, u32[]{:S(2)}) %all-to-all-start.4) | async-done | bytes 524320 | tf_op jit(solution)/shard_map/all_to_all | solution.py:29
  173.1 0.5 shard_map.116
  173.6 3.2 %collective-permute-start.17 = (bf16[128,1024]{1,0:T(8,128)(2,1)S(1)}, bf16[128,1024]{1,0:T(8,128)(2,1)S(1)}, u32[]{:S(2)}, u32[]{:S(2)}) collective-permute-start(bf16[128,1024]{1,0:T(8,128)(2,1)S(1)} %get-tuple-element.55), channel_id=1, source_target_pairs={{0,64},{64,128},{128,192},{1,65},{65,129},{129,193},{2,66},{66,130... | collective-permute-start | bytes 786440 | tf_op jit(solution)/shard_map/ppermute | solution.py:323
  176.8 0.8 maximum_bitcast_fusion
  177.6 4.2 %collective-permute-done.17 = bf16[128,1024]{1,0:T(8,128)(2,1)S(1)} collective-permute-done((bf16[128,1024]{1,0:T(8,128)(2,1)S(1)}, bf16[128,1024]{1,0:T(8,128)(2,1)S(1)}, u32[]{:S(2)}, u32[]{:S(2)}) %collective-permute-start.17) | collective-permute-done | bytes 262176 | tf_op jit(solution)/shard_map/ppermute | solution.py:323
  181.8 0.9 fusion
  (57 shorter events, 0.4 us)
Async XLA Ops:
  0.6 33.5 %copy-start = (bf16[1,128,2048]{2,1,0:T(8,128)(2,1)S(1)}, bf16[1,128,2048]{2,1,0:T(8,128)(2,1)}, u32[]{:S(2)}) copy-start(bf16[1,128,2048]{2,1,0:T(8,128)(2,1)} %param.10) | copy-start | bytes 1572868
  0.6 1.1 copy-start.11
  1.7 0.7 copy-start.14
  2.4 32.4 %copy-start.15 = (bf16[1,128,2048]{2,1,0:T(8,128)(2,1)S(1)}, bf16[1,128,2048]{2,1,0:T(8,128)(2,1)}, u32[]{:S(2)}) copy-start(bf16[1,128,2048]{2,1,0:T(8,128)(2,1)} %param.11) | copy-start | bytes 1572868
  3.8 26.0 %all-to-all-start = ((bf16[8,16,2048]{2,1,0:T(8,128)(2,1)}), bf16[8,16,2048]{2,1,0:T(8,128)(2,1)S(1)}, u32[]{:S(2)}, u32[]{:S(2)}) async-start(bf16[8,16,2048]{2,1,0:T(8,128)(2,1)} %bitcast.9), calls=%async_computation | async-start | bytes 1048576 | tf_op jit(solution)/shard_map/all_to_all | solution.py:29
  12.3 62.3 %collective-permute-start.2 = (bf16[2048,896]{1,0:T(8,128)(2,1)}, bf16[2048,896]{1,0:T(8,128)(2,1)}, u32[]{:S(2)}, u32[]{:S(2)}) collective-permute-start(bf16[2048,896]{1,0:T(8,128)(2,1)} %bitcast.42), channel_id=1, source_target_pairs={{0,4},{4,0},{1,5},{5,1},{2,6},{6,2},{3,7},{7,3},{8,12},{12,8},{9,1... | collective-permute-start | bytes 11010056 | tf_op jit(solution)/shard_map/ppermute | solution.py:25
  12.3 66.9 %collective-permute-start.5 = (bf16[896,2048]{1,0:T(8,128)(2,1)}, bf16[896,2048]{1,0:T(8,128)(2,1)}, u32[]{:S(2)}, u32[]{:S(2)}) collective-permute-start(bf16[896,2048]{1,0:T(8,128)(2,1)} %bitcast.44), channel_id=1, source_target_pairs={{0,4},{4,0},{1,5},{5,1},{2,6},{6,2},{3,7},{7,3},{8,12},{12,8},{9,1... | collective-permute-start | bytes 11010056 | tf_op jit(solution)/shard_map/ppermute | solution.py:25
  29.8 21.4 %all-to-all-start.2 = ((bf16[8,16,2048]{2,1,0:T(8,128)(2,1)}), bf16[8,16,2048]{2,1,0:T(8,128)(2,1)S(1)}, u32[]{:S(2)}, u32[]{:S(2)}) async-start(bf16[8,16,2048]{2,1,0:T(8,128)(2,1)} %bitcast.17), calls=%async_computation.2 | async-start | bytes 1048576 | tf_op jit(solution)/shard_map/all_to_all | solution.py:29
  51.2 28.0 %copy-start.12 = (bf16[8,16,2048]{2,1,0:T(8,128)(2,1)}, bf16[8,16,2048]{2,1,0:T(8,128)(2,1)S(1)}, u32[]{:S(2)}) copy-start(bf16[8,16,2048]{2,1,0:T(8,128)(2,1)S(1)} %all-to-all-done.2) | copy-start | bytes 1572868
  51.2 72.8 %all-to-all-start.1 = ((bf16[16,2,16,2048]{3,2,1,0:T(8,128)(2,1)}), bf16[16,2,16,2048]{3,2,1,0:T(8,128)(2,1)}, u32[]{:S(2)}, u32[]{:S(2)}) async-start(bf16[16,2,16,2048]{3,2,1,0:T(8,128)(2,1)} %pad_maximum_fusion), calls=%async_computation.1 | async-start | bytes 4194304 | tf_op jit(solution)/shard_map/all_to_all | solution.py:307
  55.6 14.1 %collective-permute-start = (bf16[128,2048]{1,0:T(8,128)(2,1)S(1)}, bf16[128,2048]{1,0:T(8,128)(2,1)S(1)}, u32[]{:S(2)}, u32[]{:S(2)}) collective-permute-start(bf16[128,2048]{1,0:T(8,128)(2,1)S(1)} %bitcast.56), channel_id=1, source_target_pairs={{0,1},{1,2},{2,3},{3,0},{4,5},{5,6},{6,7},{7,4},{8,9},{9,10},{10,1... | collective-permute-start | bytes 1572872 | tf_op jit(solution)/shard_map/ppermute | solution.py:25
  56.2 15.2 %collective-permute-start.4 = (bf16[128,2048]{1,0:T(8,128)(2,1)S(1)}, bf16[128,2048]{1,0:T(8,128)(2,1)S(1)}, u32[]{:S(2)}, u32[]{:S(2)}) collective-permute-start(bf16[128,2048]{1,0:T(8,128)(2,1)S(1)} %bitcast.53), channel_id=1, source_target_pairs={{0,3},{1,0},{2,1},{3,2},{4,7},{5,4},{6,5},{7,6},{8,11},{9,8},{10,9... | collective-permute-start | bytes 1572872 | tf_op jit(solution)/shard_map/ppermute | solution.py:25
  69.7 14.8 %collective-permute-start.6 = (bf16[128,2048]{1,0:T(8,128)(2,1)S(1)}, bf16[128,2048]{1,0:T(8,128)(2,1)S(1)}, u32[]{:S(2)}, u32[]{:S(2)}) collective-permute-start(bf16[128,2048]{1,0:T(8,128)(2,1)S(1)} %collective-permute-done.refs_1_), channel_id=1, source_target_pairs={{0,1},{1,2},{2,3},{3,0},{4,5},{5,6},{6,7},{7,4},{8,9},{9,10},{10,1... | collective-permute-start | bytes 1572872 | tf_op jit(solution)/shard_map/ppermute | solution.py:25
  71.4 16.0 %collective-permute-start.7 = (bf16[128,2048]{1,0:T(8,128)(2,1)S(1)}, bf16[128,2048]{1,0:T(8,128)(2,1)S(1)}, u32[]{:S(2)}, u32[]{:S(2)}) collective-permute-start(bf16[128,2048]{1,0:T(8,128)(2,1)S(1)} %collective-permute-done.4.refs_2_), channel_id=1, source_target_pairs={{0,3},{1,0},{2,1},{3,2},{4,7},{5,4},{6,5},{7,6},{8,11},{9,8},{10,9... | collective-permute-start | bytes 1572872 | tf_op jit(solution)/shard_map/ppermute | solution.py:25
  71.7 24.0 %collective-permute-start.3 = (bf16[128,2048]{1,0:T(8,128)(2,1)S(1)}, bf16[128,2048]{1,0:T(8,128)(2,1)S(1)}, u32[]{:S(2)}, u32[]{:S(2)}) collective-permute-start(bf16[128,2048]{1,0:T(8,128)(2,1)S(1)} %bitcast.54), channel_id=1, source_target_pairs={{0,1},{1,2},{2,3},{3,0},{4,5},{5,6},{6,7},{7,4},{8,9},{9,10},{10,1... | collective-permute-start | bytes 1572872 | tf_op jit(solution)/shard_map/ppermute | solution.py:25
  74.6 24.4 %collective-permute-start.1 = (bf16[128,2048]{1,0:T(8,128)(2,1)S(1)}, bf16[128,2048]{1,0:T(8,128)(2,1)S(1)}, u32[]{:S(2)}, u32[]{:S(2)}) collective-permute-start(bf16[128,2048]{1,0:T(8,128)(2,1)S(1)} %bitcast.57), channel_id=1, source_target_pairs={{0,3},{1,0},{2,1},{3,2},{4,7},{5,4},{6,5},{7,6},{8,11},{9,8},{10,9... | collective-permute-start | bytes 1572872 | tf_op jit(solution)/shard_map/ppermute | solution.py:25
  74.6 2.0 %copy-start.7 = (bf16[1,2048,896]{2,1,0:T(8,128)(2,1)S(1)}, bf16[1,2048,896]{2,1,0:T(8,128)(2,1)}, u32[]{:S(2)}) copy-start(bf16[1,2048,896]{2,1,0:T(8,128)(2,1)} %param.12) | copy-start | bytes 11010052
  76.7 3.1 %copy-start.8 = (bf16[1,896,2048]{2,1,0:T(8,128)(2,1)S(1)}, bf16[1,896,2048]{2,1,0:T(8,128)(2,1)}, u32[]{:S(2)}) copy-start(bf16[1,896,2048]{2,1,0:T(8,128)(2,1)} %param.13) | copy-start | bytes 11010052
  82.1 39.9 %copy-start.1 = (bf16[896,2048]{1,0:T(8,128)(2,1)}, bf16[896,2048]{1,0:T(8,128)(2,1)S(1)}, u32[]{:S(2)}) copy-start(bf16[896,2048]{1,0:T(8,128)(2,1)S(1)} %get-tuple-element.38.refs_2_.refs_4_) | copy-start | bytes 11010052
  82.1 39.9 %copy-start.4 = (bf16[896,2048]{1,0:T(8,128)(2,1)}, bf16[896,2048]{1,0:T(8,128)(2,1)S(1)}, u32[]{:S(2)}) copy-start(bf16[896,2048]{1,0:T(8,128)(2,1)S(1)} %get-tuple-element.39.refs_3_.refs_5_) | copy-start | bytes 11010052
  90.7 11.7 %collective-permute-start.8 = (bf16[128,1024]{1,0:T(8,128)(2,1)S(1)}, bf16[128,1024]{1,0:T(8,128)(2,1)S(1)}, u32[]{:S(2)}, u32[]{:S(2)}) collective-permute-start(bf16[128,1024]{1,0:T(8,128)(2,1)S(1)} %get-tuple-element.46), channel_id=1, source_target_pairs={{0,3},{1,0},{2,1},{3,2},{4,7},{5,4},{6,5},{7,6},{8,11},{9,8},{10,9... | collective-permute-start | bytes 786440 | tf_op jit(solution)/shard_map/ppermute | solution.py:25
  90.7 8.2 %copy-start.13 = (bf16[8,16,2048]{2,1,0:T(8,128)(2,1)S(1)}, bf16[8,16,2048]{2,1,0:T(8,128)(2,1)}, u32[]{:S(2)}) copy-start(bf16[8,16,2048]{2,1,0:T(8,128)(2,1)} %copy-done.12) | copy-start | bytes 1572868
  90.8 11.6 %collective-permute-start.9 = (bf16[128,1024]{1,0:T(8,128)(2,1)S(1)}, bf16[128,1024]{1,0:T(8,128)(2,1)S(1)}, u32[]{:S(2)}, u32[]{:S(2)}) collective-permute-start(bf16[128,1024]{1,0:T(8,128)(2,1)S(1)} %get-tuple-element.47), channel_id=1, source_target_pairs={{0,1},{1,2},{2,3},{3,0},{4,5},{5,6},{6,7},{7,4},{8,9},{9,10},{10,1... | collective-permute-start | bytes 786440 | tf_op jit(solution)/shard_map/ppermute | solution.py:25
  102.2 2.3 %copy-start.9 = (bf16[128,1792]{1,0:T(8,128)(2,1)}, bf16[128,1792]{1,0:T(8,128)(2,1)S(1)}, u32[]{:S(2)}) copy-start(bf16[128,1792]{1,0:T(8,128)(2,1)S(1)} %get-tuple-element.42.refs_2_) | copy-start | bytes 1376260
  104.5 14.9 %collective-permute-start.10 = (bf16[2,128,1024]{2,1,0:T(8,128)(2,1)S(1)}, bf16[2,128,1024]{2,1,0:T(8,128)(2,1)S(1)}, u32[]{:S(2)}, u32[]{:S(2)}) collective-permute-start(bf16[2,128,1024]{2,1,0:T(8,128)(2,1)S(1)} %get-tuple-element.48), channel_id=1, source_target_pairs={{0,1},{1,2},{2,3},{3,0},{4,5},{5,6},{6,7},{7,4},{8,9},{9,10},{10,1... | collective-permute-start | bytes 1572872 | tf_op jit(solution)/shard_map/ppermute | solution.py:25
  107.3 14.6 %collective-permute-start.11 = (bf16[2,128,1024]{2,1,0:T(8,128)(2,1)S(1)}, bf16[2,128,1024]{2,1,0:T(8,128)(2,1)S(1)}, u32[]{:S(2)}, u32[]{:S(2)}) collective-permute-start(bf16[2,128,1024]{2,1,0:T(8,128)(2,1)S(1)} %get-tuple-element.49), channel_id=1, source_target_pairs={{0,3},{1,0},{2,1},{3,2},{4,7},{5,4},{6,5},{7,6},{8,11},{9,8},{10,9... | collective-permute-start | bytes 1572872 | tf_op jit(solution)/shard_map/ppermute | solution.py:25
  109.2 22.0 %collective-permute-start.13 = (bf16[128,1024]{1,0:T(8,128)(2,1)}, bf16[128,1024]{1,0:T(8,128)(2,1)}, u32[]{:S(2)}, u32[]{:S(2)}) collective-permute-start(bf16[128,1024]{1,0:T(8,128)(2,1)} %get-tuple-element.51), channel_id=1, source_target_pairs={{0,3},{1,0},{2,1},{3,2},{4,7},{5,4},{6,5},{7,6},{8,11},{9,8},{10,9... | collective-permute-start | bytes 786440 | tf_op jit(solution)/shard_map/ppermute | solution.py:25
  109.2 22.0 %collective-permute-start.14 = (bf16[128,1024]{1,0:T(8,128)(2,1)}, bf16[128,1024]{1,0:T(8,128)(2,1)}, u32[]{:S(2)}, u32[]{:S(2)}) collective-permute-start(bf16[128,1024]{1,0:T(8,128)(2,1)} %get-tuple-element.52), channel_id=1, source_target_pairs={{0,1},{1,2},{2,3},{3,0},{4,5},{5,6},{6,7},{7,4},{8,9},{9,10},{10,1... | collective-permute-start | bytes 786440 | tf_op jit(solution)/shard_map/ppermute | solution.py:25
  122.0 8.8 %copy-start.19 = (s32[8]{0:T(128)S(1)}, s32[8]{0:T(128)}, u32[]{:S(2)}) copy-start(s32[8]{0:T(128)} %param.16) | copy-start | bytes 100
  122.0 9.0 %copy-start.18 = (s32[1,128,2]{1,2,0:T(2,128)S(1)}, s32[1,128,2]{1,2,0:T(2,128)}, u32[]{:S(2)}) copy-start(s32[1,128,2]{1,2,0:T(2,128)} %param.15) | copy-start | bytes 3076
  124.0 28.6 %all-to-all-start.3 = ((bf16[8,2,16,1024]{3,2,1,0:T(8,128)(2,1)}), bf16[8,2,16,1024]{3,2,1,0:T(8,128)(2,1)S(1)}, u32[]{:S(2)}, u32[]{:S(2)}) async-start(bf16[8,2,16,1024]{3,2,1,0:T(8,128)(2,1)} %shard_map.111), calls=%async_computation.3 | async-start | bytes 1048576 | tf_op jit(solution)/shard_map/all_to_all | solution.py:29
  131.1 10.8 %copy-start.17 = (s32[512]{0:T(512)S(1)}, s32[512]{0:T(512)}, u32[]{:S(2)}) copy-start(s32[512]{0:T(512)} %param.17) | copy-start | bytes 6148
  131.2 2.0 %copy-start.2 = (bf16[896,2048]{1,0:T(8,128)(2,1)S(1)}, bf16[896,2048]{1,0:T(8,128)(2,1)}, u32[]{:S(2)}) copy-start(bf16[896,2048]{1,0:T(8,128)(2,1)} %copy-done.1) | copy-start | bytes 11010052
  133.3 2.0 %copy-start.5 = (bf16[896,2048]{1,0:T(8,128)(2,1)S(1)}, bf16[896,2048]{1,0:T(8,128)(2,1)}, u32[]{:S(2)}) copy-start(bf16[896,2048]{1,0:T(8,128)(2,1)} %copy-done.4) | copy-start | bytes 11010052
  135.3 1.0 copy-start.10
  136.3 14.3 %copy-start.3 = (bf16[896,2048]{1,0:T(8,128)(2,1)S(1)}, bf16[896,2048]{1,0:T(8,128)(2,1)}, u32[]{:S(2)}) copy-start(bf16[896,2048]{1,0:T(8,128)(2,1)} %copy-done.1) | copy-start | bytes 11010052
  136.3 14.3 %copy-start.6 = (bf16[896,2048]{1,0:T(8,128)(2,1)S(1)}, bf16[896,2048]{1,0:T(8,128)(2,1)}, u32[]{:S(2)}) copy-start(bf16[896,2048]{1,0:T(8,128)(2,1)} %copy-done.4) | copy-start | bytes 11010052
  139.6 9.5 %collective-permute-start.15 = (bf16[2,128,1024]{2,1,0:T(8,128)(2,1)S(1)}, bf16[2,128,1024]{2,1,0:T(8,128)(2,1)S(1)}, u32[]{:S(2)}, u32[]{:S(2)}) collective-permute-start(bf16[2,128,1024]{2,1,0:T(8,128)(2,1)S(1)} %get-tuple-element.53), channel_id=1, source_target_pairs={{0,1},{1,2},{2,3},{3,0},{4,5},{5,6},{6,7},{7,4},{8,9},{9,10},{10,1... | collective-permute-start | bytes 1572872 | tf_op jit(solution)/shard_map/ppermute | solution.py:25
  140.2 10.4 %collective-permute-start.16 = (bf16[2,128,1024]{2,1,0:T(8,128)(2,1)S(1)}, bf16[2,128,1024]{2,1,0:T(8,128)(2,1)S(1)}, u32[]{:S(2)}, u32[]{:S(2)}) collective-permute-start(bf16[2,128,1024]{2,1,0:T(8,128)(2,1)S(1)} %get-tuple-element.54), channel_id=1, source_target_pairs={{0,3},{1,0},{2,1},{3,2},{4,7},{5,4},{6,5},{7,6},{8,11},{9,8},{10,9... | collective-permute-start | bytes 1572872 | tf_op jit(solution)/shard_map/ppermute | solution.py:25
  152.6 20.5 %all-to-all-start.4 = ((bf16[8,2,16,1024]{3,2,1,0:T(8,128)(2,1)}), bf16[8,2,16,1024]{3,2,1,0:T(8,128)(2,1)S(1)}, u32[]{:S(2)}, u32[]{:S(2)}) async-start(bf16[8,2,16,1024]{3,2,1,0:T(8,128)(2,1)} %shard_map.115), calls=%async_computation.4 | async-start | bytes 1048576 | tf_op jit(solution)/shard_map/all_to_all | solution.py:29
  162.9 18.9 %copy-start.16 = (bf16[8,1,16,2048]{3,2,1,0:T(8,128)(2,1)S(1)}, bf16[8,1,16,2048]{3,2,1,0:T(8,128)(2,1)}, u32[]{:S(2)}) copy-start(bf16[8,1,16,2048]{3,2,1,0:T(8,128)(2,1)} %get-tuple-element.59) | copy-start | bytes 1572868
  163.4 14.2 %collective-permute-start.12 = (bf16[128,1024]{1,0:T(8,128)(2,1)S(1)}, bf16[128,1024]{1,0:T(8,128)(2,1)S(1)}, u32[]{:S(2)}, u32[]{:S(2)}) collective-permute-start(bf16[128,1024]{1,0:T(8,128)(2,1)S(1)} %get-tuple-element.50), channel_id=1, source_target_pairs={{0,64},{64,128},{128,192},{1,65},{65,129},{129,193},{2,66},{66,130... | collective-permute-start | bytes 786440 | tf_op jit(solution)/shard_map/ppermute | solution.py:323
  173.6 8.3 %collective-permute-start.17 = (bf16[128,1024]{1,0:T(8,128)(2,1)S(1)}, bf16[128,1024]{1,0:T(8,128)(2,1)S(1)}, u32[]{:S(2)}, u32[]{:S(2)}) collective-permute-start(bf16[128,1024]{1,0:T(8,128)(2,1)S(1)} %get-tuple-element.55), channel_id=1, source_target_pairs={{0,64},{64,128},{128,192},{1,65},{65,129},{129,193},{2,66},{66,130... | collective-permute-start | bytes 786440 | tf_op jit(solution)/shard_map/ppermute | solution.py:323

commit v2 on v1

--- a/solution.py
+++ b/solution.py
@@ -256,26 +256,18 @@
 
     backs = []
     for f in range(FEATURE_CHUNKS):
-        far_first, far_second = down(far_hidden, down_own, down_other, f, (((),), ((),)))
-        for_left = shifted(far_first, "x", -1)
-        for_right = shifted(far_second, "x", 1)
-        to_left, to_right = down(
-            side_hidden,
-            down_own,
-            down_other,
-            f,
-            ((((0, None),), ()), ((), ((1, None),))),
-            (for_left, for_right),
-        )
+        to_left, to_right = down(side_hidden, down_own, down_other, f, (((), ()), ((), ())))
         got_right = shifted(to_left, "x", -1)
         got_left = shifted(to_right, "x", 1)
+        (to_far,) = down(far_hidden, down_own, down_other, f, (((), ()),))
+        got_far = shifted(to_far, "x", 2)
         (summed,) = down(
             own_hidden,
             down_own,
             down_other,
             f,
-            ((((0, 0), (1, 0)), ((0, 1), (1, 1))),),
-            (got_left, got_right),
+            (tuple(tuple((which, c) for which in range(3)) for c in range(ROW_CHUNKS)),),
+            (got_left, got_right, got_far),
             split=z_count,
         )
         backs.append(exchanged(summed).reshape(tok_rows * TOPK, -1))

time: 184 us -> 195 us (1.060)
  the two profiles are of different devices: /device:TPU:22 before, /device:TPU:8 now
where the time goes in v2:
time: 195 us; the launch traced here: 194 us
  waiting for transfers between devices  87.2 us (45%)
  starting transfers between devices  58.5 us (30%)
  Pallas kernels  27.2 us (14%)
  local copies, waits for them, and re-layouts  14.4 us (7%)
  other arithmetic  5.38 us (3%)
    ppermute x14, waiting for transfers between devices, shifted(): lax.ppermute(value, axis, [(i, (i + by) % peers) for i in range(peers)])  46.7 us
    all_to_all x4, waiting for transfers between devices, exchanged(): return lax.all_to_all(value, 'z', split_axis=0, concat_axis=0, tiled=True)  36.5 us
    all_to_all x4, starting transfers between devices, exchanged(): return lax.all_to_all(value, 'z', split_axis=0, concat_axis=0, tiled=True)  26.7 us
    ppermute x14, starting transfers between devices, shifted(): lax.ppermute(value, axis, [(i, (i + by) % peers) for i in range(peers)])  20.5 us
    pallas_call x6, Pallas kernels, down(): pl.pallas_call(functools.partial(down_kernel, len(hidden), chunk, added,...  10.4 us
    pallas_call x3, Pallas kernels, up(): pl.pallas_call(functools.partial(up_kernel, len(blocks)), out_shape=[jax....  9.8 us
    unnamed x39, local copies, waits for them, and re-layouts  8.74 us
    ppermute x2, starting transfers between devices, section_step(): lax.ppermute(delta, 'section', [(i, i + 1) for i in range(sections - 1)])  6.92 us
  transfers between devices with their start and end apart: 21, of which 11 were waited for; matrix products, arithmetic and copies ran while one was open for 5% of the time, Pallas kernels for 13%

profile of v2, /device:TPU:8, one launch (start us, length us, event | category | flops | bytes accessed | tf_op | source)
XLA Modules:
  0.0 193.7 jit_solution(9765082444570200924)
XLA Ops:
  0.7 1.1 copy-done.14
  1.7 0.7 copy-done.15
  2.4 1.4 group_rows.1
  3.8 8.5 %all-to-all-start = ((bf16[8,16,2048]{2,1,0:T(8,128)(2,1)}), bf16[8,16,2048]{2,1,0:T(8,128)(2,1)S(1)}, u32[]{:S(2)}, u32[]{:S(2)}) async-start(bf16[8,16,2048]{2,1,0:T(8,128)(2,1)} %bitcast.9), calls=%async_computation | async-start | bytes 1048576 | tf_op jit(solution)/shard_map/all_to_all | solution.py:29
  12.3 0.5 collective-permute-start.5
  12.8 17.0 %all-to-all-done = bf16[8,16,2048]{2,1,0:T(8,128)(2,1)S(1)} async-done(((bf16[8,16,2048]{2,1,0:T(8,128)(2,1)}), bf16[8,16,2048]{2,1,0:T(8,128)(2,1)S(1)}, u32[]{:S(2)}, u32[]{:S(2)}) %all-to-all-start) | async-done | bytes 524320 | tf_op jit(solution)/shard_map/all_to_all | solution.py:29
  29.8 4.1 %all-to-all-start.2 = ((bf16[8,16,2048]{2,1,0:T(8,128)(2,1)}), bf16[8,16,2048]{2,1,0:T(8,128)(2,1)}, u32[]{:S(2)}, u32[]{:S(2)}) async-start(bf16[8,16,2048]{2,1,0:T(8,128)(2,1)} %bitcast.17), calls=%async_computation.2 | async-start | bytes 1048576 | tf_op jit(solution)/shard_map/all_to_all | solution.py:29
  33.9 0.8 and_select_fusion.2
  34.7 0.1 select_reduce_fusion.1
  34.8 0.6 gather_fusion.1
  35.4 1.7 gather_fusion
  37.1 1.5 pad_maximum_fusion
  38.6 13.3 %all-to-all-done.2 = bf16[8,16,2048]{2,1,0:T(8,128)(2,1)} async-done(((bf16[8,16,2048]{2,1,0:T(8,128)(2,1)}), bf16[8,16,2048]{2,1,0:T(8,128)(2,1)}, u32[]{:S(2)}, u32[]{:S(2)}) %all-to-all-start.2) | async-done | bytes 524320 | tf_op jit(solution)/shard_map/all_to_all | solution.py:29
  51.9 4.4 %all-to-all-start.1 = ((bf16[16,2,16,2048]{3,2,1,0:T(8,128)(2,1)}), bf16[16,2,16,2048]{3,2,1,0:T(8,128)(2,1)}, u32[]{:S(2)}, u32[]{:S(2)}) async-start(bf16[16,2,16,2048]{3,2,1,0:T(8,128)(2,1)} %pad_maximum_fusion), calls=%async_computation.1 | async-start | bytes 4194304 | tf_op jit(solution)/shard_map/all_to_all | solution.py:299
  56.3 1.6 collective-permute-start
  57.9 1.8 collective-permute-start.4
  59.6 12.2 %collective-permute-done.refs_1_ = bf16[128,2048]{1,0:T(8,128)(2,1)S(1)} collective-permute-done((bf16[128,2048]{1,0:T(8,128)(2,1)}, bf16[128,2048]{1,0:T(8,128)(2,1)S(1)}, u32[]{:S(2)}, u32[]{:S(2)}) %collective-permute-start) | collective-permute-done | bytes 524320 | tf_op jit(solution)/shard_map/ppermute | solution.py:25
  71.8 0.3 collective-permute-start.8
  72.1 3.0 %collective-permute-start.9 = (bf16[128,2048]{1,0:T(8,128)(2,1)S(1)}, bf16[128,2048]{1,0:T(8,128)(2,1)S(1)}, u32[]{:S(2)}, u32[]{:S(2)}) collective-permute-start(bf16[128,2048]{1,0:T(8,128)(2,1)S(1)} %collective-permute-done.4.refs_2_), channel_id=1, source_target_pairs={{0,3},{1,0},{2,1},{3,2},{4,7},{5,4},{6,5},{7,6},{8,11},{9,8},{10,9... | collective-permute-start | bytes 1572872 | tf_op jit(solution)/shard_map/ppermute | solution.py:25
  75.0 3.2 %collective-permute-start.1 = (bf16[128,2048]{1,0:T(8,128)(2,1)}, bf16[128,2048]{1,0:T(8,128)(2,1)S(1)}, u32[]{:S(2)}, u32[]{:S(2)}) collective-permute-start(bf16[128,2048]{1,0:T(8,128)(2,1)} %bitcast.18.refs_0_), channel_id=1, source_target_pairs={{0,3},{1,0},{2,1},{3,2},{4,7},{5,4},{6,5},{7,6},{8,11},{9,8},{10,9... | collective-permute-start | bytes 1572872 | tf_op jit(solution)/shard_map/ppermute | solution.py:25
  78.3 2.0 %copy-done.6 = bf16[1,2048,896]{2,1,0:T(8,128)(2,1)S(1)} copy-done((bf16[1,2048,896]{2,1,0:T(8,128)(2,1)S(1)}, bf16[1,2048,896]{2,1,0:T(8,128)(2,1)}, u32[]{:S(2)}) %copy-start.6) | copy-done | bytes 3670040
  80.3 2.4 %shard_map.104 = (bf16[2048,896]{1,0:T(8,128)(2,1)S(1)}, bf16[2048,896]{1,0:T(8,128)(2,1)S(1)}) custom-call(bf16[2048,896]{1,0:T(8,128)(2,1)S(1)} %bitcast.43, bf16[2048,896]{1,0:T(8,128)(2,1)} %collective-permute-done.2.other_ref), custom_call_target="tpu_custom_call" | custom-call | flops 1000000 | bytes 14680064 | tf_op jit(solution)/shard_map/pallas_call | solution.py:89
  82.8 0.7 copy-done.7
  83.5 2.3 %shard_map.107 = (bf16[896,2048]{1,0:T(8,128)(2,1)S(1)}, bf16[896,2048]{1,0:T(8,128)(2,1)S(1)}) custom-call(bf16[896,2048]{1,0:T(8,128)(2,1)S(1)} %bitcast.45, bf16[896,2048]{1,0:T(8,128)(2,1)} %collective-permute-done.5.other_ref), custom_call_target="tpu_custom_call" | custom-call | flops 1000000 | bytes 14680064 | tf_op jit(solution)/shard_map/pallas_call | solution.py:89
  85.8 2.0 %collective-permute-done.8.refs_0_ = bf16[128,2048]{1,0:T(8,128)(2,1)S(1)} collective-permute-done((bf16[128,2048]{1,0:T(8,128)(2,1)S(1)}, bf16[128,2048]{1,0:T(8,128)(2,1)S(1)}, u32[]{:S(2)}, u32[]{:S(2)}) %collective-permute-start.8) | collective-permute-done | bytes 524320 | tf_op jit(solution)/shard_map/ppermute | solution.py:25
  87.8 2.1 %shard_map.109 = (bf16[128,1792]{1,0:T(8,128)(2,1)S(1)}, bf16[128,1792]{1,0:T(8,128)(2,1)S(1)}) custom-call(bf16[128,2048]{1,0:T(8,128)(2,1)S(1)} %collective-permute-done.8.refs_0_, bf16[128,2048]{1,0:T(8,128)(2,1)S(1)} %collective-permute-done.9.refs_1_, bf16[2048,896]{1,0:T(8,128)(2,1)S(1)} %get-tuple-element.30.refs_3_.refs_2_, ...), custom_call_target="tpu_custom_call" | custom-call | flops 1879048192 | bytes 8388608 | tf_op jit(solution)/shard_map/pallas_call | solution.py:127
  90.0 1.1 shard_map.114
  91.1 2.1 %collective-permute-start.14 = (bf16[2,128,1024]{2,1,0:T(8,128)(2,1)S(1)}, bf16[2,128,1024]{2,1,0:T(8,128)(2,1)S(1)}, u32[]{:S(2)}, u32[]{:S(2)}) collective-permute-start(bf16[2,128,1024]{2,1,0:T(8,128)(2,1)S(1)} %shard_map.114), channel_id=1, source_target_pairs={{0,2},{1,3},{2,0},{3,1},{4,6},{5,7},{6,4},{7,5},{8,10},{9,11},{10,... | collective-permute-start | bytes 1572872 | tf_op jit(solution)/shard_map/ppermute | solution.py:25
  93.1 15.6 %collective-permute-done.3.refs_1_ = bf16[128,2048]{1,0:T(8,128)(2,1)S(1)} collective-permute-done((bf16[128,2048]{1,0:T(8,128)(2,1)S(1)}, bf16[128,2048]{1,0:T(8,128)(2,1)S(1)}, u32[]{:S(2)}, u32[]{:S(2)}) %collective-permute-start.3) | collective-permute-done | bytes 524320 | tf_op jit(solution)/shard_map/ppermute | solution.py:25
  108.7 3.2 %shard_map.106 = (bf16[128,1792]{1,0:T(8,128)(2,1)S(1)}, bf16[128,1792]{1,0:T(8,128)(2,1)S(1)}, bf16[128,1792]{1,0:T(8,128)(2,1)S(1)}) custom-call(bf16[128,2048]{1,0:T(8,128)(2,1)S(1)} %bitcast.55, bf16[128,2048]{1,0:T(8,128)(2,1)S(1)} %collective-permute-done.3.refs_1_, bf16[128,2048]{1,0:T(8,128)(2,1)S(1)} %collective-permute-done.4.refs_2_, ...), custom_call_target="tpu_custom_call" | custom-call | flops 2818572288 | bytes 8912896 | tf_op jit(solution)/shard_map/pallas_call | solution.py:127
  112.0 4.4 %shard_map.105 = (bf16[128,1792]{1,0:T(8,128)(2,1)S(1)}, bf16[128,1792]{1,0:T(8,128)(2,1)S(1)}, bf16[128,1792]{1,0:T(8,128)(2,1)S(1)}) custom-call(bf16[128,2048]{1,0:T(8,128)(2,1)} %bitcast.18.refs_0_, bf16[128,2048]{1,0:T(8,128)(2,1)S(1)} %collective-permute-done.refs_1_, bf16[128,2048]{1,0:T(8,128)(2,1)S(1)} %collective-permute-done.1.refs_2_, ...), custom_call_target="tpu_custom_call" | custom-call | flops 2818572288 | bytes 8912896 | tf_op jit(solution)/shard_map/pallas_call | solution.py:127
  116.4 2.1 %shard_map.113 = (bf16[2,128,1024]{2,1,0:T(8,128)(2,1)S(1)}, bf16[2,128,1024]{2,1,0:T(8,128)(2,1)S(1)}) custom-call(bf16[128,1792]{1,0:T(8,128)(2,1)S(1)} %get-tuple-element.36.refs_0_, bf16[128,1792]{1,0:T(8,128)(2,1)S(1)} %get-tuple-element.37.refs_1_, bf16[128,1792]{1,0:T(8,128)(2,1)S(1)} %get-tuple-element.38.refs_2_, ...), custom_call_target="tpu_custom_call" | custom-call | flops 1879048192 | bytes 4718592 | tf_op jit(solution)/shard_map/pallas_call | solution.py:182
  118.5 0.1 collective-permute-start.12
  118.6 3.2 %collective-permute-start.13 = (bf16[2,128,1024]{2,1,0:T(8,128)(2,1)S(1)}, bf16[2,128,1024]{2,1,0:T(8,128)(2,1)S(1)}, u32[]{:S(2)}, u32[]{:S(2)}) collective-permute-start(bf16[2,128,1024]{2,1,0:T(8,128)(2,1)S(1)} %get-tuple-element.46), channel_id=1, source_target_pairs={{0,3},{1,0},{2,1},{3,2},{4,7},{5,4},{6,5},{7,6},{8,11},{9,8},{10,9... | collective-permute-start | bytes 1572872 | tf_op jit(solution)/shard_map/ppermute | solution.py:25
  121.8 7.2 %collective-permute-done.12.refs_4_ = bf16[2,128,1024]{2,1,0:T(8,128)(2,1)S(1)} collective-permute-done((bf16[2,128,1024]{2,1,0:T(8,128)(2,1)S(1)}, bf16[2,128,1024]{2,1,0:T(8,128)(2,1)S(1)}, u32[]{:S(2)}, u32[]{:S(2)}) %collective-permute-start.12) | collective-permute-done | bytes 524320 | tf_op jit(solution)/shard_map/ppermute | solution.py:25
  129.0 2.0 %shard_map.115 = bf16[8,2,16,1024]{3,2,1,0:T(8,128)(2,1)} custom-call(bf16[128,1792]{1,0:T(8,128)(2,1)S(1)} %get-tuple-element.32.refs_0_, bf16[128,1792]{1,0:T(8,128)(2,1)S(1)} %get-tuple-element.33.refs_1_, bf16[896,2048]{1,0:T(8,128)(2,1)S(1)} %get-tuple-element.34.refs_4_.refs_2_, bf16[896,2048]{1,0:T(8,128)(2,1)S(1)} %get-tuple-element.35.refs_5_.refs_3_, ...), custom_call_target="tpu_custom_call" | custom-call | flops 939524096 | bytes 4194304 | tf_op jit(solution)/shard_map/pallas_call | solution.py:182
  131.0 6.8 %all-to-all-start.4 = ((bf16[8,2,16,1024]{3,2,1,0:T(8,128)(2,1)}), bf16[8,2,16,1024]{3,2,1,0:T(8,128)(2,1)S(1)}, u32[]{:S(2)}, u32[]{:S(2)}) async-start(bf16[8,2,16,1024]{3,2,1,0:T(8,128)(2,1)} %shard_map.115), calls=%async_computation.4 | async-start | bytes 1048576 | tf_op jit(solution)/shard_map/all_to_all | solution.py:29
  137.9 0.1 broadcast_in_dim.45
  138.0 0.1 reshape.267
  138.1 0.1 copy.18
  138.2 0.1 copy.17
  138.3 2.0 %copy-done.2 = bf16[896,2048]{1,0:T(8,128)(2,1)S(1)} copy-done((bf16[896,2048]{1,0:T(8,128)(2,1)S(1)}, bf16[896,2048]{1,0:T(8,128)(2,1)}, u32[]{:S(2)}) %copy-start.2) | copy-done | bytes 3670040
  140.3 2.0 %copy-done.5 = bf16[896,2048]{1,0:T(8,128)(2,1)S(1)} copy-done((bf16[896,2048]{1,0:T(8,128)(2,1)S(1)}, bf16[896,2048]{1,0:T(8,128)(2,1)}, u32[]{:S(2)}) %copy-start.5) | copy-done | bytes 3670040
  142.4 1.1 shard_map.110
  143.5 1.5 collective-permute-start.10
  145.0 2.1 %shard_map.108 = (bf16[2,128,1024]{2,1,0:T(8,128)(2,1)S(1)}, bf16[2,128,1024]{2,1,0:T(8,128)(2,1)S(1)}) custom-call(bf16[128,1792]{1,0:T(8,128)(2,1)S(1)} %copy-done.11, bf16[128,1792]{1,0:T(8,128)(2,1)S(1)} %get-tuple-element.37.refs_1_, bf16[128,1792]{1,0:T(8,128)(2,1)S(1)} %copy-done.13, bf16[128,1792]{1,0:T(8,128)(2,1)S(1)} %copy-done.9, ...), custom_call_target="tpu_custom_call" | custom-call | flops 1879048192 | bytes 4718592 | tf_op jit(solution)/shard_map/pallas_call | solution.py:182
  147.1 2.7 %collective-permute-start.6 = (bf16[2,128,1024]{2,1,0:T(8,128)(2,1)S(1)}, bf16[2,128,1024]{2,1,0:T(8,128)(2,1)S(1)}, u32[]{:S(2)}, u32[]{:S(2)}) collective-permute-start(bf16[2,128,1024]{2,1,0:T(8,128)(2,1)S(1)} %get-tuple-element.40), channel_id=1, source_target_pairs={{0,1},{1,2},{2,3},{3,0},{4,5},{5,6},{6,7},{7,4},{8,9},{9,10},{10,1... | collective-permute-start | bytes 1572872 | tf_op jit(solution)/shard_map/ppermute | solution.py:25
  149.8 0.6 collective-permute-start.7
  150.4 0.2 select_reduce_fusion
  150.7 3.7 %collective-permute-done.10.refs_6_ = bf16[2,128,1024]{2,1,0:T(8,128)(2,1)S(1)} collective-permute-done((bf16[2,128,1024]{2,1,0:T(8,128)(2,1)S(1)}, bf16[2,128,1024]{2,1,0:T(8,128)(2,1)S(1)}, u32[]{:S(2)}, u32[]{:S(2)}) %collective-permute-start.10) | collective-permute-done | bytes 524320 | tf_op jit(solution)/shard_map/ppermute | solution.py:25
  154.4 5.5 %collective-permute-done.6.refs_4_ = bf16[2,128,1024]{2,1,0:T(8,128)(2,1)S(1)} collective-permute-done((bf16[2,128,1024]{2,1,0:T(8,128)(2,1)S(1)}, bf16[2,128,1024]{2,1,0:T(8,128)(2,1)S(1)}, u32[]{:S(2)}, u32[]{:S(2)}) %collective-permute-start.6) | collective-permute-done | bytes 524320 | tf_op jit(solution)/shard_map/ppermute | solution.py:25
  159.9 0.6 collective-permute-done.7.refs_5_
  160.5 2.0 %shard_map.111 = bf16[8,2,16,1024]{3,2,1,0:T(8,128)(2,1)} custom-call(bf16[128,1792]{1,0:T(8,128)(2,1)S(1)} %get-tuple-element.32.refs_0_, bf16[128,1792]{1,0:T(8,128)(2,1)S(1)} %get-tuple-element.33.refs_1_, bf16[896,2048]{1,0:T(8,128)(2,1)S(1)} %copy-done.3, bf16[896,2048]{1,0:T(8,128)(2,1)S(1)} %copy-done.5, ...), custom_call_target="tpu_custom_call" | custom-call | flops 939524096 | bytes 4194304 | tf_op jit(solution)/shard_map/pallas_call | solution.py:182
  162.5 7.2 %all-to-all-start.3 = ((bf16[8,2,16,1024]{3,2,1,0:T(8,128)(2,1)}), bf16[8,2,16,1024]{3,2,1,0:T(8,128)(2,1)S(1)}, u32[]{:S(2)}, u32[]{:S(2)}) async-start(bf16[8,2,16,1024]{3,2,1,0:T(8,128)(2,1)} %shard_map.111), calls=%async_computation.3 | async-start | bytes 1048576 | tf_op jit(solution)/shard_map/all_to_all | solution.py:29
  169.7 2.2 %gather_fusion.2 = bf16[8,2,16,2048]{3,2,1,0:T(8,128)(2,1)S(1)} fusion(bf16[16,2,16,2048]{3,2,1,0:T(8,128)(2,1)} %all-to-all-done.1, s32[1024]{0:T(1024)S(1)} %pad_clamp_fusion), kind=kCustom, calls=%fused_computation.2 | custom fusion | bytes 2097184 | tf_op jit(solution)/shard_map/gather | solution.py:300
  171.9 0.9 fusion.8
  172.9 0.5 shard_map.116
  173.3 3.5 %collective-permute-start.15 = (bf16[128,1024]{1,0:T(8,128)(2,1)S(1)}, bf16[128,1024]{1,0:T(8,128)(2,1)S(1)}, u32[]{:S(2)}, u32[]{:S(2)}) collective-permute-start(bf16[128,1024]{1,0:T(8,128)(2,1)S(1)} %get-tuple-element.47), channel_id=1, source_target_pairs={{0,64},{64,128},{128,192},{1,65},{65,129},{129,193},{2,66},{66,130... | collective-permute-start | bytes 786440 | tf_op jit(solution)/shard_map/ppermute | solution.py:315
  176.8 6.2 %all-to-all-done.3 = bf16[8,2,16,1024]{3,2,1,0:T(8,128)(2,1)S(1)} async-done(((bf16[8,2,16,1024]{3,2,1,0:T(8,128)(2,1)}), bf16[8,2,16,1024]{3,2,1,0:T(8,128)(2,1)S(1)}, u32[]{:S(2)}, u32[]{:S(2)}) %all-to-all-start.3) | async-done | bytes 524320 | tf_op jit(solution)/shard_map/all_to_all | solution.py:29
  183.0 0.5 shard_map.112
  183.5 3.5 %collective-permute-start.11 = (bf16[128,1024]{1,0:T(8,128)(2,1)S(1)}, bf16[128,1024]{1,0:T(8,128)(2,1)S(1)}, u32[]{:S(2)}, u32[]{:S(2)}) collective-permute-start(bf16[128,1024]{1,0:T(8,128)(2,1)S(1)} %get-tuple-element.44), channel_id=1, source_target_pairs={{0,64},{64,128},{128,192},{1,65},{65,129},{129,193},{2,66},{66,130... | collective-permute-start | bytes 786440 | tf_op jit(solution)/shard_map/ppermute | solution.py:315
  186.9 0.8 maximum_bitcast_fusion
  187.8 4.0 %collective-permute-done.11 = bf16[128,1024]{1,0:T(8,128)(2,1)S(1)} collective-permute-done((bf16[128,1024]{1,0:T(8,128)(2,1)S(1)}, bf16[128,1024]{1,0:T(8,128)(2,1)S(1)}, u32[]{:S(2)}, u32[]{:S(2)}) %collective-permute-start.11) | collective-permute-done | bytes 262176 | tf_op jit(solution)/shard_map/ppermute | solution.py:315
  191.7 2.0 %fusion = bf16[1,128,2048]{2,1,0:T(8,128)(2,1)} fusion(bf16[1,128,2048]{2,1,0:T(8,128)(2,1)} %bitcast.60, bf16[1,128,1024]{2,1,0:T(8,128)(2,1)S(1)} %bitcast.62, bf16[1,128,1024]{2,1,0:T(8,128)(2,1)S(1)} %bitcast.63), kind=kLoop, calls=%fused_computation.5 | loop fusion | flops 1835008 | bytes 1572864 | tf_op jit(solution)/shard_map/convert_element_type | solution.py:318
  (51 shorter events, 0.2 us)
Async XLA Ops:
  0.6 34.2 %copy-start = (bf16[1,128,2048]{2,1,0:T(8,128)(2,1)S(1)}, bf16[1,128,2048]{2,1,0:T(8,128)(2,1)}, u32[]{:S(2)}) copy-start(bf16[1,128,2048]{2,1,0:T(8,128)(2,1)} %param.10) | copy-start | bytes 1572868
  0.6 1.1 copy-start.14
  1.7 0.7 copy-start.15
  3.8 26.0 %all-to-all-start = ((bf16[8,16,2048]{2,1,0:T(8,128)(2,1)}), bf16[8,16,2048]{2,1,0:T(8,128)(2,1)S(1)}, u32[]{:S(2)}, u32[]{:S(2)}) async-start(bf16[8,16,2048]{2,1,0:T(8,128)(2,1)} %bitcast.9), calls=%async_computation | async-start | bytes 1048576 | tf_op jit(solution)/shard_map/all_to_all | solution.py:29
  12.3 62.8 %collective-permute-start.2 = (bf16[2048,896]{1,0:T(8,128)(2,1)}, bf16[2048,896]{1,0:T(8,128)(2,1)}, u32[]{:S(2)}, u32[]{:S(2)}) collective-permute-start(bf16[2048,896]{1,0:T(8,128)(2,1)} %bitcast.42), channel_id=1, source_target_pairs={{0,4},{4,0},{1,5},{5,1},{2,6},{6,2},{3,7},{7,3},{8,12},{12,8},{9,1... | collective-permute-start | bytes 11010056 | tf_op jit(solution)/shard_map/ppermute | solution.py:25
  12.3 70.5 %collective-permute-start.5 = (bf16[896,2048]{1,0:T(8,128)(2,1)}, bf16[896,2048]{1,0:T(8,128)(2,1)}, u32[]{:S(2)}, u32[]{:S(2)}) collective-permute-start(bf16[896,2048]{1,0:T(8,128)(2,1)} %bitcast.44), channel_id=1, source_target_pairs={{0,4},{4,0},{1,5},{5,1},{2,6},{6,2},{3,7},{7,3},{8,12},{12,8},{9,1... | collective-permute-start | bytes 11010056 | tf_op jit(solution)/shard_map/ppermute | solution.py:25
  29.8 22.1 %all-to-all-start.2 = ((bf16[8,16,2048]{2,1,0:T(8,128)(2,1)}), bf16[8,16,2048]{2,1,0:T(8,128)(2,1)}, u32[]{:S(2)}, u32[]{:S(2)}) async-start(bf16[8,16,2048]{2,1,0:T(8,128)(2,1)} %bitcast.17), calls=%async_computation.2 | async-start | bytes 1048576 | tf_op jit(solution)/shard_map/all_to_all | solution.py:29
  51.9 79.2 %all-to-all-start.1 = ((bf16[16,2,16,2048]{3,2,1,0:T(8,128)(2,1)}), bf16[16,2,16,2048]{3,2,1,0:T(8,128)(2,1)}, u32[]{:S(2)}, u32[]{:S(2)}) async-start(bf16[16,2,16,2048]{3,2,1,0:T(8,128)(2,1)} %pad_maximum_fusion), calls=%async_computation.1 | async-start | bytes 4194304 | tf_op jit(solution)/shard_map/all_to_all | solution.py:299
  56.3 15.5 %collective-permute-start = (bf16[128,2048]{1,0:T(8,128)(2,1)}, bf16[128,2048]{1,0:T(8,128)(2,1)S(1)}, u32[]{:S(2)}, u32[]{:S(2)}) collective-permute-start(bf16[128,2048]{1,0:T(8,128)(2,1)} %bitcast.18.refs_0_), channel_id=1, source_target_pairs={{0,1},{1,2},{2,3},{3,0},{4,5},{5,6},{6,7},{7,4},{8,9},{9,10},{10,1... | collective-permute-start | bytes 1572872 | tf_op jit(solution)/shard_map/ppermute | solution.py:25
  57.9 14.2 %collective-permute-start.4 = (bf16[128,2048]{1,0:T(8,128)(2,1)S(1)}, bf16[128,2048]{1,0:T(8,128)(2,1)S(1)}, u32[]{:S(2)}, u32[]{:S(2)}) collective-permute-start(bf16[128,2048]{1,0:T(8,128)(2,1)S(1)} %bitcast.53), channel_id=1, source_target_pairs={{0,3},{1,0},{2,1},{3,2},{4,7},{5,4},{6,5},{7,6},{8,11},{9,8},{10,9... | collective-permute-start | bytes 1572872 | tf_op jit(solution)/shard_map/ppermute | solution.py:25
  71.8 16.0 %collective-permute-start.8 = (bf16[128,2048]{1,0:T(8,128)(2,1)S(1)}, bf16[128,2048]{1,0:T(8,128)(2,1)S(1)}, u32[]{:S(2)}, u32[]{:S(2)}) collective-permute-start(bf16[128,2048]{1,0:T(8,128)(2,1)S(1)} %collective-permute-done.refs_1_), channel_id=1, source_target_pairs={{0,1},{1,2},{2,3},{3,0},{4,5},{5,6},{6,7},{7,4},{8,9},{9,10},{10,1... | collective-permute-start | bytes 1572872 | tf_op jit(solution)/shard_map/ppermute | solution.py:25
  72.1 15.7 %collective-permute-start.9 = (bf16[128,2048]{1,0:T(8,128)(2,1)S(1)}, bf16[128,2048]{1,0:T(8,128)(2,1)S(1)}, u32[]{:S(2)}, u32[]{:S(2)}) collective-permute-start(bf16[128,2048]{1,0:T(8,128)(2,1)S(1)} %collective-permute-done.4.refs_2_), channel_id=1, source_target_pairs={{0,3},{1,0},{2,1},{3,2},{4,7},{5,4},{6,5},{7,6},{8,11},{9,8},{10,9... | collective-permute-start | bytes 1572872 | tf_op jit(solution)/shard_map/ppermute | solution.py:25
  75.0 33.7 %collective-permute-start.3 = (bf16[128,2048]{1,0:T(8,128)(2,1)S(1)}, bf16[128,2048]{1,0:T(8,128)(2,1)S(1)}, u32[]{:S(2)}, u32[]{:S(2)}) collective-permute-start(bf16[128,2048]{1,0:T(8,128)(2,1)S(1)} %bitcast.54), channel_id=1, source_target_pairs={{0,1},{1,2},{2,3},{3,0},{4,5},{5,6},{6,7},{7,4},{8,9},{9,10},{10,1... | collective-permute-start | bytes 1572872 | tf_op jit(solution)/shard_map/ppermute | solution.py:25
  75.0 36.9 %collective-permute-start.1 = (bf16[128,2048]{1,0:T(8,128)(2,1)}, bf16[128,2048]{1,0:T(8,128)(2,1)S(1)}, u32[]{:S(2)}, u32[]{:S(2)}) collective-permute-start(bf16[128,2048]{1,0:T(8,128)(2,1)} %bitcast.18.refs_0_), channel_id=1, source_target_pairs={{0,3},{1,0},{2,1},{3,2},{4,7},{5,4},{6,5},{7,6},{8,11},{9,8},{10,9... | collective-permute-start | bytes 1572872 | tf_op jit(solution)/shard_map/ppermute | solution.py:25
  78.3 2.0 %copy-start.6 = (bf16[1,2048,896]{2,1,0:T(8,128)(2,1)S(1)}, bf16[1,2048,896]{2,1,0:T(8,128)(2,1)}, u32[]{:S(2)}) copy-start(bf16[1,2048,896]{2,1,0:T(8,128)(2,1)} %param.12) | copy-start | bytes 11010052
  80.3 3.1 %copy-start.7 = (bf16[1,896,2048]{2,1,0:T(8,128)(2,1)S(1)}, bf16[1,896,2048]{2,1,0:T(8,128)(2,1)}, u32[]{:S(2)}) copy-start(bf16[1,896,2048]{2,1,0:T(8,128)(2,1)} %param.13) | copy-start | bytes 11010052
  85.8 43.2 %copy-start.1 = (bf16[896,2048]{1,0:T(8,128)(2,1)}, bf16[896,2048]{1,0:T(8,128)(2,1)S(1)}, u32[]{:S(2)}) copy-start(bf16[896,2048]{1,0:T(8,128)(2,1)S(1)} %get-tuple-element.34.refs_4_.refs_2_) | copy-start | bytes 11010052
  85.8 43.2 %copy-start.4 = (bf16[896,2048]{1,0:T(8,128)(2,1)}, bf16[896,2048]{1,0:T(8,128)(2,1)S(1)}, u32[]{:S(2)}) copy-start(bf16[896,2048]{1,0:T(8,128)(2,1)S(1)} %get-tuple-element.35.refs_5_.refs_3_) | copy-start | bytes 11010052
  91.1 30.8 %collective-permute-start.14 = (bf16[2,128,1024]{2,1,0:T(8,128)(2,1)S(1)}, bf16[2,128,1024]{2,1,0:T(8,128)(2,1)S(1)}, u32[]{:S(2)}, u32[]{:S(2)}) collective-permute-start(bf16[2,128,1024]{2,1,0:T(8,128)(2,1)S(1)} %shard_map.114), channel_id=1, source_target_pairs={{0,2},{1,3},{2,0},{3,1},{4,6},{5,7},{6,4},{7,5},{8,10},{9,11},{10,... | collective-permute-start | bytes 1572872 | tf_op jit(solution)/shard_map/ppermute | solution.py:25
  111.9 4.5 %copy-start.8 = (bf16[128,1792]{1,0:T(8,128)(2,1)}, bf16[128,1792]{1,0:T(8,128)(2,1)S(1)}, u32[]{:S(2)}) copy-start(bf16[128,1792]{1,0:T(8,128)(2,1)S(1)} %get-tuple-element.39.refs_3_) | copy-start | bytes 1376260
  116.4 2.1 %copy-start.10 = (bf16[128,1792]{1,0:T(8,128)(2,1)}, bf16[128,1792]{1,0:T(8,128)(2,1)S(1)}, u32[]{:S(2)}) copy-start(bf16[128,1792]{1,0:T(8,128)(2,1)S(1)} %get-tuple-element.36.refs_0_) | copy-start | bytes 1376260
  116.4 2.1 %copy-start.12 = (bf16[128,1792]{1,0:T(8,128)(2,1)}, bf16[128,1792]{1,0:T(8,128)(2,1)S(1)}, u32[]{:S(2)}) copy-start(bf16[128,1792]{1,0:T(8,128)(2,1)S(1)} %get-tuple-element.38.refs_2_) | copy-start | bytes 1376260
  118.5 10.5 %collective-permute-start.12 = (bf16[2,128,1024]{2,1,0:T(8,128)(2,1)S(1)}, bf16[2,128,1024]{2,1,0:T(8,128)(2,1)S(1)}, u32[]{:S(2)}, u32[]{:S(2)}) collective-permute-start(bf16[2,128,1024]{2,1,0:T(8,128)(2,1)S(1)} %get-tuple-element.45), channel_id=1, source_target_pairs={{0,1},{1,2},{2,3},{3,0},{4,5},{5,6},{6,7},{7,4},{8,9},{9,10},{10,1... | collective-permute-start | bytes 1572872 | tf_op jit(solution)/shard_map/ppermute | solution.py:25
  118.6 10.4 %collective-permute-start.13 = (bf16[2,128,1024]{2,1,0:T(8,128)(2,1)S(1)}, bf16[2,128,1024]{2,1,0:T(8,128)(2,1)S(1)}, u32[]{:S(2)}, u32[]{:S(2)}) collective-permute-start(bf16[2,128,1024]{2,1,0:T(8,128)(2,1)S(1)} %get-tuple-element.46), channel_id=1, source_target_pairs={{0,3},{1,0},{2,1},{3,2},{4,7},{5,4},{6,5},{7,6},{8,11},{9,8},{10,9... | collective-permute-start | bytes 1572872 | tf_op jit(solution)/shard_map/ppermute | solution.py:25
  129.0 8.9 %copy-start.18 = (s32[8]{0:T(128)S(1)}, s32[8]{0:T(128)}, u32[]{:S(2)}) copy-start(s32[8]{0:T(128)} %param.16) | copy-start | bytes 100
  129.0 9.0 %copy-start.17 = (s32[1,128,2]{1,2,0:T(2,128)S(1)}, s32[1,128,2]{1,2,0:T(2,128)}, u32[]{:S(2)}) copy-start(s32[1,128,2]{1,2,0:T(2,128)} %param.15) | copy-start | bytes 3076
  131.0 31.5 %all-to-all-start.4 = ((bf16[8,2,16,1024]{3,2,1,0:T(8,128)(2,1)}), bf16[8,2,16,1024]{3,2,1,0:T(8,128)(2,1)S(1)}, u32[]{:S(2)}, u32[]{:S(2)}) async-start(bf16[8,2,16,1024]{3,2,1,0:T(8,128)(2,1)} %shard_map.115), calls=%async_computation.4 | async-start | bytes 1048576 | tf_op jit(solution)/shard_map/all_to_all | solution.py:29
  138.3 2.0 %copy-start.2 = (bf16[896,2048]{1,0:T(8,128)(2,1)S(1)}, bf16[896,2048]{1,0:T(8,128)(2,1)}, u32[]{:S(2)}) copy-start(bf16[896,2048]{1,0:T(8,128)(2,1)} %copy-done.1) | copy-start | bytes 11010052
  140.3 2.0 %copy-start.5 = (bf16[896,2048]{1,0:T(8,128)(2,1)S(1)}, bf16[896,2048]{1,0:T(8,128)(2,1)}, u32[]{:S(2)}) copy-start(bf16[896,2048]{1,0:T(8,128)(2,1)} %copy-done.4) | copy-start | bytes 11010052
  142.4 2.7 %copy-start.3 = (bf16[896,2048]{1,0:T(8,128)(2,1)S(1)}, bf16[896,2048]{1,0:T(8,128)(2,1)}, u32[]{:S(2)}) copy-start(bf16[896,2048]{1,0:T(8,128)(2,1)} %copy-done.1) | copy-start | bytes 11010052
  142.4 2.7 %copy-start.9 = (bf16[128,1792]{1,0:T(8,128)(2,1)S(1)}, bf16[128,1792]{1,0:T(8,128)(2,1)}, u32[]{:S(2)}) copy-start(bf16[128,1792]{1,0:T(8,128)(2,1)} %copy-done.8) | copy-start | bytes 1376260
  142.4 2.7 %copy-start.11 = (bf16[128,1792]{1,0:T(8,128)(2,1)S(1)}, bf16[128,1792]{1,0:T(8,128)(2,1)}, u32[]{:S(2)}) copy-start(bf16[128,1792]{1,0:T(8,128)(2,1)} %copy-done.10) | copy-start | bytes 1376260
  142.4 2.7 %copy-start.13 = (bf16[128,1792]{1,0:T(8,128)(2,1)S(1)}, bf16[128,1792]{1,0:T(8,128)(2,1)}, u32[]{:S(2)}) copy-start(bf16[128,1792]{1,0:T(8,128)(2,1)} %copy-done.12) | copy-start | bytes 1376260
  143.5 6.9 %copy-start.16 = (s32[512]{0:T(512)S(1)}, s32[512]{0:T(512)}, u32[]{:S(2)}) copy-start(s32[512]{0:T(512)} %param.17) | copy-start | bytes 6148
  143.5 10.9 %collective-permute-start.10 = (bf16[2,128,1024]{2,1,0:T(8,128)(2,1)S(1)}, bf16[2,128,1024]{2,1,0:T(8,128)(2,1)S(1)}, u32[]{:S(2)}, u32[]{:S(2)}) collective-permute-start(bf16[2,128,1024]{2,1,0:T(8,128)(2,1)S(1)} %shard_map.110), channel_id=1, source_target_pairs={{0,2},{1,3},{2,0},{3,1},{4,6},{5,7},{6,4},{7,5},{8,10},{9,11},{10,... | collective-permute-start | bytes 1572872 | tf_op jit(solution)/shard_map/ppermute | solution.py:25
  147.1 12.8 %collective-permute-start.6 = (bf16[2,128,1024]{2,1,0:T(8,128)(2,1)S(1)}, bf16[2,128,1024]{2,1,0:T(8,128)(2,1)S(1)}, u32[]{:S(2)}, u32[]{:S(2)}) collective-permute-start(bf16[2,128,1024]{2,1,0:T(8,128)(2,1)S(1)} %get-tuple-element.40), channel_id=1, source_target_pairs={{0,1},{1,2},{2,3},{3,0},{4,5},{5,6},{6,7},{7,4},{8,9},{9,10},{10,1... | collective-permute-start | bytes 1572872 | tf_op jit(solution)/shard_map/ppermute | solution.py:25
  149.8 10.7 %collective-permute-start.7 = (bf16[2,128,1024]{2,1,0:T(8,128)(2,1)S(1)}, bf16[2,128,1024]{2,1,0:T(8,128)(2,1)S(1)}, u32[]{:S(2)}, u32[]{:S(2)}) collective-permute-start(bf16[2,128,1024]{2,1,0:T(8,128)(2,1)S(1)} %get-tuple-element.41), channel_id=1, source_target_pairs={{0,3},{1,0},{2,1},{3,2},{4,7},{5,4},{6,5},{7,6},{8,11},{9,8},{10,9... | collective-permute-start | bytes 1572872 | tf_op jit(solution)/shard_map/ppermute | solution.py:25
  162.5 20.5 %all-to-all-start.3 = ((bf16[8,2,16,1024]{3,2,1,0:T(8,128)(2,1)}), bf16[8,2,16,1024]{3,2,1,0:T(8,128)(2,1)S(1)}, u32[]{:S(2)}, u32[]{:S(2)}) async-start(bf16[8,2,16,1024]{3,2,1,0:T(8,128)(2,1)} %shard_map.111), calls=%async_computation.3 | async-start | bytes 1048576 | tf_op jit(solution)/shard_map/all_to_all | solution.py:29
  173.3 14.4 %collective-permute-start.15 = (bf16[128,1024]{1,0:T(8,128)(2,1)S(1)}, bf16[128,1024]{1,0:T(8,128)(2,1)S(1)}, u32[]{:S(2)}, u32[]{:S(2)}) collective-permute-start(bf16[128,1024]{1,0:T(8,128)(2,1)S(1)} %get-tuple-element.47), channel_id=1, source_target_pairs={{0,64},{64,128},{128,192},{1,65},{65,129},{129,193},{2,66},{66,130... | collective-permute-start | bytes 786440 | tf_op jit(solution)/shard_map/ppermute | solution.py:315
  183.5 8.3 %collective-permute-start.11 = (bf16[128,1024]{1,0:T(8,128)(2,1)S(1)}, bf16[128,1024]{1,0:T(8,128)(2,1)S(1)}, u32[]{:S(2)}, u32[]{:S(2)}) collective-permute-start(bf16[128,1024]{1,0:T(8,128)(2,1)S(1)} %get-tuple-element.44), channel_id=1, source_target_pairs={{0,64},{64,128},{128,192},{1,65},{65,129},{129,193},{2,66},{66,130... | collective-permute-start | bytes 786440 | tf_op jit(solution)/shard_map/ppermute | solution.py:315

commit v3 on v2

--- a/solution.py
+++ b/solution.py
@@ -74,29 +74,24 @@
     return out[:-1], out[-1]
 
 
-def stage_kernel(own_ref, other_ref, own_out_ref, other_out_ref, sems):
-    copies = [
-        pltpu.make_async_copy(own_ref, own_out_ref, sems.at[0]),
-        pltpu.make_async_copy(other_ref, other_out_ref, sems.at[1]),
-    ]
-    for copy in copies:
-        copy.start()
-    for copy in copies:
-        copy.wait()
-
-
-def stage(own, other):
+def stage_kernel(slice_ref, out_ref, sem):
+    copy = pltpu.make_async_copy(slice_ref, out_ref, sem)
+    copy.start()
+    copy.wait()
+
+
+def stage(value):
     return pl.pallas_call(
         stage_kernel,
-        in_specs=[pl.BlockSpec(memory_space=pl.ANY)] * 2,
-        out_specs=[pl.BlockSpec(memory_space=pltpu.VMEM)] * 2,
-        out_shape=[jax.ShapeDtypeStruct(own.shape, BF16)] * 2,
-        scratch_shapes=[pltpu.SemaphoreType.DMA((2,))],
-        compiler_params=pltpu.CompilerParams(vmem_limit_bytes=LARGE_VMEM),
-        cost_estimate=pl.CostEstimate(
-            flops=1000000, bytes_accessed=8 * own.size, transcendentals=0
-        ),
-    )(own, other)
+        in_specs=[pl.BlockSpec(memory_space=pltpu.HBM)],
+        out_specs=pl.BlockSpec(memory_space=pltpu.VMEM),
+        out_shape=jax.ShapeDtypeStruct(value.shape, BF16),
+        scratch_shapes=[pltpu.SemaphoreType.DMA],
+        compiler_params=pltpu.CompilerParams(vmem_limit_bytes=LARGE_VMEM),
+        cost_estimate=pl.CostEstimate(
+            flops=1000000, bytes_accessed=4 * value.size, transcendentals=0
+        ),
+    )(value)
 
 
 def beside(first_ref, second_ref, start, stop):
@@ -136,7 +131,7 @@
     )(*blocks, own, other)
 
 
-def down_kernel(count, chunk, added, split, *refs):
+def down_kernel(count, chunk, added, *refs):
     hidden_refs, own_ref, other_ref = refs[:count], refs[count], refs[count + 1]
     extra_refs = refs[count + 2 : len(refs) - len(added)]
     out_refs = refs[len(refs) - len(added) :]
@@ -156,31 +151,81 @@
                     extra = extra_refs[which]
                     value += (extra[:, here] if lead is None else extra[lead, :, here]).astype(F32)
                 value = value.astype(BF16)
-                if split:
-                    out_ref[:, number, :, here] = value.reshape(split, rows // split, TILE)
-                elif len(parts) == 1:
+                if len(parts) == 1:
                     out_ref[:, here] = value
                 else:
                     out_ref[number, :, here] = value
                 at += rows
 
 
-def down(hidden, own, other, chunk, added, extras=(), split=0):
+def down_all_kernel(first_ref, second_ref, own_ref, other_ref, *out_refs):
+    hidden = jnp.concatenate([first_ref[...], second_ref[...]], axis=0)
+    rows = first_ref.shape[0]
+    width = out_refs[0].shape[-1]
+    for start in range(0, own_ref.shape[1], TILE):
+        out_ref, at = out_refs[start // width], start % width
+        there = slice(start, start + TILE)
+        weights = jnp.concatenate([own_ref[:, there], other_ref[:, there]], axis=0)
+        term = jnp.dot(hidden, weights, preferred_element_type=F32)
+        out_ref[0, :, at : at + TILE] = term[:rows]
+        out_ref[1, :, at : at + TILE] = term[rows:]
+
+
+def down_all(hidden, own, other):
+    rows = hidden[0].shape[0]
+    units, width = own.shape
+    out = jax.ShapeDtypeStruct((len(hidden), rows, width // FEATURE_CHUNKS), F32)
+    return pl.pallas_call(
+        down_all_kernel,
+        out_shape=[out] * FEATURE_CHUNKS,
+        compiler_params=pltpu.CompilerParams(vmem_limit_bytes=LARGE_VMEM),
+        cost_estimate=pl.CostEstimate(
+            flops=8 * rows * width * units,
+            bytes_accessed=4 * width * units + 8 * rows * width,
+            transcendentals=0,
+        ),
+        name="down_own",
+    )(*hidden, own, other)
+
+
+def total_kernel(own_ref, *refs):
+    out_ref = refs[-1]
+    groups, parts, rows, _ = out_ref.shape
+    for start in range(0, out_ref.shape[-1], TILE):
+        here = slice(start, start + TILE)
+        for number in range(parts):
+            value = own_ref[number, :, here]
+            for ref in refs[:-1]:
+                value += ref[number, :, here].astype(F32)
+            out_ref[:, number, :, here] = value.astype(BF16).reshape(groups, rows, TILE)
+
+
+def total(own, others, groups):
+    parts, rows, width = own.shape
+    return pl.pallas_call(
+        total_kernel,
+        out_shape=jax.ShapeDtypeStruct((groups, parts, rows // groups, width), BF16),
+        compiler_params=pltpu.CompilerParams(vmem_limit_bytes=LARGE_VMEM),
+        cost_estimate=pl.CostEstimate(
+            flops=4 * own.size, bytes_accessed=12 * own.size, transcendentals=0
+        ),
+    )(own, *others)
+
+
+def down(hidden, own, other, chunk, added, extras=()):
     rows, units = hidden[0].shape
     units //= 2
     width = own.shape[1] // FEATURE_CHUNKS
     out_shape = []
     for parts in added:
-        if split:
-            lead = (split, len(parts), rows // split)
-        elif len(parts) == 1:
+        if len(parts) == 1:
             lead = (rows,)
         else:
             lead = (len(parts), rows)
         out_shape.append(jax.ShapeDtypeStruct(lead + (width,), BF16))
     total = rows * len(hidden)
     return pl.pallas_call(
-        functools.partial(down_kernel, len(hidden), chunk, added, split),
+        functools.partial(down_kernel, len(hidden), chunk, added),
         out_shape=out_shape,
         compiler_params=pltpu.CompilerParams(vmem_limit_bytes=LARGE_VMEM),
         cost_estimate=pl.CostEstimate(
@@ -241,8 +286,7 @@
     blocks = [exchanged(chunk.reshape(z_count, -1, width)).reshape(-1, width) for chunk in chunks]
     up_other = shifted(up_own, "core", 1)
     down_other = shifted(down_own, "core", 1)
-    up_own, up_other = stage(up_own, up_other)
-    down_own, down_other = stage(down_own, down_other)
+    up_other, down_other = stage(up_other), stage(down_other)
     from_left = [shifted(block, "x", 1) for block in blocks]
     from_right = [shifted(block, "x", -1) for block in blocks]
     far = [shifted(from_left[0], "x", 1), shifted(from_right[1], "x", -1)]
@@ -254,23 +298,30 @@
     own_hidden = [hidden[0] for hidden in near_hidden]
     side_hidden = [hidden[1] for hidden in near_hidden] + [hidden[2] for hidden in near_hidden]
 
-    backs = []
-    for f in range(FEATURE_CHUNKS):
-        to_left, to_right = down(side_hidden, down_own, down_other, f, (((), ()), ((), ())))
-        got_right = shifted(to_left, "x", -1)
-        got_left = shifted(to_right, "x", 1)
-        (to_far,) = down(far_hidden, down_own, down_other, f, (((), ()),))
-        got_far = shifted(to_far, "x", 2)
-        (summed,) = down(
-            own_hidden,
-            down_own,
-            down_other,
-            f,
-            (tuple(tuple((which, c) for which in range(3)) for c in range(ROW_CHUNKS)),),
-            (got_left, got_right, got_far),
-            split=z_count,
-        )
-        backs.append(exchanged(summed).reshape(tok_rows * TOPK, -1))
+    own_terms = down_all(own_hidden, down_own, down_other)
+    apart = ((), ())
+    to_left, to_right = down(side_hidden, down_own, down_other, 0, (apart, apart))
+    got_right = shifted(to_left, "x", -1)
+    got_left = shifted(to_right, "x", 1)
+    (to_far,) = down(far_hidden, down_own, down_other, 0, (apart,))
+    got_far = shifted(to_far, "x", 2)
+    first_back = total(own_terms[0], (got_left, got_right, got_far), z_count)
+
+    far_first, far_second = down(far_hidden, down_own, down_other, 1, (((),), ((),)))
+    for_left = shifted(far_first, "x", -1)
+    for_right = shifted(far_second, "x", 1)
+    to_left, to_right = down(
+        side_hidden,
+        down_own,
+        down_other,
+        1,
+        ((((0, None),), ()), ((), ((1, None),))),
+        (for_left, for_right),
+    )
+    got_right = shifted(to_left, "x", -1)
+    got_left = shifted(to_right, "x", 1)
+    second_back = total(own_terms[1], (got_left, got_right), z_count)
+    backs = [exchanged(summed).reshape(tok_rows * TOPK, -1) for summed in (first_back, second_back)]
 
     own_map = lax.dynamic_slice_in_dim(sample_map, own_device * SAMP_DEV, SAMP_DEV)
     dest_dp = own_map // SAMP_DEV // x_count

time: 195 us -> 179 us (0.918)
  the two profiles are of different devices: /device:TPU:8 before, /device:TPU:22 now
where the time goes in v3:
time: 179 us; the launch traced here: 178 us
  waiting for transfers between devices  78.4 us (44%)
  starting transfers between devices  52.5 us (29%)
  Pallas kernels  26.2 us (15%)
  local copies, waits for them, and re-layouts  14.8 us (8%)
  other arithmetic  5.57 us (3%)
    ppermute x15, waiting for transfers between devices, shifted(): lax.ppermute(value, axis, [(i, (i + by) % peers) for i in range(peers)])  40.2 us
    all_to_all x4, waiting for transfers between devices, exchanged(): return lax.all_to_all(value, 'z', split_axis=0, concat_axis=0, tiled=True)  34 us
    all_to_all x4, starting transfers between devices, exchanged(): return lax.all_to_all(value, 'z', split_axis=0, concat_axis=0, tiled=True)  26.1 us
    ppermute x15, starting transfers between devices, shifted(): lax.ppermute(value, axis, [(i, (i + by) % peers) for i in range(peers)])  15.5 us
    pallas_call x3, Pallas kernels, up(): pl.pallas_call(functools.partial(up_kernel, len(blocks)), out_shape=[jax....  8.6 us
    pallas_call x4, Pallas kernels, down(): pl.pallas_call(functools.partial(down_kernel, len(hidden), chunk, added),...  7.11 us
    unnamed x31, local copies, waits for them, and re-layouts  7.09 us
    ppermute x2, starting transfers between devices, section_step(): lax.ppermute(delta, 'section', [(i, i + 1) for i in range(sections - 1)])  6.38 us
  transfers between devices with their start and end apart: 22, of which 11 were waited for; matrix products, arithmetic and copies ran while one was open for 7% of the time, Pallas kernels for 14%

profile of v3, /device:TPU:22, one launch (start us, length us, event | category | flops | bytes accessed | tf_op | source)
XLA Modules:
  0.0 178.4 jit_solution(11936617863004737289)
XLA Ops:
  0.7 1.1 copy-done.8
  1.7 0.7 copy-done.9
  2.4 1.4 group_rows.1
  3.8 8.5 %all-to-all-start = ((bf16[8,16,2048]{2,1,0:T(8,128)(2,1)}), bf16[8,16,2048]{2,1,0:T(8,128)(2,1)S(1)}, u32[]{:S(2)}, u32[]{:S(2)}) async-start(bf16[8,16,2048]{2,1,0:T(8,128)(2,1)} %bitcast.9), calls=%async_computation | async-start | bytes 1048576 | tf_op jit(solution)/shard_map/all_to_all | solution.py:29
  12.3 0.5 collective-permute-start.5
  12.8 17.0 %all-to-all-done = bf16[8,16,2048]{2,1,0:T(8,128)(2,1)S(1)} async-done(((bf16[8,16,2048]{2,1,0:T(8,128)(2,1)}), bf16[8,16,2048]{2,1,0:T(8,128)(2,1)S(1)}, u32[]{:S(2)}, u32[]{:S(2)}) %all-to-all-start) | async-done | bytes 524320 | tf_op jit(solution)/shard_map/all_to_all | solution.py:29
  29.8 3.5 %all-to-all-start.2 = ((bf16[8,16,2048]{2,1,0:T(8,128)(2,1)}), bf16[8,16,2048]{2,1,0:T(8,128)(2,1)S(1)}, u32[]{:S(2)}, u32[]{:S(2)}) async-start(bf16[8,16,2048]{2,1,0:T(8,128)(2,1)} %bitcast.17), calls=%async_computation.2 | async-start | bytes 1048576 | tf_op jit(solution)/shard_map/all_to_all | solution.py:29
  33.3 0.8 and_select_fusion.2
  34.1 0.1 select_reduce_fusion.1
  34.2 0.6 gather_fusion.1
  34.8 1.7 gather_fusion
  36.5 2.7 %pad_maximum_fusion = bf16[16,2,16,2048]{3,2,1,0:T(8,128)(2,1)} fusion(bf16[16,1,16,2048]{3,2,1,0:T(8,128)(2,1)S(1)} %bitcast.66, bf16[16,1,16,2048]{3,2,1,0:T(8,128)(2,1)} %bitcast.67), kind=kLoop, calls=%fused_computation.3 | loop fusion | flops 1048576 | bytes 4194304 | tf_op jit(solution)/shard_map/concatenate | solution.py:342
  39.2 12.0 %all-to-all-done.2 = bf16[8,16,2048]{2,1,0:T(8,128)(2,1)S(1)} async-done(((bf16[8,16,2048]{2,1,0:T(8,128)(2,1)}), bf16[8,16,2048]{2,1,0:T(8,128)(2,1)S(1)}, u32[]{:S(2)}, u32[]{:S(2)}) %all-to-all-start.2) | async-done | bytes 524320 | tf_op jit(solution)/shard_map/all_to_all | solution.py:29
  51.2 4.4 %all-to-all-start.1 = ((bf16[16,2,16,2048]{3,2,1,0:T(8,128)(2,1)}), bf16[16,2,16,2048]{3,2,1,0:T(8,128)(2,1)}, u32[]{:S(2)}, u32[]{:S(2)}) async-start(bf16[16,2,16,2048]{3,2,1,0:T(8,128)(2,1)} %pad_maximum_fusion), calls=%async_computation.1 | async-start | bytes 4194304 | tf_op jit(solution)/shard_map/all_to_all | solution.py:350
  55.6 0.5 collective-permute-start
  56.2 1.6 collective-permute-start.4
  57.7 1.7 collective-permute-start.3
  59.4 11.1 %collective-permute-done.refs_1_ = bf16[128,2048]{1,0:T(8,128)(2,1)S(1)} collective-permute-done((bf16[128,2048]{1,0:T(8,128)(2,1)S(1)}, bf16[128,2048]{1,0:T(8,128)(2,1)S(1)}, u32[]{:S(2)}, u32[]{:S(2)}) %collective-permute-start) | collective-permute-done | bytes 524320 | tf_op jit(solution)/shard_map/ppermute | solution.py:25
  70.5 0.8 collective-permute-start.1
  71.3 2.4 %collective-permute-start.8 = (bf16[128,2048]{1,0:T(8,128)(2,1)S(1)}, bf16[128,2048]{1,0:T(8,128)(2,1)S(1)}, u32[]{:S(2)}, u32[]{:S(2)}) collective-permute-start(bf16[128,2048]{1,0:T(8,128)(2,1)S(1)} %collective-permute-done.refs_1_), channel_id=1, source_target_pairs={{0,1},{1,2},{2,3},{3,0},{4,5},{5,6},{6,7},{7,4},{8,9},{9,10},{10,1... | collective-permute-start | bytes 1572872 | tf_op jit(solution)/shard_map/ppermute | solution.py:25
  73.7 2.0 %shard_map.104.refs_4_.refs_3_ = bf16[2048,896]{1,0:T(8,128)(2,1)S(1)} custom-call(bf16[2048,896]{1,0:T(8,128)(2,1)} %collective-permute-done.2.slice_ref), custom_call_target="tpu_custom_call" | custom-call | flops 1000000 | bytes 7340032 | tf_op jit(solution)/shard_map/pallas_call | solution.py:84
  75.8 5.9 %collective-permute-done.3.refs_1_ = bf16[128,2048]{1,0:T(8,128)(2,1)S(1)} collective-permute-done((bf16[128,2048]{1,0:T(8,128)(2,1)S(1)}, bf16[128,2048]{1,0:T(8,128)(2,1)S(1)}, u32[]{:S(2)}, u32[]{:S(2)}) %collective-permute-start.3) | collective-permute-done | bytes 524320 | tf_op jit(solution)/shard_map/ppermute | solution.py:25
  81.7 3.2 %shard_map.106 = (bf16[128,1792]{1,0:T(8,128)(2,1)S(1)}, bf16[128,1792]{1,0:T(8,128)(2,1)S(1)}, bf16[128,1792]{1,0:T(8,128)(2,1)S(1)}) custom-call(bf16[128,2048]{1,0:T(8,128)(2,1)S(1)} %bitcast.61, bf16[128,2048]{1,0:T(8,128)(2,1)S(1)} %collective-permute-done.3.refs_1_, bf16[128,2048]{1,0:T(8,128)(2,1)S(1)} %collective-permute-done.4.refs_2_, ...), custom_call_target="tpu_custom_call" | custom-call | flops 2818572288 | bytes 8912896 | tf_op jit(solution)/shard_map/pallas_call | solution.py:122
  85.0 2.0 %shard_map.107.other_ref.refs_5_.refs_3_ = bf16[896,2048]{1,0:T(8,128)(2,1)S(1)} custom-call(bf16[896,2048]{1,0:T(8,128)(2,1)} %collective-permute-done.5.slice_ref), custom_call_target="tpu_custom_call" | custom-call | flops 1000000 | bytes 7340032 | tf_op jit(solution)/shard_map/pallas_call | solution.py:84
  87.0 3.2 %shard_map.105 = (bf16[128,1792]{1,0:T(8,128)(2,1)S(1)}, bf16[128,1792]{1,0:T(8,128)(2,1)S(1)}, bf16[128,1792]{1,0:T(8,128)(2,1)S(1)}) custom-call(bf16[128,2048]{1,0:T(8,128)(2,1)S(1)} %bitcast.64, bf16[128,2048]{1,0:T(8,128)(2,1)S(1)} %collective-permute-done.refs_1_, bf16[128,2048]{1,0:T(8,128)(2,1)S(1)} %collective-permute-done.1.refs_2_, ...), custom_call_target="tpu_custom_call" | custom-call | flops 2818572288 | bytes 8912896 | tf_op jit(solution)/shard_map/pallas_call | solution.py:122
  90.3 0.1 copy-done.3
  90.4 2.1 %shard_map.108 = (bf16[2,128,1024]{2,1,0:T(8,128)(2,1)S(1)}, bf16[2,128,1024]{2,1,0:T(8,128)(2,1)S(1)}) custom-call(bf16[128,1792]{1,0:T(8,128)(2,1)S(1)} %get-tuple-element.33.refs_0_, bf16[128,1792]{1,0:T(8,128)(2,1)S(1)} %get-tuple-element.34.refs_1_, bf16[128,1792]{1,0:T(8,128)(2,1)S(1)} %get-tuple-element.35.refs_2_, ...), custom_call_target="tpu_custom_call" | custom-call | flops 1879048192 | bytes 4718592 | tf_op jit(solution)/shard_map/pallas_call | solution.py:227
  92.5 1.8 collective-permute-start.6
  94.2 0.3 collective-permute-start.7
  94.6 0.9 collective-permute-done.9.refs_1_
  95.5 2.1 %shard_map.109 = (bf16[128,1792]{1,0:T(8,128)(2,1)S(1)}, bf16[128,1792]{1,0:T(8,128)(2,1)S(1)}) custom-call(bf16[128,2048]{1,0:T(8,128)(2,1)S(1)} %collective-permute-done.8.refs_0_, bf16[128,2048]{1,0:T(8,128)(2,1)S(1)} %collective-permute-done.9.refs_1_, bf16[2048,896]{1,0:T(8,128)(2,1)S(1)} %bitcast.51, bf16[2048,896]{1,0:T(8,128)(2,1)S(1)} %shard_map.104.refs_4_.refs_3_), custom_call_target="tpu_custom_call" | custom-call | flops 1879048192 | bytes 8388608 | tf_op jit(solution)/shard_map/pallas_call | solution.py:122
  97.6 1.1 shard_map.110
  98.8 0.6 collective-permute-start.10
  99.3 1.9 %shard_map.113 = (bf16[128,1024]{1,0:T(8,128)(2,1)}, bf16[128,1024]{1,0:T(8,128)(2,1)}) custom-call(bf16[128,1792]{1,0:T(8,128)(2,1)S(1)} %get-tuple-element.39.refs_0_, bf16[128,1792]{1,0:T(8,128)(2,1)S(1)} %get-tuple-element.40.refs_1_, bf16[896,2048]{1,0:T(8,128)(2,1)S(1)} %bitcast.45, bf16[896,2048]{1,0:T(8,128)(2,1)S(1)} %shard_map.107.other_ref.refs_5_.refs_3_), custom_call_target="tpu_custom_call" | custom-call | flops 939524096 | bytes 4194304 | tf_op jit(solution)/shard_map/pallas_call | solution.py:227
  101.2 2.4 %collective-permute-start.12 = (bf16[128,1024]{1,0:T(8,128)(2,1)}, bf16[128,1024]{1,0:T(8,128)(2,1)S(1)}, u32[]{:S(2)}, u32[]{:S(2)}) collective-permute-start(bf16[128,1024]{1,0:T(8,128)(2,1)} %get-tuple-element.43), channel_id=1, source_target_pairs={{0,3},{1,0},{2,1},{3,2},{4,7},{5,4},{6,5},{7,6},{8,11},{9,8},{10,9... | collective-permute-start | bytes 786440 | tf_op jit(solution)/shard_map/ppermute | solution.py:25
  103.6 0.9 collective-permute-start.13
  104.5 2.1 %down_own.1 = (f32[2,128,1024]{2,1,0:T(8,128)S(1)}, f32[2,128,1024]{2,1,0:T(8,128)S(1)}) custom-call(bf16[128,1792]{1,0:T(8,128)(2,1)S(1)} %get-tuple-element.30.first_ref, bf16[128,1792]{1,0:T(8,128)(2,1)S(1)} %get-tuple-element.31.second_ref, bf16[896,2048]{1,0:T(8,128)(2,1)S(1)} %bitcast.46, bf16[896,2048]{1,0:T(8,128)(2,1)S(1)} %shard_map.107.other_ref.refs_5_.refs_3_), custom_call_target="tpu_custom_call" | custom-call | flops 1879048192 | bytes 9437184 | tf_op jit(solution)/shard_map/down_own/pallas_call | solution.py:178
  106.5 1.0 copy-done.6
  107.5 9.7 %collective-permute-done.6.refs_0_ = bf16[2,128,1024]{2,1,0:T(8,128)(2,1)S(1)} collective-permute-done((bf16[2,128,1024]{2,1,0:T(8,128)(2,1)S(1)}, bf16[2,128,1024]{2,1,0:T(8,128)(2,1)S(1)}, u32[]{:S(2)}, u32[]{:S(2)}) %collective-permute-start.6) | collective-permute-done | bytes 524320 | tf_op jit(solution)/shard_map/ppermute | solution.py:25
  117.2 4.2 %collective-permute-done.7.refs_1_ = bf16[2,128,1024]{2,1,0:T(8,128)(2,1)S(1)} collective-permute-done((bf16[2,128,1024]{2,1,0:T(8,128)(2,1)S(1)}, bf16[2,128,1024]{2,1,0:T(8,128)(2,1)S(1)}, u32[]{:S(2)}, u32[]{:S(2)}) %collective-permute-start.7) | collective-permute-done | bytes 524320 | tf_op jit(solution)/shard_map/ppermute | solution.py:25
  121.5 1.0 shard_map.111
  122.5 7.0 %all-to-all-start.3 = ((bf16[8,2,16,1024]{3,2,1,0:T(8,128)(2,1)}), bf16[8,2,16,1024]{3,2,1,0:T(8,128)(2,1)S(1)}, u32[]{:S(2)}, u32[]{:S(2)}) async-start(bf16[8,2,16,1024]{3,2,1,0:T(8,128)(2,1)} %shard_map.111), calls=%async_computation.3 | async-start | bytes 1048576 | tf_op jit(solution)/shard_map/all_to_all | solution.py:29
  129.5 0.7 reshape.267
  130.3 0.1 copy.18
  130.4 0.1 copy.17
  130.5 2.0 %copy-done.2 = bf16[896,2048]{1,0:T(8,128)(2,1)S(1)} copy-done((bf16[896,2048]{1,0:T(8,128)(2,1)S(1)}, bf16[896,2048]{1,0:T(8,128)(2,1)}, u32[]{:S(2)}) %copy-start.2) | copy-done | bytes 3670040
  132.6 2.0 %copy-done.4 = bf16[1,896,2048]{2,1,0:T(8,128)(2,1)S(1)} copy-done((bf16[1,896,2048]{2,1,0:T(8,128)(2,1)S(1)}, bf16[1,896,2048]{2,1,0:T(8,128)(2,1)}, u32[]{:S(2)}) %copy-start.4) | copy-done | bytes 3670040
  134.6 2.1 %shard_map.114 = (bf16[2,128,1024]{2,1,0:T(8,128)(2,1)S(1)}, bf16[2,128,1024]{2,1,0:T(8,128)(2,1)S(1)}) custom-call(bf16[128,1792]{1,0:T(8,128)(2,1)S(1)} %get-tuple-element.33.refs_0_, bf16[128,1792]{1,0:T(8,128)(2,1)S(1)} %get-tuple-element.34.refs_1_, bf16[128,1792]{1,0:T(8,128)(2,1)S(1)} %get-tuple-element.35.refs_2_, ...), custom_call_target="tpu_custom_call" | custom-call | flops 1879048192 | bytes 4718592 | tf_op jit(solution)/shard_map/pallas_call | solution.py:227
  136.8 2.0 %collective-permute-start.15 = (bf16[2,128,1024]{2,1,0:T(8,128)(2,1)S(1)}, bf16[2,128,1024]{2,1,0:T(8,128)(2,1)S(1)}, u32[]{:S(2)}, u32[]{:S(2)}) collective-permute-start(bf16[2,128,1024]{2,1,0:T(8,128)(2,1)S(1)} %get-tuple-element.46), channel_id=1, source_target_pairs={{0,3},{1,0},{2,1},{3,2},{4,7},{5,4},{6,5},{7,6},{8,11},{9,8},{10,9... | collective-permute-start | bytes 1572872 | tf_op jit(solution)/shard_map/ppermute | solution.py:25
  138.8 0.2 select_reduce_fusion
  139.0 6.9 %collective-permute-done.14.refs_0_ = bf16[2,128,1024]{2,1,0:T(8,128)(2,1)S(1)} collective-permute-done((bf16[2,128,1024]{2,1,0:T(8,128)(2,1)S(1)}, bf16[2,128,1024]{2,1,0:T(8,128)(2,1)S(1)}, u32[]{:S(2)}, u32[]{:S(2)}) %collective-permute-start.14) | collective-permute-done | bytes 524320 | tf_op jit(solution)/shard_map/ppermute | solution.py:25
  145.9 1.3 collective-permute-done.15.refs_1_
  147.2 1.0 shard_map.115
  148.2 7.2 %all-to-all-start.4 = ((bf16[8,2,16,1024]{3,2,1,0:T(8,128)(2,1)}), bf16[8,2,16,1024]{3,2,1,0:T(8,128)(2,1)S(1)}, u32[]{:S(2)}, u32[]{:S(2)}) async-start(bf16[8,2,16,1024]{3,2,1,0:T(8,128)(2,1)} %shard_map.115), calls=%async_computation.4 | async-start | bytes 1048576 | tf_op jit(solution)/shard_map/all_to_all | solution.py:29
  155.4 3.2 %gather_fusion.2 = bf16[8,2,16,2048]{3,2,1,0:T(8,128)(2,1)} fusion(bf16[16,2,16,2048]{3,2,1,0:T(8,128)(2,1)} %all-to-all-done.1, s32[1024]{0:T(1024)S(1)} %pad_clamp_fusion), kind=kCustom, calls=%fused_computation.2 | custom fusion | bytes 2097184 | tf_op jit(solution)/shard_map/gather | solution.py:351
  158.6 1.3 fusion.8
  160.0 0.5 shard_map.112
  160.4 3.2 %collective-permute-start.11 = (bf16[128,1024]{1,0:T(8,128)(2,1)S(1)}, bf16[128,1024]{1,0:T(8,128)(2,1)S(1)}, u32[]{:S(2)}, u32[]{:S(2)}) collective-permute-start(bf16[128,1024]{1,0:T(8,128)(2,1)S(1)} %get-tuple-element.41), channel_id=1, source_target_pairs={{0,64},{64,128},{128,192},{1,65},{65,129},{129,193},{2,66},{66,130... | collective-permute-start | bytes 786440 | tf_op jit(solution)/shard_map/ppermute | solution.py:366
  163.6 5.1 %all-to-all-done.4 = bf16[8,2,16,1024]{3,2,1,0:T(8,128)(2,1)S(1)} async-done(((bf16[8,2,16,1024]{3,2,1,0:T(8,128)(2,1)}), bf16[8,2,16,1024]{3,2,1,0:T(8,128)(2,1)S(1)}, u32[]{:S(2)}, u32[]{:S(2)}) %all-to-all-start.4) | async-done | bytes 524320 | tf_op jit(solution)/shard_map/all_to_all | solution.py:29
  168.7 0.5 shard_map.116
  169.2 3.2 %collective-permute-start.16 = (bf16[128,1024]{1,0:T(8,128)(2,1)S(1)}, bf16[128,1024]{1,0:T(8,128)(2,1)S(1)}, u32[]{:S(2)}, u32[]{:S(2)}) collective-permute-start(bf16[128,1024]{1,0:T(8,128)(2,1)S(1)} %get-tuple-element.47), channel_id=1, source_target_pairs={{0,64},{64,128},{128,192},{1,65},{65,129},{129,193},{2,66},{66,130... | collective-permute-start | bytes 786440 | tf_op jit(solution)/shard_map/ppermute | solution.py:366
  172.4 0.8 maximum_bitcast_fusion
  173.2 4.2 %collective-permute-done.16 = bf16[128,1024]{1,0:T(8,128)(2,1)S(1)} collective-permute-done((bf16[128,1024]{1,0:T(8,128)(2,1)S(1)}, bf16[128,1024]{1,0:T(8,128)(2,1)S(1)}, u32[]{:S(2)}, u32[]{:S(2)}) %collective-permute-start.16) | collective-permute-done | bytes 262176 | tf_op jit(solution)/shard_map/ppermute | solution.py:366
  177.4 0.9 fusion
  (46 shorter events, 0.3 us)
Async XLA Ops:
  0.6 33.5 %copy-start = (bf16[1,128,2048]{2,1,0:T(8,128)(2,1)S(1)}, bf16[1,128,2048]{2,1,0:T(8,128)(2,1)}, u32[]{:S(2)}) copy-start(bf16[1,128,2048]{2,1,0:T(8,128)(2,1)} %param.10) | copy-start | bytes 1572868
  0.6 1.1 copy-start.8
  1.7 0.7 copy-start.9
  2.4 32.4 %copy-start.10 = (bf16[1,128,2048]{2,1,0:T(8,128)(2,1)S(1)}, bf16[1,128,2048]{2,1,0:T(8,128)(2,1)}, u32[]{:S(2)}) copy-start(bf16[1,128,2048]{2,1,0:T(8,128)(2,1)} %param.11) | copy-start | bytes 1572868
  3.8 26.0 %all-to-all-start = ((bf16[8,16,2048]{2,1,0:T(8,128)(2,1)}), bf16[8,16,2048]{2,1,0:T(8,128)(2,1)S(1)}, u32[]{:S(2)}, u32[]{:S(2)}) async-start(bf16[8,16,2048]{2,1,0:T(8,128)(2,1)} %bitcast.9), calls=%async_computation | async-start | bytes 1048576 | tf_op jit(solution)/shard_map/all_to_all | solution.py:29
  12.3 61.5 %collective-permute-start.2 = (bf16[2048,896]{1,0:T(8,128)(2,1)}, bf16[2048,896]{1,0:T(8,128)(2,1)}, u32[]{:S(2)}, u32[]{:S(2)}) collective-permute-start(bf16[2048,896]{1,0:T(8,128)(2,1)} %bitcast.48), channel_id=1, source_target_pairs={{0,4},{4,0},{1,5},{5,1},{2,6},{6,2},{3,7},{7,3},{8,12},{12,8},{9,1... | collective-permute-start | bytes 11010056 | tf_op jit(solution)/shard_map/ppermute | solution.py:25
  12.3 72.7 %collective-permute-start.5 = (bf16[896,2048]{1,0:T(8,128)(2,1)}, bf16[896,2048]{1,0:T(8,128)(2,1)}, u32[]{:S(2)}, u32[]{:S(2)}) collective-permute-start(bf16[896,2048]{1,0:T(8,128)(2,1)} %bitcast.42), channel_id=1, source_target_pairs={{0,4},{4,0},{1,5},{5,1},{2,6},{6,2},{3,7},{7,3},{8,12},{12,8},{9,1... | collective-permute-start | bytes 11010056 | tf_op jit(solution)/shard_map/ppermute | solution.py:25
  29.8 21.4 %all-to-all-start.2 = ((bf16[8,16,2048]{2,1,0:T(8,128)(2,1)}), bf16[8,16,2048]{2,1,0:T(8,128)(2,1)S(1)}, u32[]{:S(2)}, u32[]{:S(2)}) async-start(bf16[8,16,2048]{2,1,0:T(8,128)(2,1)} %bitcast.17), calls=%async_computation.2 | async-start | bytes 1048576 | tf_op jit(solution)/shard_map/all_to_all | solution.py:29
  51.2 71.3 %all-to-all-start.1 = ((bf16[16,2,16,2048]{3,2,1,0:T(8,128)(2,1)}), bf16[16,2,16,2048]{3,2,1,0:T(8,128)(2,1)}, u32[]{:S(2)}, u32[]{:S(2)}) async-start(bf16[16,2,16,2048]{3,2,1,0:T(8,128)(2,1)} %pad_maximum_fusion), calls=%async_computation.1 | async-start | bytes 4194304 | tf_op jit(solution)/shard_map/all_to_all | solution.py:350
  55.6 26.1 %copy-start.5 = (bf16[1,2048,896]{2,1,0:T(8,128)(2,1)S(1)}, bf16[1,2048,896]{2,1,0:T(8,128)(2,1)}, u32[]{:S(2)}) copy-start(bf16[1,2048,896]{2,1,0:T(8,128)(2,1)} %param.12) | copy-start | bytes 11010052
  55.6 14.9 %collective-permute-start = (bf16[128,2048]{1,0:T(8,128)(2,1)S(1)}, bf16[128,2048]{1,0:T(8,128)(2,1)S(1)}, u32[]{:S(2)}, u32[]{:S(2)}) collective-permute-start(bf16[128,2048]{1,0:T(8,128)(2,1)S(1)} %bitcast.62), channel_id=1, source_target_pairs={{0,1},{1,2},{2,3},{3,0},{4,5},{5,6},{6,7},{7,4},{8,9},{9,10},{10,1... | collective-permute-start | bytes 1572872 | tf_op jit(solution)/shard_map/ppermute | solution.py:25
  56.2 15.1 %collective-permute-start.4 = (bf16[128,2048]{1,0:T(8,128)(2,1)S(1)}, bf16[128,2048]{1,0:T(8,128)(2,1)S(1)}, u32[]{:S(2)}, u32[]{:S(2)}) collective-permute-start(bf16[128,2048]{1,0:T(8,128)(2,1)S(1)} %bitcast.59), channel_id=1, source_target_pairs={{0,3},{1,0},{2,1},{3,2},{4,7},{5,4},{6,5},{7,6},{8,11},{9,8},{10,9... | collective-permute-start | bytes 1572872 | tf_op jit(solution)/shard_map/ppermute | solution.py:25
  57.7 24.0 %collective-permute-start.3 = (bf16[128,2048]{1,0:T(8,128)(2,1)S(1)}, bf16[128,2048]{1,0:T(8,128)(2,1)S(1)}, u32[]{:S(2)}, u32[]{:S(2)}) collective-permute-start(bf16[128,2048]{1,0:T(8,128)(2,1)S(1)} %bitcast.60), channel_id=1, source_target_pairs={{0,1},{1,2},{2,3},{3,0},{4,5},{5,6},{6,7},{7,4},{8,9},{9,10},{10,1... | collective-permute-start | bytes 1572872 | tf_op jit(solution)/shard_map/ppermute | solution.py:25
  70.5 16.6 %collective-permute-start.1 = (bf16[128,2048]{1,0:T(8,128)(2,1)S(1)}, bf16[128,2048]{1,0:T(8,128)(2,1)S(1)}, u32[]{:S(2)}, u32[]{:S(2)}) collective-permute-start(bf16[128,2048]{1,0:T(8,128)(2,1)S(1)} %bitcast.63), channel_id=1, source_target_pairs={{0,3},{1,0},{2,1},{3,2},{4,7},{5,4},{6,5},{7,6},{8,11},{9,8},{10,9... | collective-permute-start | bytes 1572872 | tf_op jit(solution)/shard_map/ppermute | solution.py:25
  71.3 23.3 %collective-permute-start.8 = (bf16[128,2048]{1,0:T(8,128)(2,1)S(1)}, bf16[128,2048]{1,0:T(8,128)(2,1)S(1)}, u32[]{:S(2)}, u32[]{:S(2)}) collective-permute-start(bf16[128,2048]{1,0:T(8,128)(2,1)S(1)} %collective-permute-done.refs_1_), channel_id=1, source_target_pairs={{0,1},{1,2},{2,3},{3,0},{4,5},{5,6},{6,7},{7,4},{8,9},{9,10},{10,1... | collective-permute-start | bytes 1572872 | tf_op jit(solution)/shard_map/ppermute | solution.py:25
  73.7 21.8 %collective-permute-start.9 = (bf16[128,2048]{1,0:T(8,128)(2,1)S(1)}, bf16[128,2048]{1,0:T(8,128)(2,1)S(1)}, u32[]{:S(2)}, u32[]{:S(2)}) collective-permute-start(bf16[128,2048]{1,0:T(8,128)(2,1)S(1)} %collective-permute-done.4.refs_2_), channel_id=1, source_target_pairs={{0,3},{1,0},{2,1},{3,2},{4,7},{5,4},{6,5},{7,6},{8,11},{9,8},{10,9... | collective-permute-start | bytes 1572872 | tf_op jit(solution)/shard_map/ppermute | solution.py:25
  87.0 17.4 %copy-start.1 = (bf16[896,2048]{1,0:T(8,128)(2,1)}, bf16[896,2048]{1,0:T(8,128)(2,1)S(1)}, u32[]{:S(2)}) copy-start(bf16[896,2048]{1,0:T(8,128)(2,1)S(1)} %shard_map.107.other_ref.refs_5_.refs_3_) | copy-start | bytes 11010052
  87.0 3.4 %copy-start.3 = (bf16[1,896,2048]{2,1,0:T(8,128)(2,1)S(1)}, bf16[1,896,2048]{2,1,0:T(8,128)(2,1)}, u32[]{:S(2)}) copy-start(bf16[1,896,2048]{2,1,0:T(8,128)(2,1)} %param.13) | copy-start | bytes 11010052
  92.5 24.8 %collective-permute-start.6 = (bf16[2,128,1024]{2,1,0:T(8,128)(2,1)S(1)}, bf16[2,128,1024]{2,1,0:T(8,128)(2,1)S(1)}, u32[]{:S(2)}, u32[]{:S(2)}) collective-permute-start(bf16[2,128,1024]{2,1,0:T(8,128)(2,1)S(1)} %get-tuple-element.37), channel_id=1, source_target_pairs={{0,1},{1,2},{2,3},{3,0},{4,5},{5,6},{6,7},{7,4},{8,9},{9,10},{10,1... | collective-permute-start | bytes 1572872 | tf_op jit(solution)/shard_map/ppermute | solution.py:25
  94.2 27.2 %collective-permute-start.7 = (bf16[2,128,1024]{2,1,0:T(8,128)(2,1)S(1)}, bf16[2,128,1024]{2,1,0:T(8,128)(2,1)S(1)}, u32[]{:S(2)}, u32[]{:S(2)}) collective-permute-start(bf16[2,128,1024]{2,1,0:T(8,128)(2,1)S(1)} %get-tuple-element.38), channel_id=1, source_target_pairs={{0,3},{1,0},{2,1},{3,2},{4,7},{5,4},{6,5},{7,6},{8,11},{9,8},{10,9... | collective-permute-start | bytes 1572872 | tf_op jit(solution)/shard_map/ppermute | solution.py:25
  98.8 22.7 %collective-permute-start.10 = (bf16[2,128,1024]{2,1,0:T(8,128)(2,1)S(1)}, bf16[2,128,1024]{2,1,0:T(8,128)(2,1)S(1)}, u32[]{:S(2)}, u32[]{:S(2)}) collective-permute-start(bf16[2,128,1024]{2,1,0:T(8,128)(2,1)S(1)} %shard_map.110), channel_id=1, source_target_pairs={{0,2},{1,3},{2,0},{3,1},{4,6},{5,7},{6,4},{7,5},{8,10},{9,11},{10,... | collective-permute-start | bytes 1572872 | tf_op jit(solution)/shard_map/ppermute | solution.py:25
  101.2 29.3 %collective-permute-start.12 = (bf16[128,1024]{1,0:T(8,128)(2,1)}, bf16[128,1024]{1,0:T(8,128)(2,1)S(1)}, u32[]{:S(2)}, u32[]{:S(2)}) collective-permute-start(bf16[128,1024]{1,0:T(8,128)(2,1)} %get-tuple-element.43), channel_id=1, source_target_pairs={{0,3},{1,0},{2,1},{3,2},{4,7},{5,4},{6,5},{7,6},{8,11},{9,8},{10,9... | collective-permute-start | bytes 786440 | tf_op jit(solution)/shard_map/ppermute | solution.py:25
  103.6 26.9 %collective-permute-start.13 = (bf16[128,1024]{1,0:T(8,128)(2,1)}, bf16[128,1024]{1,0:T(8,128)(2,1)S(1)}, u32[]{:S(2)}, u32[]{:S(2)}) collective-permute-start(bf16[128,1024]{1,0:T(8,128)(2,1)} %get-tuple-element.44), channel_id=1, source_target_pairs={{0,1},{1,2},{2,3},{3,0},{4,5},{5,6},{6,7},{7,4},{8,9},{9,10},{10,1... | collective-permute-start | bytes 786440 | tf_op jit(solution)/shard_map/ppermute | solution.py:25
  106.5 1.0 copy-start.6
  107.5 22.0 %copy-start.14 = (s32[8]{0:T(128)S(1)}, s32[8]{0:T(128)}, u32[]{:S(2)}) copy-start(s32[8]{0:T(128)} %param.16) | copy-start | bytes 100
  107.5 22.8 %copy-start.13 = (s32[1,128,2]{1,2,0:T(2,128)S(1)}, s32[1,128,2]{1,2,0:T(2,128)}, u32[]{:S(2)}) copy-start(s32[1,128,2]{1,2,0:T(2,128)} %param.15) | copy-start | bytes 3076
  122.5 25.7 %all-to-all-start.3 = ((bf16[8,2,16,1024]{3,2,1,0:T(8,128)(2,1)}), bf16[8,2,16,1024]{3,2,1,0:T(8,128)(2,1)S(1)}, u32[]{:S(2)}, u32[]{:S(2)}) async-start(bf16[8,2,16,1024]{3,2,1,0:T(8,128)(2,1)} %shard_map.111), calls=%async_computation.3 | async-start | bytes 1048576 | tf_op jit(solution)/shard_map/all_to_all | solution.py:29
  130.4 8.4 %copy-start.12 = (s32[512]{0:T(512)S(1)}, s32[512]{0:T(512)}, u32[]{:S(2)}) copy-start(s32[512]{0:T(512)} %param.17) | copy-start | bytes 6148
  130.5 2.0 %copy-start.2 = (bf16[896,2048]{1,0:T(8,128)(2,1)S(1)}, bf16[896,2048]{1,0:T(8,128)(2,1)}, u32[]{:S(2)}) copy-start(bf16[896,2048]{1,0:T(8,128)(2,1)} %copy-done.1) | copy-start | bytes 11010052
  132.6 2.0 %copy-start.4 = (bf16[1,896,2048]{2,1,0:T(8,128)(2,1)S(1)}, bf16[1,896,2048]{2,1,0:T(8,128)(2,1)}, u32[]{:S(2)}) copy-start(bf16[1,896,2048]{2,1,0:T(8,128)(2,1)} %param.13) | copy-start | bytes 11010052
  134.6 12.6 %copy-start.7 = (f32[2,128,1024]{2,1,0:T(8,128)S(1)}, f32[2,128,1024]{2,1,0:T(8,128)}, u32[]{:S(2)}) copy-start(f32[2,128,1024]{2,1,0:T(8,128)} %copy-done.6) | copy-start | bytes 3145732
  136.7 18.8 %copy-start.11 = (s32[128,1]{1,0:T(8,128)S(1)}, s32[128,1]{1,0:T(8,128)}, u32[]{:S(2)}) copy-start(s32[128,1]{1,0:T(8,128)} %reshape.267) | copy-start | bytes 1540
  136.7 9.3 %collective-permute-start.14 = (bf16[2,128,1024]{2,1,0:T(8,128)(2,1)S(1)}, bf16[2,128,1024]{2,1,0:T(8,128)(2,1)S(1)}, u32[]{:S(2)}, u32[]{:S(2)}) collective-permute-start(bf16[2,128,1024]{2,1,0:T(8,128)(2,1)S(1)} %get-tuple-element.45), channel_id=1, source_target_pairs={{0,1},{1,2},{2,3},{3,0},{4,5},{5,6},{6,7},{7,4},{8,9},{9,10},{10,1... | collective-permute-start | bytes 1572872 | tf_op jit(solution)/shard_map/ppermute | solution.py:25
  136.8 10.5 %collective-permute-start.15 = (bf16[2,128,1024]{2,1,0:T(8,128)(2,1)S(1)}, bf16[2,128,1024]{2,1,0:T(8,128)(2,1)S(1)}, u32[]{:S(2)}, u32[]{:S(2)}) collective-permute-start(bf16[2,128,1024]{2,1,0:T(8,128)(2,1)S(1)} %get-tuple-element.46), channel_id=1, source_target_pairs={{0,3},{1,0},{2,1},{3,2},{4,7},{5,4},{6,5},{7,6},{8,11},{9,8},{10,9... | collective-permute-start | bytes 1572872 | tf_op jit(solution)/shard_map/ppermute | solution.py:25
  148.2 20.5 %all-to-all-start.4 = ((bf16[8,2,16,1024]{3,2,1,0:T(8,128)(2,1)}), bf16[8,2,16,1024]{3,2,1,0:T(8,128)(2,1)S(1)}, u32[]{:S(2)}, u32[]{:S(2)}) async-start(bf16[8,2,16,1024]{3,2,1,0:T(8,128)(2,1)} %shard_map.115), calls=%async_computation.4 | async-start | bytes 1048576 | tf_op jit(solution)/shard_map/all_to_all | solution.py:29
  160.4 12.8 %collective-permute-start.11 = (bf16[128,1024]{1,0:T(8,128)(2,1)S(1)}, bf16[128,1024]{1,0:T(8,128)(2,1)S(1)}, u32[]{:S(2)}, u32[]{:S(2)}) collective-permute-start(bf16[128,1024]{1,0:T(8,128)(2,1)S(1)} %get-tuple-element.41), channel_id=1, source_target_pairs={{0,64},{64,128},{128,192},{1,65},{65,129},{129,193},{2,66},{66,130... | collective-permute-start | bytes 786440 | tf_op jit(solution)/shard_map/ppermute | solution.py:366
  169.2 8.3 %collective-permute-start.16 = (bf16[128,1024]{1,0:T(8,128)(2,1)S(1)}, bf16[128,1024]{1,0:T(8,128)(2,1)S(1)}, u32[]{:S(2)}, u32[]{:S(2)}) collective-permute-start(bf16[128,1024]{1,0:T(8,128)(2,1)S(1)} %get-tuple-element.47), channel_id=1, source_target_pairs={{0,64},{64,128},{128,192},{1,65},{65,129},{129,193},{2,66},{66,130... | collective-permute-start | bytes 786440 | tf_op jit(solution)/shard_map/ppermute | solution.py:366

commit v4 on v3

--- a/solution.py
+++ b/solution.py
@@ -29,8 +29,8 @@
     return lax.all_to_all(value, "z", split_axis=0, concat_axis=0, tiled=True)
 
 
-def group_kernel(routing_ref, tokens_ref, *out_refs):
-    chunk_refs, slot_ref = out_refs[:-1], out_refs[-1]
+def group_kernel(plane_ref, routing_ref, tokens_ref, *out_refs):
+    chunk_ref, piece_refs, slot_ref = out_refs[0], out_refs[1:-1], out_refs[-1]
     rows = tokens_ref.shape[0]
     per_expert = rows * TOPK // EXPERTS
     part = per_expert // ROW_CHUNKS
@@ -52,26 +52,61 @@
     slot_ref[1:2, :] = slot_second
     tokens = tokens_ref[...]
     index = lax.broadcasted_iota(jnp.int32, (EXPERTS * part, rows), 0)
-    for chunk, chunk_ref in enumerate(chunk_refs):
-        wanted = index // part * per_expert + chunk * part + index % part
+    for chunk in range(ROW_CHUNKS):
+        expert = index // part
+        if chunk:
+            expert = (expert + plane_ref[0]) % EXPERTS
+        wanted = expert * per_expert + chunk * part + index % part
         chosen = ((slot_first == wanted) | (slot_second == wanted)).astype(F32).astype(BF16)
-        chunk_ref[...] = jnp.dot(chosen, tokens, preferred_element_type=F32).astype(BF16)
-
-
-def group_rows(routing, tokens):
+        picked = jnp.dot(chosen, tokens, preferred_element_type=F32).astype(BF16)
+        if chunk:
+            for away, ref in enumerate(piece_refs):
+                ref[...] = picked[away * part : (away + 1) * part]
+        else:
+            chunk_ref[...] = picked
+
+
+def join_kernel(plane_ref, *refs):
+    out_ref = refs[-1]
+    for away, ref in enumerate(refs[:-1]):
+        rows = ref.shape[0]
+        source = (plane_ref[0] + EXPERTS - away) % EXPERTS
+        out_ref[pl.ds(pl.multiple_of(source * rows, rows), rows), :] = ref[...]
+
+
+def join(plane, pieces):
+    rows, width = pieces[0].shape
+    vmem = pl.BlockSpec(memory_space=pltpu.VMEM)
+    return pl.pallas_call(
+        join_kernel,
+        in_specs=[pl.BlockSpec(memory_space=pltpu.SMEM)] + [vmem] * len(pieces),
+        out_shape=jax.ShapeDtypeStruct((rows * len(pieces), width), BF16),
+        compiler_params=pltpu.CompilerParams(vmem_limit_bytes=SMALL_VMEM),
+        cost_estimate=pl.CostEstimate(
+            flops=1000000, bytes_accessed=4 * rows * len(pieces) * width, transcendentals=0
+        ),
+    )(plane, *pieces)
+
+
+def group_rows(plane, routing, tokens):
     rows, width = tokens.shape
     slots = rows * TOPK
     chunk = jax.ShapeDtypeStruct((slots // ROW_CHUNKS, width), BF16)
+    piece = jax.ShapeDtypeStruct((slots // ROW_CHUNKS // EXPERTS, width), BF16)
+    vmem = pl.BlockSpec(memory_space=pltpu.VMEM)
     out = pl.pallas_call(
         group_kernel,
-        out_shape=(chunk,) * ROW_CHUNKS + (jax.ShapeDtypeStruct((TOPK, rows), jnp.int32),),
+        in_specs=[pl.BlockSpec(memory_space=pltpu.SMEM), vmem, vmem],
+        out_shape=(chunk,)
+        + (piece,) * EXPERTS
+        + (jax.ShapeDtypeStruct((TOPK, rows), jnp.int32),),
         compiler_params=pltpu.CompilerParams(vmem_limit_bytes=SMALL_VMEM),
         cost_estimate=pl.CostEstimate(
             flops=2 * slots * rows * width, bytes_accessed=3 * slots * width, transcendentals=0
         ),
         name="group_rows",
-    )(routing, tokens)
-    return out[:-1], out[-1]
+    )(plane, routing, tokens)
+    return out[0], out[1:-1], out[-1]
 
 
 def stage_kernel(slice_ref, out_ref, sem):
@@ -94,26 +129,36 @@
     )(value)
 
 
-def beside(first_ref, second_ref, start, stop):
-    width = first_ref.shape[1]
-    if stop <= width:
-        return first_ref[:, start:stop]
-    if start >= width:
-        return second_ref[:, start - width : stop - width]
-    return jnp.concatenate([first_ref[:, start:], second_ref[:, : stop - width]], axis=1)
-
-
 def up_kernel(count, *refs):
     row_refs, own_ref, other_ref, out_refs = refs[:count], refs[count], refs[count + 1], refs[count + 2 :]
     rows = jnp.concatenate([ref[...] for ref in row_refs], axis=0)
-    for start in range(0, 2 * own_ref.shape[1], TILE):
-        weights = beside(own_ref, other_ref, start, start + TILE)
+    units = own_ref.shape[1]
+    left = units % TILE
+
+    def tile(weights, start):
         value = jnp.dot(rows, weights, preferred_element_type=F32)
         hidden = (value / (1.0 + jnp.exp(-value))).astype(BF16)
         at = 0
         for ref in out_refs:
-            ref[:, start : start + TILE] = hidden[at : at + ref.shape[0]]
+            ref[:, pl.ds(start, TILE)] = hidden[at : at + ref.shape[0]]
             at += ref.shape[0]
+
+    def own_tile(number, carry):
+        start = pl.multiple_of(number * TILE, TILE)
+        tile(own_ref[:, pl.ds(start, TILE)], start)
+        return carry
+
+    def other_tile(number, carry):
+        start = pl.multiple_of(number * TILE + TILE - left, TILE // 2)
+        tile(other_ref[:, pl.ds(start, TILE)], pl.multiple_of(number * TILE + units + TILE - left, TILE))
+        return carry
+
+    lax.fori_loop(0, units // TILE, own_tile, 0)
+    tile(
+        jnp.concatenate([own_ref[:, units - left :], other_ref[:, : TILE - left]], axis=1),
+        units - left,
+    )
+    lax.fori_loop(0, units // TILE, other_tile, 0)
 
 
 def up(blocks, own, other):
@@ -200,6 +245,40 @@
             out_ref[:, number, :, here] = value.astype(BF16).reshape(groups, rows, TILE)
 
 
+def total_pieces_kernel(plane_ref, own_ref, *refs):
+    extra_refs, piece_refs, sum_ref = refs[: -EXPERTS - 1], refs[-EXPERTS - 1 : -1], refs[-1]
+    parts, rows, width = own_ref.shape
+    rows //= EXPERTS
+    for start in range(0, width, TILE):
+        here = slice(start, start + TILE)
+        for number in range(parts):
+            value = own_ref[number, :, here]
+            for ref in extra_refs:
+                value += ref[number, :, here].astype(F32)
+            sum_ref[number, :, here] = value.astype(BF16)
+    for away, ref in enumerate(piece_refs):
+        source = (plane_ref[0] + away) % EXPERTS
+        from_rows = pl.ds(pl.multiple_of(source * rows, rows), rows)
+        for number in range(parts):
+            ref[number * rows : (number + 1) * rows, :] = sum_ref[number, from_rows, :]
+
+
+def total_pieces(plane, own, others):
+    parts, rows, width = own.shape
+    vmem = pl.BlockSpec(memory_space=pltpu.VMEM)
+    piece = jax.ShapeDtypeStruct((parts * rows // EXPERTS, width), BF16)
+    return pl.pallas_call(
+        total_pieces_kernel,
+        in_specs=[pl.BlockSpec(memory_space=pltpu.SMEM)] + [vmem] * (1 + len(others)),
+        out_shape=[piece] * EXPERTS,
+        scratch_shapes=[pltpu.VMEM(own.shape, BF16)],
+        compiler_params=pltpu.CompilerParams(vmem_limit_bytes=LARGE_VMEM),
+        cost_estimate=pl.CostEstimate(
+            flops=4 * own.size, bytes_accessed=12 * own.size, transcendentals=0
+        ),
+    )(plane, own, *others)
+
+
 def total(own, others, groups):
     parts, rows, width = own.shape
     return pl.pallas_call(
@@ -236,9 +315,10 @@
     )(*hidden, own, other, *extras)
 
 
-def combine_kernel(slot_ref, gate_ref, live_ref, moved_ref, back_ref, delta_ref, cache_ref):
+def combine_kernel(slot_ref, gate_ref, live_ref, moved_ref, *refs):
+    back_refs, (delta_ref, cache_ref) = refs[:-2], refs[-2:]
     rows = slot_ref.shape[0]
-    back = back_ref[...]
+    back = jnp.concatenate([ref[...] for ref in back_refs], axis=0)
     slots = back.shape[0]
     slot_lanes = lax.broadcasted_iota(jnp.int32, (rows, slots), 1)
     slot = slot_ref[...]
@@ -267,7 +347,7 @@
             bytes_accessed=(2 * TOPK + 6) * moved.size,
             transcendentals=0,
         ),
-    )(slot, gates, live, moved, back)
+    )(slot, gates, live, moved, *back)
 
 
 def section_step(
@@ -281,9 +361,13 @@
     own_dp = lax.axis_index(("z", "core"))
     own_device = own_dp * x_count + lax.axis_index("x")
 
-    chunks, slot = group_rows(routing[0].T, inputs[0])
+    plane = lax.axis_index("z").astype(jnp.int32)[None]
+    order = sorted(range(1, z_count), key=lambda away: -min(away, z_count - away))
+    chunk, pieces, slot = group_rows(plane, routing[0].T, inputs[0])
     up_own, down_own = w_up[0], w_down[0]
-    blocks = [exchanged(chunk.reshape(z_count, -1, width)).reshape(-1, width) for chunk in chunks]
+    blocks = [exchanged(chunk.reshape(z_count, -1, width)).reshape(-1, width)]
+    got = {away: shifted(pieces[away], "z", away) for away in order}
+    blocks.append(join(plane, [pieces[0]] + [got[away] for away in range(1, z_count)]))
     up_other = shifted(up_own, "core", 1)
     down_other = shifted(down_own, "core", 1)
     up_other, down_other = stage(up_other), stage(down_other)
@@ -320,8 +404,12 @@
     )
     got_right = shifted(to_left, "x", -1)
     got_left = shifted(to_right, "x", 1)
-    second_back = total(own_terms[1], (got_left, got_right), z_count)
-    backs = [exchanged(summed).reshape(tok_rows * TOPK, -1) for summed in (first_back, second_back)]
+    second_back = total_pieces(plane, own_terms[1], (got_left, got_right))
+    got = {away: shifted(second_back[away], "z", away) for away in order}
+    backs = [
+        [exchanged(first_back).reshape(tok_rows * TOPK, -1)],
+        [second_back[0]] + [got[away] for away in range(1, z_count)],
+    ]
 
     own_map = lax.dynamic_slice_in_dim(sample_map, own_device * SAMP_DEV, SAMP_DEV)
     dest_dp = own_map // SAMP_DEV // x_count
@@ -356,12 +444,14 @@
         jnp.arange(tok_rows, dtype=jnp.int32) % ROWS < jnp.repeat(lengths, ROWS)
     ).astype(jnp.int32)[:, None]
     slot = slot.T
+    per_expert = tok_rows * TOPK // EXPERTS
+    behind = (plane[0] + EXPERTS - slot // per_expert) % EXPERTS * per_expert + slot % per_expert
     sections = lax.axis_size("section")
     caches, arrivals = [], []
     part = width // FEATURE_CHUNKS
     for f, back in enumerate(backs):
         columns = out_moved[:, f * part : (f + 1) * part]
-        delta, cache = combine(back, slot, gate_table[0], live, columns)
+        delta, cache = combine(back, behind if f else slot, gate_table[0], live, columns)
         caches.append(cache)
         arrivals.append(lax.ppermute(delta, "section", [(i, i + 1) for i in range(sections - 1)]))
     new_out = jnp.concatenate(caches, axis=1)

time: 179 us -> 187 us (1.045)
  the two profiles are of different devices: /device:TPU:22 before, /device:TPU:14 now
where the time goes in v4:
time: 187 us
  starting transfers between devices  79.7 us (43%)
  waiting for transfers between devices  50.9 us (27%)
  Pallas kernels  32.5 us (17%)
  local copies, waits for them, and re-layouts  16.9 us (9%)
  other arithmetic  5.65 us (3%)
    ppermute x29, starting transfers between devices, shifted(): lax.ppermute(value, axis, [(i, (i + by) % peers) for i in range(peers)])  53.3 us
    ppermute x29, waiting for transfers between devices, shifted(): lax.ppermute(value, axis, [(i, (i + by) % peers) for i in range(peers)])  46.7 us
    all_to_all x2, starting transfers between devices, exchanged(): return lax.all_to_all(value, 'z', split_axis=0, concat_axis=0, tiled=True)  15.3 us
    pallas_call x3, Pallas kernels, up(): pl.pallas_call(functools.partial(up_kernel, len(blocks)), out_shape=[jax....  13.2 us
    unnamed x31, local copies, waits for them, and re-layouts  8.74 us
    pallas_call x4, Pallas kernels, down(): pl.pallas_call(functools.partial(down_kernel, len(hidden), chunk, added),...  8.16 us
    ppermute x2, starting transfers between devices, section_step(): lax.ppermute(delta, 'section', [(i, i + 1) for i in range(sections - 1)])  6.68 us
    all_to_all x1, starting transfers between devices, section_step(): lax.all_to_all(sent, ('z', 'core'), split_axis=0, concat_axis=0, tiled=True)  4.49 us
  transfers between devices with their start and end apart: 34, of which 12 were waited for; matrix products, arithmetic and copies ran while one was open for 7% of the time, Pallas kernels for 17%

profile of v4, /device:TPU:14, one launch (start us, length us, event | category | flops | bytes accessed | tf_op | source)
XLA Modules:
  0.0 186.7 jit_solution(9239060317749771287)
XLA Ops:
  0.7 0.5 collective-permute-start.12
  1.2 1.0 copy-done.6
  2.3 0.7 copy-done.11
  3.0 1.2 group_rows.1
  4.2 8.5 %all-to-all-start.1 = ((bf16[8,16,2048]{2,1,0:T(8,128)(2,1)}), bf16[8,16,2048]{2,1,0:T(8,128)(2,1)S(1)}, u32[]{:S(2)}, u32[]{:S(2)}) async-start(bf16[8,16,2048]{2,1,0:T(8,128)(2,1)} %bitcast.16), calls=%async_computation.1 | async-start | bytes 1048576 | tf_op jit(solution)/shard_map/all_to_all | solution.py:29
  12.7 2.0 %collective-permute-start = (bf16[16,2048]{1,0:T(8,128)(2,1)S(1)}, bf16[16,2048]{1,0:T(8,128)(2,1)S(1)}, u32[]{:S(2)}, u32[]{:S(2)}) collective-permute-start(bf16[16,2048]{1,0:T(8,128)(2,1)S(1)} %get-tuple-element.42), channel_id=1, source_target_pairs={{0,8},{8,16},{16,24},{24,32},{32,40},{40,48},{48,56},{56,0},{1,9},... | collective-permute-start | bytes 196616 | tf_op jit(solution)/shard_map/ppermute | solution.py:25
  14.7 2.4 %collective-permute-start.1 = (bf16[16,2048]{1,0:T(8,128)(2,1)S(1)}, bf16[16,2048]{1,0:T(8,128)(2,1)S(1)}, u32[]{:S(2)}, u32[]{:S(2)}) collective-permute-start(bf16[16,2048]{1,0:T(8,128)(2,1)S(1)} %get-tuple-element.43), channel_id=1, source_target_pairs={{0,16},{8,24},{16,32},{24,40},{32,48},{40,56},{48,0},{56,8},{1,17}... | collective-permute-start | bytes 196616 | tf_op jit(solution)/shard_map/ppermute | solution.py:25
  17.1 2.7 %collective-permute-start.2 = (bf16[16,2048]{1,0:T(8,128)(2,1)S(1)}, bf16[16,2048]{1,0:T(8,128)(2,1)S(1)}, u32[]{:S(2)}, u32[]{:S(2)}) collective-permute-start(bf16[16,2048]{1,0:T(8,128)(2,1)S(1)} %get-tuple-element.44), channel_id=1, source_target_pairs={{0,24},{8,32},{16,40},{24,48},{32,56},{40,0},{48,8},{56,16},{1,25}... | collective-permute-start | bytes 196616 | tf_op jit(solution)/shard_map/ppermute | solution.py:25
  19.7 0.8 and_select_fusion.2
  20.6 10.2 %collective-permute-done.refs_1_ = bf16[16,2048]{1,0:T(8,128)(2,1)S(1)} collective-permute-done((bf16[16,2048]{1,0:T(8,128)(2,1)S(1)}, bf16[16,2048]{1,0:T(8,128)(2,1)S(1)}, u32[]{:S(2)}, u32[]{:S(2)}) %collective-permute-start) | collective-permute-done | bytes 65568 | tf_op jit(solution)/shard_map/ppermute | solution.py:25
  30.8 2.8 %collective-permute-start.3 = (bf16[16,2048]{1,0:T(8,128)(2,1)S(1)}, bf16[16,2048]{1,0:T(8,128)(2,1)S(1)}, u32[]{:S(2)}, u32[]{:S(2)}) collective-permute-start(bf16[16,2048]{1,0:T(8,128)(2,1)S(1)} %get-tuple-element.45), channel_id=1, source_target_pairs={{0,32},{8,40},{16,48},{24,56},{32,0},{40,8},{48,16},{56,24},{1,33}... | collective-permute-start | bytes 196616 | tf_op jit(solution)/shard_map/ppermute | solution.py:25
  33.6 0.6 gather_fusion.1
  34.2 2.7 %gather_fusion = bf16[16,16,2048]{2,1,0:T(8,128)(2,1)} fusion(bf16[8,16,2048]{2,1,0:T(8,128)(2,1)} %bitcast.62, s32[1024]{0:T(1024)S(1)} %pad_clamp_fusion.1), kind=kCustom, calls=%fused_computation | custom fusion | bytes 2097216 | tf_op jit(solution)/shard_map/gather | solution.py:432
  37.3 5.1 %collective-permute-start.5 = (bf16[16,2048]{1,0:T(8,128)(2,1)S(1)}, bf16[16,2048]{1,0:T(8,128)(2,1)S(1)}, u32[]{:S(2)}, u32[]{:S(2)}) collective-permute-start(bf16[16,2048]{1,0:T(8,128)(2,1)S(1)} %get-tuple-element.47), channel_id=1, source_target_pairs={{0,48},{8,56},{16,0},{24,8},{32,16},{40,24},{48,32},{56,40},{1,49}... | collective-permute-start | bytes 196616 | tf_op jit(solution)/shard_map/ppermute | solution.py:25
  42.3 2.7 %pad_maximum_fusion = bf16[16,2,16,2048]{3,2,1,0:T(8,128)(2,1)} fusion(bf16[16,1,16,2048]{3,2,1,0:T(8,128)(2,1)S(1)} %bitcast.60, bf16[16,1,16,2048]{3,2,1,0:T(8,128)(2,1)} %bitcast.61), kind=kLoop, calls=%fused_computation.3 | loop fusion | flops 1048576 | bytes 4194304 | tf_op jit(solution)/shard_map/concatenate | solution.py:430
  45.5 1.5 collective-permute-done.6.refs_7_
  47.0 4.5 %all-to-all-start = ((bf16[16,2,16,2048]{3,2,1,0:T(8,128)(2,1)}), bf16[16,2,16,2048]{3,2,1,0:T(8,128)(2,1)}, u32[]{:S(2)}, u32[]{:S(2)}) async-start(bf16[16,2,16,2048]{3,2,1,0:T(8,128)(2,1)} %pad_maximum_fusion), calls=%async_computation | async-start | bytes 4194304 | tf_op jit(solution)/shard_map/all_to_all | solution.py:438
  51.5 0.9 collective-permute-start.11
  52.4 2.4 %collective-permute-start.7 = (bf16[128,2048]{1,0:T(8,128)(2,1)S(1)}, bf16[128,2048]{1,0:T(8,128)(2,1)S(1)}, u32[]{:S(2)}, u32[]{:S(2)}) collective-permute-start(bf16[128,2048]{1,0:T(8,128)(2,1)S(1)} %bitcast.56), channel_id=1, source_target_pairs={{0,1},{1,2},{2,3},{3,0},{4,5},{5,6},{6,7},{7,4},{8,9},{9,10},{10,1... | collective-permute-start | bytes 1572872 | tf_op jit(solution)/shard_map/ppermute | solution.py:25
  54.9 12.1 %collective-permute-done.11.refs_2_ = bf16[128,2048]{1,0:T(8,128)(2,1)} collective-permute-done((bf16[128,2048]{1,0:T(8,128)(2,1)S(1)}, bf16[128,2048]{1,0:T(8,128)(2,1)}, u32[]{:S(2)}, u32[]{:S(2)}) %collective-permute-start.11) | collective-permute-done | bytes 524320 | tf_op jit(solution)/shard_map/ppermute | solution.py:25
  66.9 3.2 %collective-permute-start.15 = (bf16[128,2048]{1,0:T(8,128)(2,1)S(1)}, bf16[128,2048]{1,0:T(8,128)(2,1)S(1)}, u32[]{:S(2)}, u32[]{:S(2)}) collective-permute-start(bf16[128,2048]{1,0:T(8,128)(2,1)S(1)} %collective-permute-done.7.refs_1_), channel_id=1, source_target_pairs={{0,1},{1,2},{2,3},{3,0},{4,5},{5,6},{6,7},{7,4},{8,9},{9,10},{10,1... | collective-permute-start | bytes 1572872 | tf_op jit(solution)/shard_map/ppermute | solution.py:25
  70.6 2.2 %collective-permute-start.8 = (bf16[128,2048]{1,0:T(8,128)(2,1)S(1)}, bf16[128,2048]{1,0:T(8,128)(2,1)S(1)}, u32[]{:S(2)}, u32[]{:S(2)}) collective-permute-start(bf16[128,2048]{1,0:T(8,128)(2,1)S(1)} %bitcast.57), channel_id=1, source_target_pairs={{0,3},{1,0},{2,1},{3,2},{4,7},{5,4},{6,5},{7,6},{8,11},{9,8},{10,9... | collective-permute-start | bytes 1572872 | tf_op jit(solution)/shard_map/ppermute | solution.py:25
  72.8 2.0 %shard_map.105.refs_4_.refs_3_ = bf16[2048,896]{1,0:T(8,128)(2,1)S(1)} custom-call(bf16[2048,896]{1,0:T(8,128)(2,1)} %collective-permute-done.9.slice_ref), custom_call_target="tpu_custom_call" | custom-call | flops 1000000 | bytes 7340032 | tf_op jit(solution)/shard_map/pallas_call | solution.py:119
  74.9 2.2 %shard_map.108.other_ref.refs_5_.refs_3_ = bf16[896,2048]{1,0:T(8,128)(2,1)S(1)} custom-call(bf16[896,2048]{1,0:T(8,128)(2,1)} %collective-permute-done.12.slice_ref), custom_call_target="tpu_custom_call" | custom-call | flops 1000000 | bytes 7340032 | tf_op jit(solution)/shard_map/pallas_call | solution.py:119
  77.1 6.0 %collective-permute-done.16.refs_1_ = bf16[128,2048]{1,0:T(8,128)(2,1)S(1)} collective-permute-done((bf16[128,2048]{1,0:T(8,128)(2,1)}, bf16[128,2048]{1,0:T(8,128)(2,1)S(1)}, u32[]{:S(2)}, u32[]{:S(2)}) %collective-permute-start.16) | collective-permute-done | bytes 524320 | tf_op jit(solution)/shard_map/ppermute | solution.py:25
  83.1 3.3 %shard_map.110 = (bf16[128,1792]{1,0:T(8,128)(2,1)S(1)}, bf16[128,1792]{1,0:T(8,128)(2,1)S(1)}) custom-call(bf16[128,2048]{1,0:T(8,128)(2,1)S(1)} %collective-permute-done.15.refs_0_, bf16[128,2048]{1,0:T(8,128)(2,1)S(1)} %collective-permute-done.16.refs_1_, bf16[2048,896]{1,0:T(8,128)(2,1)S(1)} %bitcast.48, bf16[2048,896]{1,0:T(8,128)(2,1)S(1)} %shard_map.105.refs_4_.refs_3_), custom_call_target="tpu_custom_call" | custom-call | flops 1879048192 | bytes 8388608 | tf_op jit(solution)/shard_map/pallas_call | solution.py:167
  86.5 1.1 shard_map.114
  87.7 3.2 %collective-permute-start.20 = (bf16[128,1024]{1,0:T(8,128)(2,1)S(1)}, bf16[128,1024]{1,0:T(8,128)(2,1)S(1)}, u32[]{:S(2)}, u32[]{:S(2)}) collective-permute-start(bf16[128,1024]{1,0:T(8,128)(2,1)S(1)} %get-tuple-element.66), channel_id=1, source_target_pairs={{0,1},{1,2},{2,3},{3,0},{4,5},{5,6},{6,7},{7,4},{8,9},{9,10},{10,1... | collective-permute-start | bytes 786440 | tf_op jit(solution)/shard_map/ppermute | solution.py:25
  90.9 2.8 %collective-permute-done.10.refs_1_ = bf16[128,2048]{1,0:T(8,128)(2,1)} collective-permute-done((bf16[128,2048]{1,0:T(8,128)(2,1)S(1)}, bf16[128,2048]{1,0:T(8,128)(2,1)}, u32[]{:S(2)}, u32[]{:S(2)}) %collective-permute-start.10) | collective-permute-done | bytes 524320 | tf_op jit(solution)/shard_map/ppermute | solution.py:25
  93.7 5.5 %shard_map.107 = (bf16[128,1792]{1,0:T(8,128)(2,1)S(1)}, bf16[128,1792]{1,0:T(8,128)(2,1)S(1)}, bf16[128,1792]{1,0:T(8,128)(2,1)S(1)}) custom-call(bf16[128,2048]{1,0:T(8,128)(2,1)S(1)} %shard_map.104.refs_0_, bf16[128,2048]{1,0:T(8,128)(2,1)} %collective-permute-done.10.refs_1_, bf16[128,2048]{1,0:T(8,128)(2,1)} %collective-permute-done.11.refs_2_, ...), custom_call_target="tpu_custom_call" | custom-call | flops 2818572288 | bytes 8912896 | tf_op jit(solution)/shard_map/pallas_call | solution.py:167
  99.2 0.8 copy-done.7
  100.0 4.3 %shard_map.106 = (bf16[128,1792]{1,0:T(8,128)(2,1)S(1)}, bf16[128,1792]{1,0:T(8,128)(2,1)S(1)}, bf16[128,1792]{1,0:T(8,128)(2,1)S(1)}) custom-call(bf16[128,2048]{1,0:T(8,128)(2,1)S(1)} %bitcast.58, bf16[128,2048]{1,0:T(8,128)(2,1)S(1)} %collective-permute-done.7.refs_1_, bf16[128,2048]{1,0:T(8,128)(2,1)S(1)} %collective-permute-done.8.refs_2_, ...), custom_call_target="tpu_custom_call" | custom-call | flops 2818572288 | bytes 8912896 | tf_op jit(solution)/shard_map/pallas_call | solution.py:167
  104.3 3.0 %shard_map.109 = (bf16[2,128,1024]{2,1,0:T(8,128)(2,1)}, bf16[2,128,1024]{2,1,0:T(8,128)(2,1)}) custom-call(bf16[128,1792]{1,0:T(8,128)(2,1)S(1)} %get-tuple-element.55.refs_0_, bf16[128,1792]{1,0:T(8,128)(2,1)S(1)} %get-tuple-element.56.refs_1_, bf16[128,1792]{1,0:T(8,128)(2,1)S(1)} %get-tuple-element.57.refs_2_, ...), custom_call_target="tpu_custom_call" | custom-call | flops 1879048192 | bytes 4718592 | tf_op jit(solution)/shard_map/pallas_call | solution.py:306
  107.3 3.8 %collective-permute-start.13 = (bf16[2,128,1024]{2,1,0:T(8,128)(2,1)}, bf16[2,128,1024]{2,1,0:T(8,128)(2,1)}, u32[]{:S(2)}, u32[]{:S(2)}) collective-permute-start(bf16[2,128,1024]{2,1,0:T(8,128)(2,1)} %get-tuple-element.59), channel_id=1, source_target_pairs={{0,1},{1,2},{2,3},{3,0},{4,5},{5,6},{6,7},{7,4},{8,9},{9,10},{10,1... | collective-permute-start | bytes 1572872 | tf_op jit(solution)/shard_map/ppermute | solution.py:25
  111.1 1.1 shard_map.111
  112.2 1.5 collective-permute-start.17
  113.8 3.0 %shard_map.115 = (bf16[2,128,1024]{2,1,0:T(8,128)(2,1)}, bf16[2,128,1024]{2,1,0:T(8,128)(2,1)}) custom-call(bf16[128,1792]{1,0:T(8,128)(2,1)S(1)} %get-tuple-element.55.refs_0_, bf16[128,1792]{1,0:T(8,128)(2,1)S(1)} %get-tuple-element.56.refs_1_, bf16[128,1792]{1,0:T(8,128)(2,1)S(1)} %get-tuple-element.57.refs_2_, ...), custom_call_target="tpu_custom_call" | custom-call | flops 1879048192 | bytes 4718592 | tf_op jit(solution)/shard_map/pallas_call | solution.py:306
  116.8 1.8 collective-permute-start.21
  118.6 0.8 collective-permute-start.22
  119.7 2.0 %copy-done.2 = bf16[896,2048]{1,0:T(8,128)(2,1)S(1)} copy-done((bf16[896,2048]{1,0:T(8,128)(2,1)S(1)}, bf16[896,2048]{1,0:T(8,128)(2,1)}, u32[]{:S(2)}) %copy-start.2) | copy-done | bytes 3670040
  121.7 2.0 %copy-done.4 = bf16[1,896,2048]{2,1,0:T(8,128)(2,1)S(1)} copy-done((bf16[1,896,2048]{2,1,0:T(8,128)(2,1)S(1)}, bf16[1,896,2048]{2,1,0:T(8,128)(2,1)}, u32[]{:S(2)}) %copy-start.4) | copy-done | bytes 3670040
  123.7 1.0 copy-done.8
  124.8 1.0 copy-done.10
  125.8 2.1 %down_own.1 = (f32[2,128,1024]{2,1,0:T(8,128)S(1)}, f32[2,128,1024]{2,1,0:T(8,128)S(1)}) custom-call(bf16[128,1792]{1,0:T(8,128)(2,1)S(1)} %copy-done.10, bf16[128,1792]{1,0:T(8,128)(2,1)S(1)} %copy-done.8, bf16[896,2048]{1,0:T(8,128)(2,1)S(1)} %bitcast.46, bf16[896,2048]{1,0:T(8,128)(2,1)S(1)} %copy-done.2), custom_call_target="tpu_custom_call" | custom-call | flops 1879048192 | bytes 9437184 | tf_op jit(solution)/shard_map/down_own/pallas_call | solution.py:223
  127.8 6.8 %collective-permute-done.13.refs_0_ = bf16[2,128,1024]{2,1,0:T(8,128)(2,1)} collective-permute-done((bf16[2,128,1024]{2,1,0:T(8,128)(2,1)}, bf16[2,128,1024]{2,1,0:T(8,128)(2,1)}, u32[]{:S(2)}, u32[]{:S(2)}) %collective-permute-start.13) | collective-permute-done | bytes 524320 | tf_op jit(solution)/shard_map/ppermute | solution.py:25
  134.7 4.0 %collective-permute-done.14.refs_1_ = bf16[2,128,1024]{2,1,0:T(8,128)(2,1)} collective-permute-done((bf16[2,128,1024]{2,1,0:T(8,128)(2,1)}, bf16[2,128,1024]{2,1,0:T(8,128)(2,1)}, u32[]{:S(2)}, u32[]{:S(2)}) %collective-permute-start.14) | collective-permute-done | bytes 524320 | tf_op jit(solution)/shard_map/ppermute | solution.py:25
  138.6 2.4 %shard_map.112 = bf16[8,2,16,1024]{3,2,1,0:T(8,128)(2,1)} custom-call(f32[2,128,1024]{2,1,0:T(8,128)S(1)} %get-tuple-element.54.own_ref, bf16[2,128,1024]{2,1,0:T(8,128)(2,1)} %collective-permute-done.13.refs_0_, bf16[2,128,1024]{2,1,0:T(8,128)(2,1)} %collective-permute-done.14.refs_1_, bf16[2,128,1024]{2,1,0:T(8,128)(2,1)} %collective-permute-done.17.refs_2_), custom_call_target="tpu_custom_call" | custom-call | flops 1048576 | bytes 3145728 | tf_op jit(solution)/shard_map/pallas_call | solution.py:284
  141.0 6.8 %all-to-all-start.2 = ((bf16[8,2,16,1024]{3,2,1,0:T(8,128)(2,1)}), bf16[8,2,16,1024]{3,2,1,0:T(8,128)(2,1)S(1)}, u32[]{:S(2)}, u32[]{:S(2)}) async-start(bf16[8,2,16,1024]{3,2,1,0:T(8,128)(2,1)} %shard_map.112), calls=%async_computation.2 | async-start | bytes 1048576 | tf_op jit(solution)/shard_map/all_to_all | solution.py:29
  148.0 3.2 %gather_fusion.2 = bf16[8,2,16,2048]{3,2,1,0:T(8,128)(2,1)} fusion(bf16[16,2,16,2048]{3,2,1,0:T(8,128)(2,1)} %all-to-all-done, s32[1024]{0:T(1024)S(1)} %pad_clamp_fusion), kind=kCustom, calls=%fused_computation.2 | custom fusion | bytes 2097184 | tf_op jit(solution)/shard_map/gather | solution.py:439
  151.5 2.1 %collective-permute-start.23 = (bf16[32,1024]{1,0:T(8,128)(2,1)S(1)}, bf16[32,1024]{1,0:T(8,128)(2,1)S(1)}, u32[]{:S(2)}, u32[]{:S(2)}) collective-permute-start(bf16[32,1024]{1,0:T(8,128)(2,1)S(1)} %get-tuple-element.70), channel_id=1, source_target_pairs={{0,8},{8,16},{16,24},{24,32},{32,40},{40,48},{48,56},{56,0},{1,9},... | collective-permute-start | bytes 196616 | tf_op jit(solution)/shard_map/ppermute | solution.py:25
  153.6 2.4 %collective-permute-start.24 = (bf16[32,1024]{1,0:T(8,128)(2,1)S(1)}, bf16[32,1024]{1,0:T(8,128)(2,1)S(1)}, u32[]{:S(2)}, u32[]{:S(2)}) collective-permute-start(bf16[32,1024]{1,0:T(8,128)(2,1)S(1)} %get-tuple-element.71), channel_id=1, source_target_pairs={{0,16},{8,24},{16,32},{24,40},{32,48},{40,56},{48,0},{56,8},{1,17}... | collective-permute-start | bytes 196616 | tf_op jit(solution)/shard_map/ppermute | solution.py:25
  155.9 1.3 fusion.13
  157.2 2.8 %collective-permute-start.25 = (bf16[32,1024]{1,0:T(8,128)(2,1)S(1)}, bf16[32,1024]{1,0:T(8,128)(2,1)S(1)}, u32[]{:S(2)}, u32[]{:S(2)}) collective-permute-start(bf16[32,1024]{1,0:T(8,128)(2,1)S(1)} %get-tuple-element.72), channel_id=1, source_target_pairs={{0,24},{8,32},{16,40},{24,48},{32,56},{40,0},{48,8},{56,16},{1,25}... | collective-permute-start | bytes 196616 | tf_op jit(solution)/shard_map/ppermute | solution.py:25
  159.9 2.4 %collective-permute-start.26 = (bf16[32,1024]{1,0:T(8,128)(2,1)S(1)}, bf16[32,1024]{1,0:T(8,128)(2,1)S(1)}, u32[]{:S(2)}, u32[]{:S(2)}) collective-permute-start(bf16[32,1024]{1,0:T(8,128)(2,1)S(1)} %get-tuple-element.73), channel_id=1, source_target_pairs={{0,32},{8,40},{16,48},{24,56},{32,0},{40,8},{48,16},{56,24},{1,33}... | collective-permute-start | bytes 196616 | tf_op jit(solution)/shard_map/ppermute | solution.py:25
  162.3 2.7 %collective-permute-start.27 = (bf16[32,1024]{1,0:T(8,128)(2,1)S(1)}, bf16[32,1024]{1,0:T(8,128)(2,1)S(1)}, u32[]{:S(2)}, u32[]{:S(2)}) collective-permute-start(bf16[32,1024]{1,0:T(8,128)(2,1)S(1)} %get-tuple-element.74), channel_id=1, source_target_pairs={{0,40},{8,48},{16,56},{24,0},{32,8},{40,16},{48,24},{56,32},{1,41}... | collective-permute-start | bytes 196616 | tf_op jit(solution)/shard_map/ppermute | solution.py:25
  165.0 3.6 %collective-permute-start.28 = (bf16[32,1024]{1,0:T(8,128)(2,1)S(1)}, bf16[32,1024]{1,0:T(8,128)(2,1)S(1)}, u32[]{:S(2)}, u32[]{:S(2)}) collective-permute-start(bf16[32,1024]{1,0:T(8,128)(2,1)S(1)} %get-tuple-element.75), channel_id=1, source_target_pairs={{0,48},{8,56},{16,0},{24,8},{32,16},{40,24},{48,32},{56,40},{1,49}... | collective-permute-start | bytes 196616 | tf_op jit(solution)/shard_map/ppermute | solution.py:25
  168.6 1.5 collective-permute-start.29
  170.1 2.3 %collective-permute-done.28.refs_6_ = bf16[32,1024]{1,0:T(8,128)(2,1)S(1)} collective-permute-done((bf16[32,1024]{1,0:T(8,128)(2,1)S(1)}, bf16[32,1024]{1,0:T(8,128)(2,1)S(1)}, u32[]{:S(2)}, u32[]{:S(2)}) %collective-permute-start.28) | collective-permute-done | bytes 65568 | tf_op jit(solution)/shard_map/ppermute | solution.py:25
  172.3 0.7 collective-permute-done.29.refs_7_
  173.5 3.5 %collective-permute-start.30 = (bf16[128,1024]{1,0:T(8,128)(2,1)S(1)}, bf16[128,1024]{1,0:T(8,128)(2,1)S(1)}, u32[]{:S(2)}, u32[]{:S(2)}) collective-permute-start(bf16[128,1024]{1,0:T(8,128)(2,1)S(1)} %get-tuple-element.77), channel_id=1, source_target_pairs={{0,64},{64,128},{128,192},{1,65},{65,129},{129,193},{2,66},{66,130... | collective-permute-start | bytes 786440 | tf_op jit(solution)/shard_map/ppermute | solution.py:456
  177.5 3.2 %collective-permute-start.18 = (bf16[128,1024]{1,0:T(8,128)(2,1)S(1)}, bf16[128,1024]{1,0:T(8,128)(2,1)S(1)}, u32[]{:S(2)}, u32[]{:S(2)}) collective-permute-start(bf16[128,1024]{1,0:T(8,128)(2,1)S(1)} %get-tuple-element.63), channel_id=1, source_target_pairs={{0,64},{64,128},{128,192},{1,65},{65,129},{129,193},{2,66},{66,130... | collective-permute-start | bytes 786440 | tf_op jit(solution)/shard_map/ppermute | solution.py:456
  180.7 0.8 maximum_bitcast_fusion
  181.8 4.0 %collective-permute-done.18 = bf16[128,1024]{1,0:T(8,128)(2,1)S(1)} collective-permute-done((bf16[128,1024]{1,0:T(8,128)(2,1)S(1)}, bf16[128,1024]{1,0:T(8,128)(2,1)S(1)}, u32[]{:S(2)}, u32[]{:S(2)}) %collective-permute-start.18) | collective-permute-done | bytes 262176 | tf_op jit(solution)/shard_map/ppermute | solution.py:456
  185.7 0.9 fusion
  (72 shorter events, 3.5 us)
Async XLA Ops:
  0.6 32.9 %copy-start = (bf16[1,128,2048]{2,1,0:T(8,128)(2,1)S(1)}, bf16[1,128,2048]{2,1,0:T(8,128)(2,1)}, u32[]{:S(2)}) copy-start(bf16[1,128,2048]{2,1,0:T(8,128)(2,1)} %param.10) | copy-start | bytes 1572868
  0.6 70.0 %collective-permute-start.9 = (bf16[2048,896]{1,0:T(8,128)(2,1)}, bf16[2048,896]{1,0:T(8,128)(2,1)}, u32[]{:S(2)}, u32[]{:S(2)}) collective-permute-start(bf16[2048,896]{1,0:T(8,128)(2,1)} %bitcast.47), channel_id=1, source_target_pairs={{0,4},{4,0},{1,5},{5,1},{2,6},{6,2},{3,7},{7,3},{8,12},{12,8},{9,1... | collective-permute-start | bytes 11010056 | tf_op jit(solution)/shard_map/ppermute | solution.py:25
  0.7 74.1 %collective-permute-start.12 = (bf16[896,2048]{1,0:T(8,128)(2,1)}, bf16[896,2048]{1,0:T(8,128)(2,1)}, u32[]{:S(2)}, u32[]{:S(2)}) collective-permute-start(bf16[896,2048]{1,0:T(8,128)(2,1)} %bitcast.41), channel_id=1, source_target_pairs={{0,4},{4,0},{1,5},{5,1},{2,6},{6,2},{3,7},{7,3},{8,12},{12,8},{9,1... | collective-permute-start | bytes 11010056 | tf_op jit(solution)/shard_map/ppermute | solution.py:25
  1.2 1.0 copy-start.6
  2.3 0.7 copy-start.11
  4.2 42.8 %all-to-all-start.1 = ((bf16[8,16,2048]{2,1,0:T(8,128)(2,1)}), bf16[8,16,2048]{2,1,0:T(8,128)(2,1)S(1)}, u32[]{:S(2)}, u32[]{:S(2)}) async-start(bf16[8,16,2048]{2,1,0:T(8,128)(2,1)} %bitcast.16), calls=%async_computation.1 | async-start | bytes 1048576 | tf_op jit(solution)/shard_map/all_to_all | solution.py:29
  12.7 18.1 %collective-permute-start = (bf16[16,2048]{1,0:T(8,128)(2,1)S(1)}, bf16[16,2048]{1,0:T(8,128)(2,1)S(1)}, u32[]{:S(2)}, u32[]{:S(2)}) collective-permute-start(bf16[16,2048]{1,0:T(8,128)(2,1)S(1)} %get-tuple-element.42), channel_id=1, source_target_pairs={{0,8},{8,16},{16,24},{24,32},{32,40},{40,48},{48,56},{56,0},{1,9},... | collective-permute-start | bytes 196616 | tf_op jit(solution)/shard_map/ppermute | solution.py:25
  14.7 22.2 %collective-permute-start.1 = (bf16[16,2048]{1,0:T(8,128)(2,1)S(1)}, bf16[16,2048]{1,0:T(8,128)(2,1)S(1)}, u32[]{:S(2)}, u32[]{:S(2)}) collective-permute-start(bf16[16,2048]{1,0:T(8,128)(2,1)S(1)} %get-tuple-element.43), channel_id=1, source_target_pairs={{0,16},{8,24},{16,32},{24,40},{32,48},{40,56},{48,0},{56,8},{1,17}... | collective-permute-start | bytes 196616 | tf_op jit(solution)/shard_map/ppermute | solution.py:25
  17.1 20.2 %collective-permute-start.2 = (bf16[16,2048]{1,0:T(8,128)(2,1)S(1)}, bf16[16,2048]{1,0:T(8,128)(2,1)S(1)}, u32[]{:S(2)}, u32[]{:S(2)}) collective-permute-start(bf16[16,2048]{1,0:T(8,128)(2,1)S(1)} %get-tuple-element.44), channel_id=1, source_target_pairs={{0,24},{8,32},{16,40},{24,48},{32,56},{40,0},{48,8},{56,16},{1,25}... | collective-permute-start | bytes 196616 | tf_op jit(solution)/shard_map/ppermute | solution.py:25
  30.8 11.6 %collective-permute-start.3 = (bf16[16,2048]{1,0:T(8,128)(2,1)S(1)}, bf16[16,2048]{1,0:T(8,128)(2,1)S(1)}, u32[]{:S(2)}, u32[]{:S(2)}) collective-permute-start(bf16[16,2048]{1,0:T(8,128)(2,1)S(1)} %get-tuple-element.45), channel_id=1, source_target_pairs={{0,32},{8,40},{16,48},{24,56},{32,0},{40,8},{48,16},{56,24},{1,33}... | collective-permute-start | bytes 196616 | tf_op jit(solution)/shard_map/ppermute | solution.py:25
  36.9 8.2 %collective-permute-start.4 = (bf16[16,2048]{1,0:T(8,128)(2,1)S(1)}, bf16[16,2048]{1,0:T(8,128)(2,1)S(1)}, u32[]{:S(2)}, u32[]{:S(2)}) collective-permute-start(bf16[16,2048]{1,0:T(8,128)(2,1)S(1)} %get-tuple-element.46), channel_id=1, source_target_pairs={{0,40},{8,48},{16,56},{24,0},{32,8},{40,16},{48,24},{56,32},{1,41}... | collective-permute-start | bytes 196616 | tf_op jit(solution)/shard_map/ppermute | solution.py:25
  37.3 8.2 %collective-permute-start.5 = (bf16[16,2048]{1,0:T(8,128)(2,1)S(1)}, bf16[16,2048]{1,0:T(8,128)(2,1)S(1)}, u32[]{:S(2)}, u32[]{:S(2)}) collective-permute-start(bf16[16,2048]{1,0:T(8,128)(2,1)S(1)} %get-tuple-element.47), channel_id=1, source_target_pairs={{0,48},{8,56},{16,0},{24,8},{32,16},{40,24},{48,32},{56,40},{1,49}... | collective-permute-start | bytes 196616 | tf_op jit(solution)/shard_map/ppermute | solution.py:25
  42.3 4.6 %collective-permute-start.6 = (bf16[16,2048]{1,0:T(8,128)(2,1)S(1)}, bf16[16,2048]{1,0:T(8,128)(2,1)S(1)}, u32[]{:S(2)}, u32[]{:S(2)}) collective-permute-start(bf16[16,2048]{1,0:T(8,128)(2,1)S(1)} %get-tuple-element.48), channel_id=1, source_target_pairs={{0,56},{8,0},{16,8},{24,16},{32,24},{40,32},{48,40},{56,48},{1,57}... | collective-permute-start | bytes 196616 | tf_op jit(solution)/shard_map/ppermute | solution.py:25
  45.1 25.2 %copy-start.12 = (s32[512]{0:T(512)S(1)}, s32[512]{0:T(512)}, u32[]{:S(2)}) copy-start(s32[512]{0:T(512)} %param.17) | copy-start | bytes 6148
  45.1 25.4 %copy-start.14 = (s32[8]{0:T(128)S(1)}, s32[8]{0:T(128)}, u32[]{:S(2)}) copy-start(s32[8]{0:T(128)} %param.16) | copy-start | bytes 100
  47.0 94.0 %all-to-all-start = ((bf16[16,2,16,2048]{3,2,1,0:T(8,128)(2,1)}), bf16[16,2,16,2048]{3,2,1,0:T(8,128)(2,1)}, u32[]{:S(2)}, u32[]{:S(2)}) async-start(bf16[16,2,16,2048]{3,2,1,0:T(8,128)(2,1)} %pad_maximum_fusion), calls=%async_computation | async-start | bytes 4194304 | tf_op jit(solution)/shard_map/all_to_all | solution.py:438
  51.5 15.4 %collective-permute-start.11 = (bf16[128,2048]{1,0:T(8,128)(2,1)S(1)}, bf16[128,2048]{1,0:T(8,128)(2,1)}, u32[]{:S(2)}, u32[]{:S(2)}) collective-permute-start(bf16[128,2048]{1,0:T(8,128)(2,1)S(1)} %shard_map.104.refs_0_), channel_id=1, source_target_pairs={{0,3},{1,0},{2,1},{3,2},{4,7},{5,4},{6,5},{7,6},{8,11},{9,8},{10,9... | collective-permute-start | bytes 1572872 | tf_op jit(solution)/shard_map/ppermute | solution.py:25
  52.4 14.5 %collective-permute-start.7 = (bf16[128,2048]{1,0:T(8,128)(2,1)S(1)}, bf16[128,2048]{1,0:T(8,128)(2,1)S(1)}, u32[]{:S(2)}, u32[]{:S(2)}) collective-permute-start(bf16[128,2048]{1,0:T(8,128)(2,1)S(1)} %bitcast.56), channel_id=1, source_target_pairs={{0,1},{1,2},{2,3},{3,0},{4,5},{5,6},{6,7},{7,4},{8,9},{9,10},{10,1... | collective-permute-start | bytes 1572872 | tf_op jit(solution)/shard_map/ppermute | solution.py:25
  66.9 16.2 %collective-permute-start.16 = (bf16[128,2048]{1,0:T(8,128)(2,1)}, bf16[128,2048]{1,0:T(8,128)(2,1)S(1)}, u32[]{:S(2)}, u32[]{:S(2)}) collective-permute-start(bf16[128,2048]{1,0:T(8,128)(2,1)} %collective-permute-done.11.refs_2_), channel_id=1, source_target_pairs={{0,3},{1,0},{2,1},{3,2},{4,7},{5,4},{6,5},{7,6},{8,11},{9,8},{10,9... | collective-permute-start | bytes 1572872 | tf_op jit(solution)/shard_map/ppermute | solution.py:25
  66.9 16.2 %collective-permute-start.15 = (bf16[128,2048]{1,0:T(8,128)(2,1)S(1)}, bf16[128,2048]{1,0:T(8,128)(2,1)S(1)}, u32[]{:S(2)}, u32[]{:S(2)}) collective-permute-start(bf16[128,2048]{1,0:T(8,128)(2,1)S(1)} %collective-permute-done.7.refs_1_), channel_id=1, source_target_pairs={{0,1},{1,2},{2,3},{3,0},{4,5},{5,6},{6,7},{7,4},{8,9},{9,10},{10,1... | collective-permute-start | bytes 1572872 | tf_op jit(solution)/shard_map/ppermute | solution.py:25
  70.2 23.5 %collective-permute-start.10 = (bf16[128,2048]{1,0:T(8,128)(2,1)S(1)}, bf16[128,2048]{1,0:T(8,128)(2,1)}, u32[]{:S(2)}, u32[]{:S(2)}) collective-permute-start(bf16[128,2048]{1,0:T(8,128)(2,1)S(1)} %shard_map.104.refs_0_), channel_id=1, source_target_pairs={{0,1},{1,2},{2,3},{3,0},{4,5},{5,6},{6,7},{7,4},{8,9},{9,10},{10,1... | collective-permute-start | bytes 1572872 | tf_op jit(solution)/shard_map/ppermute | solution.py:25
  70.6 29.4 %collective-permute-start.8 = (bf16[128,2048]{1,0:T(8,128)(2,1)S(1)}, bf16[128,2048]{1,0:T(8,128)(2,1)S(1)}, u32[]{:S(2)}, u32[]{:S(2)}) collective-permute-start(bf16[128,2048]{1,0:T(8,128)(2,1)S(1)} %bitcast.57), channel_id=1, source_target_pairs={{0,3},{1,0},{2,1},{3,2},{4,7},{5,4},{6,5},{7,6},{8,11},{9,8},{10,9... | collective-permute-start | bytes 1572872 | tf_op jit(solution)/shard_map/ppermute | solution.py:25
  74.9 8.3 %copy-start.5 = (bf16[1,2048,896]{2,1,0:T(8,128)(2,1)S(1)}, bf16[1,2048,896]{2,1,0:T(8,128)(2,1)}, u32[]{:S(2)}) copy-start(bf16[1,2048,896]{2,1,0:T(8,128)(2,1)} %param.12) | copy-start | bytes 11010052
  77.1 36.7 %copy-start.1 = (bf16[896,2048]{1,0:T(8,128)(2,1)}, bf16[896,2048]{1,0:T(8,128)(2,1)S(1)}, u32[]{:S(2)}) copy-start(bf16[896,2048]{1,0:T(8,128)(2,1)S(1)} %shard_map.108.other_ref.refs_5_.refs_3_) | copy-start | bytes 11010052
  77.1 9.4 %copy-start.3 = (bf16[1,896,2048]{2,1,0:T(8,128)(2,1)S(1)}, bf16[1,896,2048]{2,1,0:T(8,128)(2,1)}, u32[]{:S(2)}) copy-start(bf16[1,896,2048]{2,1,0:T(8,128)(2,1)} %param.13) | copy-start | bytes 11010052
  87.6 26.2 %collective-permute-start.19 = (bf16[128,1024]{1,0:T(8,128)(2,1)S(1)}, bf16[128,1024]{1,0:T(8,128)(2,1)S(1)}, u32[]{:S(2)}, u32[]{:S(2)}) collective-permute-start(bf16[128,1024]{1,0:T(8,128)(2,1)S(1)} %get-tuple-element.65), channel_id=1, source_target_pairs={{0,3},{1,0},{2,1},{3,2},{4,7},{5,4},{6,5},{7,6},{8,11},{9,8},{10,9... | collective-permute-start | bytes 786440 | tf_op jit(solution)/shard_map/ppermute | solution.py:25
  87.7 26.1 %collective-permute-start.20 = (bf16[128,1024]{1,0:T(8,128)(2,1)S(1)}, bf16[128,1024]{1,0:T(8,128)(2,1)S(1)}, u32[]{:S(2)}, u32[]{:S(2)}) collective-permute-start(bf16[128,1024]{1,0:T(8,128)(2,1)S(1)} %get-tuple-element.66), channel_id=1, source_target_pairs={{0,1},{1,2},{2,3},{3,0},{4,5},{5,6},{6,7},{7,4},{8,9},{9,10},{10,1... | collective-permute-start | bytes 786440 | tf_op jit(solution)/shard_map/ppermute | solution.py:25
  99.2 0.8 copy-start.7
  104.3 3.0 %copy-start.9 = (bf16[128,1792]{1,0:T(8,128)(2,1)}, bf16[128,1792]{1,0:T(8,128)(2,1)S(1)}, u32[]{:S(2)}) copy-start(bf16[128,1792]{1,0:T(8,128)(2,1)S(1)} %get-tuple-element.52.first_ref) | copy-start | bytes 1376260
  107.3 27.3 %collective-permute-start.13 = (bf16[2,128,1024]{2,1,0:T(8,128)(2,1)}, bf16[2,128,1024]{2,1,0:T(8,128)(2,1)}, u32[]{:S(2)}, u32[]{:S(2)}) collective-permute-start(bf16[2,128,1024]{2,1,0:T(8,128)(2,1)} %get-tuple-element.59), channel_id=1, source_target_pairs={{0,1},{1,2},{2,3},{3,0},{4,5},{5,6},{6,7},{7,4},{8,9},{9,10},{10,1... | collective-permute-start | bytes 1572872 | tf_op jit(solution)/shard_map/ppermute | solution.py:25
  111.1 27.5 %collective-permute-start.14 = (bf16[2,128,1024]{2,1,0:T(8,128)(2,1)}, bf16[2,128,1024]{2,1,0:T(8,128)(2,1)}, u32[]{:S(2)}, u32[]{:S(2)}) collective-permute-start(bf16[2,128,1024]{2,1,0:T(8,128)(2,1)} %get-tuple-element.60), channel_id=1, source_target_pairs={{0,3},{1,0},{2,1},{3,2},{4,7},{5,4},{6,5},{7,6},{8,11},{9,8},{10,9... | collective-permute-start | bytes 1572872 | tf_op jit(solution)/shard_map/ppermute | solution.py:25
  112.2 7.2 %copy-start.13 = (s32[1,128,2]{1,2,0:T(2,128)S(1)}, s32[1,128,2]{1,2,0:T(2,128)}, u32[]{:S(2)}) copy-start(s32[1,128,2]{1,2,0:T(2,128)} %param.15) | copy-start | bytes 3076
  112.2 26.4 %collective-permute-start.17 = (bf16[2,128,1024]{2,1,0:T(8,128)(2,1)S(1)}, bf16[2,128,1024]{2,1,0:T(8,128)(2,1)}, u32[]{:S(2)}, u32[]{:S(2)}) collective-permute-start(bf16[2,128,1024]{2,1,0:T(8,128)(2,1)S(1)} %shard_map.111), channel_id=1, source_target_pairs={{0,2},{1,3},{2,0},{3,1},{4,6},{5,7},{6,4},{7,5},{8,10},{9,11},{10,... | collective-permute-start | bytes 1572872 | tf_op jit(solution)/shard_map/ppermute | solution.py:25
  116.8 34.4 %collective-permute-start.21 = (bf16[2,128,1024]{2,1,0:T(8,128)(2,1)}, bf16[2,128,1024]{2,1,0:T(8,128)(2,1)S(1)}, u32[]{:S(2)}, u32[]{:S(2)}) collective-permute-start(bf16[2,128,1024]{2,1,0:T(8,128)(2,1)} %get-tuple-element.67), channel_id=1, source_target_pairs={{0,1},{1,2},{2,3},{3,0},{4,5},{5,6},{6,7},{7,4},{8,9},{9,10},{10,1... | collective-permute-start | bytes 1572872 | tf_op jit(solution)/shard_map/ppermute | solution.py:25
  118.6 32.6 %collective-permute-start.22 = (bf16[2,128,1024]{2,1,0:T(8,128)(2,1)}, bf16[2,128,1024]{2,1,0:T(8,128)(2,1)S(1)}, u32[]{:S(2)}, u32[]{:S(2)}) collective-permute-start(bf16[2,128,1024]{2,1,0:T(8,128)(2,1)} %get-tuple-element.68), channel_id=1, source_target_pairs={{0,3},{1,0},{2,1},{3,2},{4,7},{5,4},{6,5},{7,6},{8,11},{9,8},{10,9... | collective-permute-start | bytes 1572872 | tf_op jit(solution)/shard_map/ppermute | solution.py:25
  119.7 2.0 %copy-start.2 = (bf16[896,2048]{1,0:T(8,128)(2,1)S(1)}, bf16[896,2048]{1,0:T(8,128)(2,1)}, u32[]{:S(2)}) copy-start(bf16[896,2048]{1,0:T(8,128)(2,1)} %copy-done.1) | copy-start | bytes 11010052
  121.7 2.0 %copy-start.4 = (bf16[1,896,2048]{2,1,0:T(8,128)(2,1)S(1)}, bf16[1,896,2048]{2,1,0:T(8,128)(2,1)}, u32[]{:S(2)}) copy-start(bf16[1,896,2048]{2,1,0:T(8,128)(2,1)} %param.13) | copy-start | bytes 11010052
  123.7 1.0 copy-start.8
  124.8 1.0 copy-start.10
  141.0 36.0 %all-to-all-start.2 = ((bf16[8,2,16,1024]{3,2,1,0:T(8,128)(2,1)}), bf16[8,2,16,1024]{3,2,1,0:T(8,128)(2,1)S(1)}, u32[]{:S(2)}, u32[]{:S(2)}) async-start(bf16[8,2,16,1024]{3,2,1,0:T(8,128)(2,1)} %shard_map.112), calls=%async_computation.2 | async-start | bytes 1048576 | tf_op jit(solution)/shard_map/all_to_all | solution.py:29
  151.5 13.5 %collective-permute-start.23 = (bf16[32,1024]{1,0:T(8,128)(2,1)S(1)}, bf16[32,1024]{1,0:T(8,128)(2,1)S(1)}, u32[]{:S(2)}, u32[]{:S(2)}) collective-permute-start(bf16[32,1024]{1,0:T(8,128)(2,1)S(1)} %get-tuple-element.70), channel_id=1, source_target_pairs={{0,8},{8,16},{16,24},{24,32},{32,40},{40,48},{48,56},{56,0},{1,9},... | collective-permute-start | bytes 196616 | tf_op jit(solution)/shard_map/ppermute | solution.py:25
  153.6 15.0 %collective-permute-start.24 = (bf16[32,1024]{1,0:T(8,128)(2,1)S(1)}, bf16[32,1024]{1,0:T(8,128)(2,1)S(1)}, u32[]{:S(2)}, u32[]{:S(2)}) collective-permute-start(bf16[32,1024]{1,0:T(8,128)(2,1)S(1)} %get-tuple-element.71), channel_id=1, source_target_pairs={{0,16},{8,24},{16,32},{24,40},{32,48},{40,56},{48,0},{56,8},{1,17}... | collective-permute-start | bytes 196616 | tf_op jit(solution)/shard_map/ppermute | solution.py:25
  157.2 12.9 %collective-permute-start.25 = (bf16[32,1024]{1,0:T(8,128)(2,1)S(1)}, bf16[32,1024]{1,0:T(8,128)(2,1)S(1)}, u32[]{:S(2)}, u32[]{:S(2)}) collective-permute-start(bf16[32,1024]{1,0:T(8,128)(2,1)S(1)} %get-tuple-element.72), channel_id=1, source_target_pairs={{0,24},{8,32},{16,40},{24,48},{32,56},{40,0},{48,8},{56,16},{1,25}... | collective-permute-start | bytes 196616 | tf_op jit(solution)/shard_map/ppermute | solution.py:25
  159.9 10.1 %collective-permute-start.26 = (bf16[32,1024]{1,0:T(8,128)(2,1)S(1)}, bf16[32,1024]{1,0:T(8,128)(2,1)S(1)}, u32[]{:S(2)}, u32[]{:S(2)}) collective-permute-start(bf16[32,1024]{1,0:T(8,128)(2,1)S(1)} %get-tuple-element.73), channel_id=1, source_target_pairs={{0,32},{8,40},{16,48},{24,56},{32,0},{40,8},{48,16},{56,24},{1,33}... | collective-permute-start | bytes 196616 | tf_op jit(solution)/shard_map/ppermute | solution.py:25
  162.3 7.8 %collective-permute-start.27 = (bf16[32,1024]{1,0:T(8,128)(2,1)S(1)}, bf16[32,1024]{1,0:T(8,128)(2,1)S(1)}, u32[]{:S(2)}, u32[]{:S(2)}) collective-permute-start(bf16[32,1024]{1,0:T(8,128)(2,1)S(1)} %get-tuple-element.74), channel_id=1, source_target_pairs={{0,40},{8,48},{16,56},{24,0},{32,8},{40,16},{48,24},{56,32},{1,41}... | collective-permute-start | bytes 196616 | tf_op jit(solution)/shard_map/ppermute | solution.py:25
  165.0 7.4 %collective-permute-start.28 = (bf16[32,1024]{1,0:T(8,128)(2,1)S(1)}, bf16[32,1024]{1,0:T(8,128)(2,1)S(1)}, u32[]{:S(2)}, u32[]{:S(2)}) collective-permute-start(bf16[32,1024]{1,0:T(8,128)(2,1)S(1)} %get-tuple-element.75), channel_id=1, source_target_pairs={{0,48},{8,56},{16,0},{24,8},{32,16},{40,24},{48,32},{56,40},{1,49}... | collective-permute-start | bytes 196616 | tf_op jit(solution)/shard_map/ppermute | solution.py:25
  168.6 4.5 %collective-permute-start.29 = (bf16[32,1024]{1,0:T(8,128)(2,1)S(1)}, bf16[32,1024]{1,0:T(8,128)(2,1)S(1)}, u32[]{:S(2)}, u32[]{:S(2)}) collective-permute-start(bf16[32,1024]{1,0:T(8,128)(2,1)S(1)} %get-tuple-element.76), channel_id=1, source_target_pairs={{0,56},{8,0},{16,8},{24,16},{32,24},{40,32},{48,40},{56,48},{1,57}... | collective-permute-start | bytes 196616 | tf_op jit(solution)/shard_map/ppermute | solution.py:25
  173.5 8.3 %collective-permute-start.30 = (bf16[128,1024]{1,0:T(8,128)(2,1)S(1)}, bf16[128,1024]{1,0:T(8,128)(2,1)S(1)}, u32[]{:S(2)}, u32[]{:S(2)}) collective-permute-start(bf16[128,1024]{1,0:T(8,128)(2,1)S(1)} %get-tuple-element.77), channel_id=1, source_target_pairs={{0,64},{64,128},{128,192},{1,65},{65,129},{129,193},{2,66},{66,130... | collective-permute-start | bytes 786440 | tf_op jit(solution)/shard_map/ppermute | solution.py:456
  177.5 8.3 %collective-permute-start.18 = (bf16[128,1024]{1,0:T(8,128)(2,1)S(1)}, bf16[128,1024]{1,0:T(8,128)(2,1)S(1)}, u32[]{:S(2)}, u32[]{:S(2)}) collective-permute-start(bf16[128,1024]{1,0:T(8,128)(2,1)S(1)} %get-tuple-element.63), channel_id=1, source_target_pairs={{0,64},{64,128},{128,192},{1,65},{65,129},{129,193},{2,66},{66,130... | collective-permute-start | bytes 786440 | tf_op jit(solution)/shard_map/ppermute | solution.py:456
